TPU v7x, 256 devices: a whole 4x4x8 slice. The times are simulated.
256 devices in a mesh: slab: 256 (over x, z, y, core).
Axes of the slice: x: 4, y: 4, z: 8, core: 2. Of those that a mesh axis runs over, the one named last changes fastest.
Arguments:
- coords: float32 [3, 524288], P(None, 'slab'), may hold values from -18 to 2048, as said below
- charges: float32 [524288], P('slab'), may hold values from -3.6 to 3.6
- radii: float32 [524288], P('slab'), may hold values from 1.2 to 2
- screens: float32 [524288], P('slab'), may hold values from 0.6 to 0.9
- tile_lists: int32 [4096, 8], P('slab'), may hold values from 0 to 79, as said below
- tile_counts: int32 [4096], P('slab'), may hold values from 1 to 8, as said below
- slab_fill: int32 [256], P('slab'), may hold values from 1921 to 2048
Outputs:
- born_radii: float32 [524288], P('slab')
- energy: float32 [524288], P('slab')
- total: float32 [], replicated
Inputs may be any that keep to these rules, and one draw needn't show every extreme that they name: `coords`: x and y lie within 18 of the fibre axis; z of atoms of slab s lies in [8 s, 8 s + 8]. `tile_lists`: entry 0 of tile g's list is its own tile, 32 + g % 16; the entries of a row are distinct; listed tiles lie in slabs that exist (the fibre does not close) and within 32 window tiles of the own tile. `tile_counts`: every slab has a tile whose count is 8.
All inputs are finite; a program needn't handle non-finite values.
Results may differ from a plain program's by a relative error of at most 0.0003.
Values sent between devices are 32-bit elements; how exact they have to be, the bound alone decides.
No kernel may reach another device: no remote copies, remote signals or barrier semaphores. Data moves between devices by JAX's collectives and lax.ppermute only.
A program may use at most 64 MiB of HBM per device.

v0:
```python
import jax
import jax.numpy as jnp
from jax import lax
from jax.sharding import Mesh
from jax.sharding import PartitionSpec as P

SLAB = ("slab_0", "slab_1", "slab_2", "slab_3")


OFFSET = 0.09
SOFTEN = 1.0
group_tiles = 4


def passed_along(value, axis, steps):
    count = lax.axis_size(axis)
    pairs = [(source, (source + steps) % count) for source in range(count)]
    return lax.ppermute(value, axis, pairs)


def by_axis(shard, axes):
    for axis in axes:
        shard = lax.psum(shard, axis)
    return shard


def pair_geometry(own_atoms, partner_atoms, list_block, count_block, first_block):
    squared = jnp.zeros((own_atoms.shape[1], 128, partner_atoms.shape[2], 128), jnp.float32)
    for component in range(3):
        offsets = own_atoms[component][:, :, None, None] - partner_atoms[component][:, None, :, :]
        squared = squared + offsets * offsets
    slot_ids = jnp.arange(partner_atoms.shape[2], dtype=jnp.int32)
    used_slot = (slot_ids[None, :] < count_block[:, None])[:, None, :, None]
    partner_mask = (
        used_slot & (partner_atoms[6] > 0.5)[:, None, :, :] & (own_atoms[6] > 0.5)[:, :, None, None]
    )
    lanes = jnp.arange(128, dtype=jnp.int32)
    own_ids = first_block[:, None] * 128 + lanes[None, :]
    partner_ids = list_block[:, :, None] * 128 + lanes[None, None, :]
    distinct = own_ids[:, :, None, None] != partner_ids[:, None, :, :]
    return (squared, partner_mask, distinct)


def born_block(own_atoms, partner_atoms, list_block, count_block, first_block):
    squared, partner_mask, distinct = pair_geometry(
        own_atoms, partner_atoms, list_block, count_block, first_block
    )
    own_live = own_atoms[6] > 0.5
    radius_own = jnp.where(own_live, own_atoms[4], 1.5)
    radius_partner = jnp.where(partner_atoms[6] > 0.5, partner_atoms[4], 1.5)[:, None, :, :]
    screen_partner = jnp.where(partner_atoms[6] > 0.5, partner_atoms[5], 0.8)[:, None, :, :]
    offset_radius = (radius_own - OFFSET)[:, :, None, None]
    scaled_radius = screen_partner * (radius_partner - OFFSET)
    distance = jnp.sqrt(squared + SOFTEN)
    upper_end = distance + scaled_radius
    lower_end = jnp.maximum(offset_radius, jnp.abs(distance - scaled_radius))
    pair_term = 0.5 * (
        1.0 / lower_end
        - 1.0 / upper_end
        + 0.25
        * (distance - scaled_radius * scaled_radius / distance)
        * (1.0 / (upper_end * upper_end) - 1.0 / (lower_end * lower_end))
        + 0.5 * jnp.log(lower_end / upper_end) / distance
    )
    pair_term = pair_term + jnp.where(
        offset_radius < scaled_radius - distance, 2.0 * (1.0 / offset_radius - 1.0 / lower_end), 0.0
    )
    counted = partner_mask & distinct & (offset_radius < upper_end)
    integral = jnp.sum(jnp.where(counted, pair_term, 0.0), axis=(2, 3))
    inner_radius = radius_own - OFFSET
    psi_value = integral * inner_radius
    bending = jnp.tanh(
        psi_value - 0.8 * psi_value * psi_value + 4.85 * psi_value * psi_value * psi_value
    )
    result = 1.0 / (1.0 / inner_radius - bending / radius_own)
    return jnp.where(own_live, result, 0.0)


def energy_block(
    own_atoms, partner_atoms, radius_own, radius_partner, list_block, count_block, first_block
):
    squared, partner_mask, distinct = pair_geometry(
        own_atoms, partner_atoms, list_block, count_block, first_block
    )
    own_live = own_atoms[6] > 0.5
    born_own = jnp.where(own_live, radius_own, 1.0)[:, :, None, None]
    born_partner = jnp.where(partner_atoms[6] > 0.5, radius_partner, 1.0)[:, None, :, :]
    product = born_own * born_partner
    screened = jnp.sqrt(squared + product * jnp.exp(-squared / (4.0 * product)))
    pair_term = jnp.where(partner_mask, partner_atoms[3][:, None, :, :] / screened, 0.0)
    result = -0.5 * own_atoms[3] * jnp.sum(pair_term, axis=(2, 3))
    return jnp.where(own_live, result, 0.0)


def tile_setup(window, lists, counts):
    width = window.shape[1]
    tiles = width // 640
    blocks = tiles // group_tiles
    tiled = window.reshape(window.shape[0], width // 128, 128)
    own_atoms = (
        tiled[:, 2 * tiles : 3 * tiles]
        .reshape(window.shape[0], blocks, group_tiles, 128)
        .transpose(1, 0, 2, 3)
    )
    list_groups = lists.reshape(blocks, group_tiles, lists.shape[1])
    count_groups = counts.reshape(blocks, group_tiles)
    first_tiles = (2 * tiles + jnp.arange(tiles, dtype=jnp.int32)).reshape(blocks, group_tiles)
    return (tiled, own_atoms, list_groups, count_groups, first_tiles)


def slab_born(window, lists, counts):
    tiled, own_atoms, list_groups, count_groups, first_tiles = tile_setup(window, lists, counts)

    def one_block(inputs):
        own_block, list_block, count_block, first_block = inputs
        partner_atoms = jnp.take(tiled, list_block, axis=1)
        return born_block(own_block, partner_atoms, list_block, count_block, first_block)

    result = lax.map(one_block, (own_atoms, list_groups, count_groups, first_tiles))
    return result.reshape(-1)


def slab_energy(window, radius_window, lists, counts):
    tiled, own_atoms, list_groups, count_groups, first_tiles = tile_setup(window, lists, counts)
    radius_tiled = radius_window.reshape(-1, 128)
    tiles = radius_tiled.shape[0] // 5
    radius_groups = radius_tiled[2 * tiles : 3 * tiles].reshape(-1, group_tiles, 128)

    def one_block(inputs):
        own_block, radius_block, list_block, count_block, first_block = inputs
        partner_atoms = jnp.take(tiled, list_block, axis=1)
        partner_radii = jnp.take(radius_tiled, list_block, axis=0)
        return energy_block(
            own_block,
            partner_atoms,
            radius_block,
            partner_radii,
            list_block,
            count_block,
            first_block,
        )

    result = lax.map(one_block, (own_atoms, radius_groups, list_groups, count_groups, first_tiles))
    return result.reshape(-1)


def window_of(values):
    nearby = [passed_along(values, SLAB, shift_by) for shift_by in (1, -1)]
    distant = [passed_along(values, SLAB, shift_by) for shift_by in (2, -2)]
    return jnp.concatenate([distant[0], nearby[0], values, nearby[1], distant[1]], axis=-1)


def shards(coords, charges, radii, screens, tile_lists, tile_counts, slab_fill):
    atom_count = coords.shape[1]
    live_flag = (jnp.arange(atom_count, dtype=jnp.int32) < slab_fill[0]).astype(jnp.float32)
    packed = jnp.concatenate(
        [coords, charges[None], radii[None], screens[None], live_flag[None]], axis=0
    )
    window = window_of(packed)
    born_radii = slab_born(window, tile_lists, tile_counts)
    radius_window = window_of(born_radii)
    energy = slab_energy(window, radius_window, tile_lists, tile_counts)
    total = by_axis(jnp.sum(energy), SLAB)
    return (born_radii, energy, total)


def solution(mesh):
    torus = Mesh(mesh.devices.reshape(4, 8, 4, 2), ("slab_0", "slab_1", "slab_2", "slab_3"))
    placed = (P(None, SLAB), P(SLAB), P(SLAB), P(SLAB), P(SLAB, None), P(SLAB), P(SLAB))
    return jax.shard_map(
        shards, mesh=torus, in_specs=placed, out_specs=(P(SLAB), P(SLAB), P()), check_vma=False
    )
```

profile of v0, /device:TPU:1, one launch (start us, length us, event | category | flops | bytes accessed | tf_op | source)
XLA Modules:
  0.0 163.9 jit_solution(10497928802857674621)
XLA Ops:
  1.3 0.8 concatenate.21
  2.1 2.2 %collective-permute-start = (f32[7,2048]{1,0:T(8,128)S(1)}, f32[7,2048]{1,0:T(8,128)S(1)}, u32[]{:S(2)}, u32[]{:S(2)}) collective-permute-start(f32[7,2048]{1,0:T(8,128)S(1)} %concatenate.21), channel_id=1, source_target_pairs={{0,2},{1,3},{2,4},{3,5},{4,6},{5,7},{6,8},{7,9},{8,10},{9,11},{10,... | collective-permute-start | bytes 172040 | tf_op jit(solution)/shard_map/ppermute | solution.py:18
  4.3 2.1 %collective-permute-start.1 = (f32[7,2048]{1,0:T(8,128)S(1)}, f32[7,2048]{1,0:T(8,128)S(1)}, u32[]{:S(2)}, u32[]{:S(2)}) collective-permute-start(f32[7,2048]{1,0:T(8,128)S(1)} %concatenate.21), channel_id=1, source_target_pairs={{0,1},{1,2},{2,3},{3,4},{4,5},{5,6},{6,7},{7,8},{8,9},{9,10},{10,1... | collective-permute-start | bytes 172040 | tf_op jit(solution)/shard_map/ppermute | solution.py:18
  6.5 7.6 %collective-permute-start.3 = (f32[7,2048]{1,0:T(8,128)S(1)}, f32[7,2048]{1,0:T(8,128)S(1)}, u32[]{:S(2)}, u32[]{:S(2)}) collective-permute-start(f32[7,2048]{1,0:T(8,128)S(1)} %concatenate.21), channel_id=1, source_target_pairs={{0,254},{1,255},{2,0},{3,1},{4,2},{5,3},{6,4},{7,5},{8,6},{9,7},{1... | collective-permute-start | bytes 172040 | tf_op jit(solution)/shard_map/ppermute | solution.py:18
  14.1 0.8 copy.25
  14.9 0.7 reshape.487
  15.7 0.3 collective-permute-done.3
  16.1 47.0 %while.23 = (s32[]{:T(128)}, f32[4,4,128]{2,1,0:T(4,128)S(1)}, f32[4,7,4,128]{3,2,1,0:T(4,128)S(1)}, s32[4,4]{1,0:T(4,128)S(1)}, s32[4,4,8]{2,1,0:T(4,128)S(1)},...) while((s32[]{:T(128)}, f32[4,4,128]{2,1,0:T(4,128)S(1)}, ...), condition=%wide.region_2.4_spmd, body=%wide.region_0.3_spmd.sunk | while | flops 23141128 | bytes 918585 | solution.py:119
  16.1 0.1 reshape.539
  16.2 0.6 gather_fusion
  16.8 0.1 select_bitcast_fusion.2
  17.4 10.4 %fusion.63 = f32[4,128]{1,0:T(4,128)S(1)} fusion(f32[4,128]{1,0:T(4,128)S(1)} %get-tuple-element.337, f32[4,8,128]{2,1,0:T(8,128)S(1)} %get-tuple-element.345, f32[4,8,128]{2,1,0:T(8,128)S(1)} %get-tuple-element.346, f32[4,8,128]{2,1,0:T(8,128)S(1)} %bitcast.188, f32[4,128]{1,0:T(4,128)S(1)} %get-tuple-element.348, f32[4,8,128]{2,1,0:T(8,128)S(1)} %bitcast.189, ...), kind=kLoop, calls=%fused_computation.16.clone.1 | loop fusion | flops 23068160 | bytes 117248 | tf_op jit(solution)/shard_map/while/body/eval_jaxpr/reduce_sum | solution.py:69
  28.0 0.6 gather_fusion
  28.5 0.1 select_bitcast_fusion.2
  29.1 10.4 %fusion.63 = f32[4,128]{1,0:T(4,128)S(1)} fusion(f32[4,128]{1,0:T(4,128)S(1)} %get-tuple-element.337, f32[4,8,128]{2,1,0:T(8,128)S(1)} %get-tuple-element.345, f32[4,8,128]{2,1,0:T(8,128)S(1)} %get-tuple-element.346, f32[4,8,128]{2,1,0:T(8,128)S(1)} %bitcast.188, f32[4,128]{1,0:T(4,128)S(1)} %get-tuple-element.348, f32[4,8,128]{2,1,0:T(8,128)S(1)} %bitcast.189, ...), kind=kLoop, calls=%fused_computation.16.clone.1 | loop fusion | flops 23068160 | bytes 117248 | tf_op jit(solution)/shard_map/while/body/eval_jaxpr/reduce_sum | solution.py:69
  39.7 0.6 gather_fusion
  40.3 0.1 select_bitcast_fusion.2
  40.9 10.4 %fusion.63 = f32[4,128]{1,0:T(4,128)S(1)} fusion(f32[4,128]{1,0:T(4,128)S(1)} %get-tuple-element.337, f32[4,8,128]{2,1,0:T(8,128)S(1)} %get-tuple-element.345, f32[4,8,128]{2,1,0:T(8,128)S(1)} %get-tuple-element.346, f32[4,8,128]{2,1,0:T(8,128)S(1)} %bitcast.188, f32[4,128]{1,0:T(4,128)S(1)} %get-tuple-element.348, f32[4,8,128]{2,1,0:T(8,128)S(1)} %bitcast.189, ...), kind=kLoop, calls=%fused_computation.16.clone.1 | loop fusion | flops 23068160 | bytes 117248 | tf_op jit(solution)/shard_map/while/body/eval_jaxpr/reduce_sum | solution.py:69
  51.5 0.6 gather_fusion
  52.0 0.1 select_bitcast_fusion.2
  52.6 10.4 %fusion.63 = f32[4,128]{1,0:T(4,128)S(1)} fusion(f32[4,128]{1,0:T(4,128)S(1)} %get-tuple-element.337, f32[4,8,128]{2,1,0:T(8,128)S(1)} %get-tuple-element.345, f32[4,8,128]{2,1,0:T(8,128)S(1)} %get-tuple-element.346, f32[4,8,128]{2,1,0:T(8,128)S(1)} %bitcast.188, f32[4,128]{1,0:T(4,128)S(1)} %get-tuple-element.348, f32[4,8,128]{2,1,0:T(8,128)S(1)} %bitcast.189, ...), kind=kLoop, calls=%fused_computation.16.clone.1 | loop fusion | flops 23068160 | bytes 117248 | tf_op jit(solution)/shard_map/while/body/eval_jaxpr/reduce_sum | solution.py:69
  63.1 0.1 collective-permute-start.4
  63.2 1.4 collective-permute-start.5
  64.6 0.8 collective-permute-start.6
  65.4 7.4 %collective-permute-start.7 = (f32[2048]{0:T(1024)S(1)}, f32[2048]{0:T(1024)S(1)}, u32[]{:S(2)}, u32[]{:S(2)}) collective-permute-start(f32[2048]{0:T(1024)S(1)} %bitcast.195), channel_id=1, source_target_pairs={{0,254},{1,255},{2,0},{3,1},{4,2},{5,3},{6,4},{7,5},{8,6},{9,7},{1... | collective-permute-start | bytes 24584 | tf_op jit(solution)/shard_map/ppermute | solution.py:18
  72.8 0.7 collective-permute-done.7
  73.6 44.1 %while.24 = (s32[]{:T(128)}, f32[4,4,128]{2,1,0:T(4,128)S(1)}, f32[4,7,4,128]{3,2,1,0:T(4,128)S(1)}, s32[4,4]{1,0:T(4,128)S(1)}, s32[4,4,8]{2,1,0:T(4,128)S(1)},...) while((s32[]{:T(128)}, f32[4,4,128]{2,1,0:T(4,128)S(1)}, ...), condition=%wide.region_5.7_spmd, body=%wide.region_3.6_spmd.sunk | while | flops 9486662 | bytes 816557 | solution.py:143
  73.7 0.6 gather_fusion.1
  74.5 0.1 reshape.545
  74.6 0.6 gather_fusion.2
  75.3 9.3 %select_reduce_fusion.2 = f32[4,128]{1,0:T(4,128)S(1)} fusion(f32[4,8,128]{2,1,0:T(8,128)S(1)} %fusion.66, f32[4,128]{1,0:T(4,128)S(1)} %get-tuple-element.368, f32[4,8,128]{2,1,0:T(8,128)S(1)} %get-tuple-element.369, f32[4,128]{1,0:T(4,128)S(1)} %get-tuple-element.370, f32[4,8,128]{2,1,0:T(8,128)S(1)} %get-tuple-element.371, ...), kind=kLoop, calls=%fused_computation.63.clone.1 | loop fusion | flops 9436672 | bytes 96768 | tf_op jit(solution)/shard_map/while/body/eval_jaxpr/reduce_sum | solution.py:91
  84.7 0.6 gather_fusion.1
  85.6 0.1 reshape.545
  85.7 0.6 gather_fusion.2
  86.4 9.3 %select_reduce_fusion.2 = f32[4,128]{1,0:T(4,128)S(1)} fusion(f32[4,8,128]{2,1,0:T(8,128)S(1)} %fusion.66, f32[4,128]{1,0:T(4,128)S(1)} %get-tuple-element.368, f32[4,8,128]{2,1,0:T(8,128)S(1)} %get-tuple-element.369, f32[4,128]{1,0:T(4,128)S(1)} %get-tuple-element.370, f32[4,8,128]{2,1,0:T(8,128)S(1)} %get-tuple-element.371, ...), kind=kLoop, calls=%fused_computation.63.clone.1 | loop fusion | flops 9436672 | bytes 96768 | tf_op jit(solution)/shard_map/while/body/eval_jaxpr/reduce_sum | solution.py:91
  95.8 0.6 gather_fusion.1
  96.6 0.1 reshape.545
  96.7 0.6 gather_fusion.2
  97.4 9.3 %select_reduce_fusion.2 = f32[4,128]{1,0:T(4,128)S(1)} fusion(f32[4,8,128]{2,1,0:T(8,128)S(1)} %fusion.66, f32[4,128]{1,0:T(4,128)S(1)} %get-tuple-element.368, f32[4,8,128]{2,1,0:T(8,128)S(1)} %get-tuple-element.369, f32[4,128]{1,0:T(4,128)S(1)} %get-tuple-element.370, f32[4,8,128]{2,1,0:T(8,128)S(1)} %get-tuple-element.371, ...), kind=kLoop, calls=%fused_computation.63.clone.1 | loop fusion | flops 9436672 | bytes 96768 | tf_op jit(solution)/shard_map/while/body/eval_jaxpr/reduce_sum | solution.py:91
  106.8 0.6 gather_fusion.1
  107.6 0.1 reshape.545
  107.7 0.6 gather_fusion.2
  108.4 9.3 %select_reduce_fusion.2 = f32[4,128]{1,0:T(4,128)S(1)} fusion(f32[4,8,128]{2,1,0:T(8,128)S(1)} %fusion.66, f32[4,128]{1,0:T(4,128)S(1)} %get-tuple-element.368, f32[4,8,128]{2,1,0:T(8,128)S(1)} %get-tuple-element.369, f32[4,128]{1,0:T(4,128)S(1)} %get-tuple-element.370, f32[4,8,128]{2,1,0:T(8,128)S(1)} %get-tuple-element.371, ...), kind=kLoop, calls=%fused_computation.63.clone.1 | loop fusion | flops 9436672 | bytes 96768 | tf_op jit(solution)/shard_map/while/body/eval_jaxpr/reduce_sum | solution.py:91
  117.7 0.6 reduce_sum.35
  118.3 6.6 %psum.28 = f32[]{:T(128)} all-reduce(f32[]{:T(128)} %reduce_sum.35), channel_id=1, replica_groups=mesh['slab_0'=4,'slab_1'=8,'slab_2'=4,'slab_3'=2] {'slab_0'}, use_global_device_ids=true, to_apply=%region_7.9 | all-reduce | flops 1 | bytes 8 | tf_op jit(solution)/shard_map/psum | solution.py:23
  124.9 12.9 %psum.29 = f32[]{:T(128)} all-reduce(f32[]{:T(128)} %psum.28), channel_id=1, replica_groups=mesh['slab_0'=4,'slab_1'=8,'slab_2'=4,'slab_3'=2] {'slab_1'}, use_global_device_ids=true, to_apply=%region_8.10 | all-reduce | flops 1 | bytes 8 | tf_op jit(solution)/shard_map/psum | solution.py:23
  137.9 12.6 %psum.30 = f32[]{:T(128)} all-reduce(f32[]{:T(128)} %psum.29), channel_id=1, replica_groups=mesh['slab_0'=4,'slab_1'=8,'slab_2'=4,'slab_3'=2] {'slab_2'}, use_global_device_ids=true, to_apply=%region_9.11 | all-reduce | flops 1 | bytes 8 | tf_op jit(solution)/shard_map/psum | solution.py:23
  150.5 13.3 %psum.31 = f32[]{:T(128)} all-reduce(f32[]{:T(128)} %psum.30), channel_id=1, replica_groups=mesh['slab_0'=4,'slab_1'=8,'slab_2'=4,'slab_3'=2] {'slab_3'}, use_global_device_ids=true, to_apply=%region_10.12 | all-reduce | flops 1 | bytes 8 | tf_op jit(solution)/shard_map/psum | solution.py:23
  (138 shorter events, 4.2 us)
Async XLA Ops:
  2.1 13.5 %collective-permute-start = (f32[7,2048]{1,0:T(8,128)S(1)}, f32[7,2048]{1,0:T(8,128)S(1)}, u32[]{:S(2)}, u32[]{:S(2)}) collective-permute-start(f32[7,2048]{1,0:T(8,128)S(1)} %concatenate.21), channel_id=1, source_target_pairs={{0,2},{1,3},{2,4},{3,5},{4,6},{5,7},{6,8},{7,9},{8,10},{9,11},{10,... | collective-permute-start | bytes 172040 | tf_op jit(solution)/shard_map/ppermute | solution.py:18
  4.3 11.3 %collective-permute-start.1 = (f32[7,2048]{1,0:T(8,128)S(1)}, f32[7,2048]{1,0:T(8,128)S(1)}, u32[]{:S(2)}, u32[]{:S(2)}) collective-permute-start(f32[7,2048]{1,0:T(8,128)S(1)} %concatenate.21), channel_id=1, source_target_pairs={{0,1},{1,2},{2,3},{3,4},{4,5},{5,6},{6,7},{7,8},{8,9},{9,10},{10,1... | collective-permute-start | bytes 172040 | tf_op jit(solution)/shard_map/ppermute | solution.py:18
  6.5 9.2 %collective-permute-start.2 = (f32[7,2048]{1,0:T(8,128)S(1)}, f32[7,2048]{1,0:T(8,128)S(1)}, u32[]{:S(2)}, u32[]{:S(2)}) collective-permute-start(f32[7,2048]{1,0:T(8,128)S(1)} %concatenate.21), channel_id=1, source_target_pairs={{0,255},{1,0},{2,1},{3,2},{4,3},{5,4},{6,5},{7,6},{8,7},{9,8},{10,... | collective-permute-start | bytes 172040 | tf_op jit(solution)/shard_map/ppermute | solution.py:18
  6.5 9.5 %collective-permute-start.3 = (f32[7,2048]{1,0:T(8,128)S(1)}, f32[7,2048]{1,0:T(8,128)S(1)}, u32[]{:S(2)}, u32[]{:S(2)}) collective-permute-start(f32[7,2048]{1,0:T(8,128)S(1)} %concatenate.21), channel_id=1, source_target_pairs={{0,254},{1,255},{2,0},{3,1},{4,2},{5,3},{6,4},{7,5},{8,6},{9,7},{1... | collective-permute-start | bytes 172040 | tf_op jit(solution)/shard_map/ppermute | solution.py:18
  63.1 9.7 %collective-permute-start.4 = (f32[2048]{0:T(1024)S(1)}, f32[2048]{0:T(1024)S(1)}, u32[]{:S(2)}, u32[]{:S(2)}) collective-permute-start(f32[2048]{0:T(1024)S(1)} %bitcast.192), channel_id=1, source_target_pairs={{0,2},{1,3},{2,4},{3,5},{4,6},{5,7},{6,8},{7,9},{8,10},{9,11},{10,... | collective-permute-start | bytes 24584 | tf_op jit(solution)/shard_map/ppermute | solution.py:18
  63.2 9.6 %collective-permute-start.5 = (f32[2048]{0:T(1024)S(1)}, f32[2048]{0:T(1024)S(1)}, u32[]{:S(2)}, u32[]{:S(2)}) collective-permute-start(f32[2048]{0:T(1024)S(1)} %bitcast.193), channel_id=1, source_target_pairs={{0,1},{1,2},{2,3},{3,4},{4,5},{5,6},{6,7},{7,8},{8,9},{9,10},{10,1... | collective-permute-start | bytes 24584 | tf_op jit(solution)/shard_map/ppermute | solution.py:18
  64.6 8.2 %collective-permute-start.6 = (f32[2048]{0:T(1024)S(1)}, f32[2048]{0:T(1024)S(1)}, u32[]{:S(2)}, u32[]{:S(2)}) collective-permute-start(f32[2048]{0:T(1024)S(1)} %bitcast.194), channel_id=1, source_target_pairs={{0,255},{1,0},{2,1},{3,2},{4,3},{5,4},{6,5},{7,6},{8,7},{9,8},{10,... | collective-permute-start | bytes 24584 | tf_op jit(solution)/shard_map/ppermute | solution.py:18
  65.4 8.2 %collective-permute-start.7 = (f32[2048]{0:T(1024)S(1)}, f32[2048]{0:T(1024)S(1)}, u32[]{:S(2)}, u32[]{:S(2)}) collective-permute-start(f32[2048]{0:T(1024)S(1)} %bitcast.195), channel_id=1, source_target_pairs={{0,254},{1,255},{2,0},{3,1},{4,2},{5,3},{6,4},{7,5},{8,6},{9,7},{1... | collective-permute-start | bytes 24584 | tf_op jit(solution)/shard_map/ppermute | solution.py:18
  117.7 46.2 %copy-start = (f32[4,4,128]{2,1,0:T(4,128)}, f32[4,4,128]{2,1,0:T(4,128)S(1)}, u32[]{:S(2)}) copy-start(f32[4,4,128]{2,1,0:T(4,128)S(1)} %get-tuple-element.470) | copy-start | bytes 24580
  117.7 46.1 %copy-start.1 = (f32[4,4,128]{2,1,0:T(4,128)}, f32[4,4,128]{2,1,0:T(4,128)S(1)}, u32[]{:S(2)}) copy-start(f32[4,4,128]{2,1,0:T(4,128)S(1)} %get-tuple-element.156) | copy-start | bytes 24580
where the time goes:
time: 164 us
  other arithmetic  82.8 us (50%)
  blocking collectives  45.5 us (28%)
  starting transfers between devices  21.7 us (13%)
  local copies, waits for them, and re-layouts  10.9 us (7%)
    psum x4, blocking collectives, by_axis(): shard = lax.psum(shard, axis)  45.5 us
    reduce_sum x4, other arithmetic, born_block(): integral = jnp.sum(jnp.where(counted, pair_term, 0.0), axis=(2, 3))  41.8 us
    reduce_sum x4, other arithmetic, energy_block(): result = -0.5 * own_atoms[3] * jnp.sum(pair_term, axis=(2, 3))  37 us
    ppermute x8, starting transfers between devices, passed_along(): return lax.ppermute(value, axis, pairs)  21.7 us
    gather x8, local copies, waits for them, and re-layouts, one_block(): partner_atoms = jnp.take(tiled, list_block, axis=1)  4.68 us
  transfers between devices with their start and end apart: 8, of which 2 were waited for; matrix products, arithmetic and copies ran while one was open for 1% of the time, Pallas kernels for 0%

commit v1 on v0

v1 whole, which is shorter than its diff:
```python
import jax
import jax.numpy as jnp
from jax import lax
from jax.experimental import pallas as pl
from jax.experimental.pallas import tpu as pltpu
from jax.sharding import Mesh
from jax.sharding import PartitionSpec as P

SLAB = ("slab_0", "slab_1", "slab_2", "slab_3")
OFFSET = 0.09
LOG2E = 1.4426950408889634
TILES = 16
UNROLL = 4
FAR_GAP = 3.5
ROWS = 88


def swaps(count):
    def chip_swap(odd):
        pairs = []
        for chip in range(count // 2):
            other = ((chip + odd) ^ 1) - odd
            for core in (0, 1):
                if 0 <= other < count // 2:
                    pairs.append((2 * chip + core, 2 * other + core))
                else:
                    pairs.append((2 * chip + core, 2 * chip + 1 - core))
        return pairs

    inner = [(i, i ^ 1) for i in range(count)]
    outer = [(i, (((i + 1) ^ 1) - 1) % count) for i in range(count)]
    return inner, outer, chip_swap(0), chip_swap(1)


def neighbours(value):
    return [lax.ppermute(value, SLAB, pairs) for pairs in swaps(lax.axis_size(SLAB))]


def slots(slab):
    inner = jnp.where(slab % 2 == 0, 3, 1)
    chip = jnp.where((slab // 2) % 2 == 0, 4, 0)
    return inner, 4 - inner, chip, 4 - chip


def rows_of(shape, axis=0):
    return lax.broadcasted_iota(jnp.int32, shape, axis)


def prep_kernel(slab_ref, fill_ref, coords_ref, charges_ref, radii_ref, screens_ref, out_ref):
    fill = fill_ref[0]
    middle = (8 * slab_ref[0] + 4).astype(jnp.float32)
    slot = rows_of((TILES, 128)) * 128 + rows_of((TILES, 128), 1)
    live = slot < fill
    scaled = jnp.where(live, screens_ref[...] * (radii_ref[...] - OFFSET), 0.0)
    charge = jnp.where(live, charges_ref[...], 0.0)
    home = jnp.where(rows_of((3, 128)) == 2, middle, 0.0)
    lane = rows_of((3, 128), 1)
    column = rows_of((1, 128), 1)
    low = jnp.zeros((1, 128), jnp.float32)
    high = jnp.zeros((1, 128), jnp.float32)
    for t in range(TILES):
        xyz = jnp.where(lane + t * 128 < fill, coords_ref[:, t * 128 : (t + 1) * 128], home)
        out_ref[5 * t : 5 * t + 3, :] = xyz
        out_ref[5 * t + 3 : 5 * t + 4, :] = scaled[t : t + 1]
        out_ref[5 * t + 4 : 5 * t + 5, :] = charge[t : t + 1]
        low = jnp.where(column == t, jnp.min(xyz[2:3], axis=1, keepdims=True), low)
        high = jnp.where(column == t, jnp.max(xyz[2:3], axis=1, keepdims=True), high)
    out_ref[80:81, :] = low
    out_ref[81:82, :] = high
    out_ref[82:88, :] = jnp.zeros((6, 128), jnp.float32)


def fill_blocks(blocks_ref, packed_ref, base, centre):
    row = rows_of((8, 128))
    shift = jnp.where(row == 2, centre, 0.0)
    tail = jnp.where(row == 6, 1.0, 0.0)
    for t in range(TILES):
        block = packed_ref[5 * t : 5 * t + 8, :] - shift
        square = block * block
        norm = square[0:1] + square[1:2] + square[2:3]
        blocks_ref[base + t] = jnp.where(row < 5, block, jnp.where(row == 5, norm, tail))


def parts_of(rows):
    first = rows.astype(jnp.bfloat16).astype(jnp.float32)
    rest = rows - first
    second = rest.astype(jnp.bfloat16).astype(jnp.float32)
    third = (rest - second).astype(jnp.bfloat16).astype(jnp.float32)
    return first, second, third


def fill_left(left_ref, blocks_ref):
    row = rows_of((8, 128))
    for g in range(TILES):
        block = blocks_ref[2 * TILES + g]
        norm = block[5:6] + 1.0
        left = jnp.where(
            row < 3,
            -2.0 * block,
            jnp.where(row == 5, 1.0, jnp.where(row == 6, jnp.broadcast_to(norm, (8, 128)), 0.0)),
        )
        a1, a2, a3 = parts_of(left)
        stack = jnp.concatenate([a1, a1, a1, a2, a2, a3], axis=0)
        left_ref[g] = stack.T.astype(jnp.bfloat16)


def column_of(row):
    return jnp.broadcast_to(row, (128, 128)).T


def softened(left_ref, blocks_ref, g, w):
    b1, b2, b3 = parts_of(blocks_ref[w])
    right = jnp.concatenate([b1, b2, b3, b1, b2, b1], axis=0).astype(jnp.bfloat16)
    return jnp.dot(left_ref[g], right, preferred_element_type=jnp.float32)


def run_list(count, entry_of, buffers, produce, consume):
    def fetch(base):
        for u in range(UNROLL):
            w, slot = entry_of(base + u)
            buffers[u][...] = produce(w, jnp.minimum(slot, TILES - 1))

    fetch(0)

    @pl.loop(0, (count + UNROLL - 1) // UNROLL)
    def _(step):
        base = step * UNROLL
        for u in range(UNROLL):
            w, slot = entry_of(base + u)
            consume(w, slot, buffers[u])
        fetch(base + UNROLL)


def pad_list(list_ref, count):
    for u in range(2 * UNROLL):
        list_ref[count + u] = 2 * TILES * 32 + TILES


def entry_in(list_ref):
    def entry_of(index):
        entry = list_ref[index]
        return entry >> 5, entry & 31

    return entry_of


def born_kernel(
    slab_ref, fill_ref, lists_ref, counts_ref, own_ref, p0_ref, p1_ref, p2_ref, p3_ref, radii_ref,
    blocks_ref, left_ref, born_ref, send_ref,
    offsets_ref, acc_ref, buf0, buf1, buf2, buf3, near_ref, far_ref, range_ref, sums_ref, sem,
):
    slab = slab_ref[0]
    places = (2,) + slots(slab)
    packed = (own_ref, p0_ref, p1_ref, p2_ref, p3_ref)
    copies = [
        pltpu.make_async_copy(ref.at[pl.ds(80, 8), :], range_ref.at[place], sem.at[i])
        for i, (ref, place) in enumerate(zip(packed, places))
    ]
    for copy in copies:
        copy.start()
    centre = (8 * slab + 4).astype(jnp.float32)
    for ref, place in zip(packed, places):
        fill_blocks(blocks_ref, ref, place * TILES, centre)
    fill_left(left_ref, blocks_ref)
    offset = radii_ref[...] - OFFSET
    for g in range(TILES):
        offsets_ref[g] = column_of(offset[g : g + 1])
    offsets_ref[TILES] = offsets_ref[0]
    for copy in copies:
        copy.wait()

    near = jnp.int32(0)
    far = jnp.int32(0)
    for g in range(TILES):
        low = range_ref[2, 0, g]
        high = range_ref[2, 1, g]
        for k in range(1, 8):
            w = lists_ref[g, k]
            used = (k < counts_ref[g]).astype(jnp.int32)
            gap = jnp.maximum(
                range_ref[w >> 4, 0, w & 15] - high, low - range_ref[w >> 4, 1, w & 15]
            )
            apart = (gap >= FAR_GAP).astype(jnp.int32) * used
            near_ref[near] = w * 32 + g
            far_ref[far] = w * 32 + g
            far = far + apart
            near = near + used - apart
    pad_list(near_ref, near)
    pad_list(far_ref, far)

    buffers = (buf0, buf1, buf2, buf3)

    def produce(w, g):
        return softened(left_ref, blocks_ref, g, w)

    def near_term(soft, scaled, offset):
        inverse = lax.rsqrt(soft)
        distance = soft * inverse
        upper = distance + scaled
        gap = distance - scaled
        lower = jnp.minimum(jnp.maximum(offset, jnp.abs(gap)), upper)
        ratio = 1.0 / (lower * upper)
        difference = (upper - lower) * ratio
        total = (upper + lower) * ratio
        weight = gap * upper * inverse
        logs = jnp.log(lower * lower * ratio)
        term = difference * (4.0 - weight * total) + (inverse + inverse) * logs
        inside = jnp.where(offset < -gap, 16.0 * (1.0 / offset - 1.0 / lower), 0.0)
        return term + inside

    def consume_near(w, slot, buffer, diagonal=False):
        scaled = blocks_ref[w, 3:4, :]
        for v in range(8):
            rows = slice(16 * v, 16 * v + 16)
            c = jnp.broadcast_to(scaled, (16, 128))
            if diagonal:
                same = rows_of((16, 128)) + 16 * v == rows_of((16, 128), 1)
                c = jnp.where(same, 0.0, c)
            term = near_term(buffer[rows, :], c, offsets_ref[slot, rows, :])
            if diagonal:
                acc_ref[slot, rows, :] = term
            else:
                acc_ref[slot, rows, :] += term

    def consume_far(w, slot, buffer):
        scaled = blocks_ref[w, 3:4, :]
        for v in range(8):
            rows = slice(16 * v, 16 * v + 16)
            soft = buffer[rows, :]
            inverse = lax.rsqrt(soft)
            gap = soft * inverse - scaled
            ratio = 1.0 / (soft - scaled * scaled)
            logs = jnp.log(gap * gap * ratio)
            acc_ref[slot, rows, :] += (4.0 * scaled) * ratio + (inverse + inverse) * logs

    run_list(
        TILES,
        lambda index: (2 * TILES + jnp.minimum(index, TILES - 1), index),
        buffers,
        produce,
        lambda w, slot, buffer: consume_near(w, slot, buffer, True),
    )
    run_list(near, entry_in(near_ref), buffers, produce, consume_near)
    run_list(far, entry_in(far_ref), buffers, produce, consume_far)

    for g in range(TILES):
        sums_ref[g : g + 1, :] = jnp.sum(acc_ref[g].T, axis=0, keepdims=True)
    slot = rows_of((TILES, 128)) * 128 + rows_of((TILES, 128), 1)
    live = slot < fill_ref[0]
    radius = jnp.where(live, radii_ref[...], 1.5)
    inner = radius - OFFSET
    psi = 0.125 * sums_ref[...] * inner
    bending = jnp.tanh(psi - 0.8 * psi * psi + 4.85 * psi * psi * psi)
    born = 1.0 / (1.0 / inner - bending / radius)
    born_ref[...] = jnp.where(live, born, 0.0)
    send_ref[...] = jnp.where(live, born, 1.0)


def energy_kernel(
    slab_ref, lists_ref, counts_ref, blocks_ref, left_ref, own_ref, r0_ref, r1_ref, r2_ref, r3_ref,
    energy_ref, share_ref,
    born_ref, column_ref, inverse_ref, acc_ref, buf0, buf1, buf2, buf3, list_ref, charge_ref,
):
    places = (2,) + slots(slab_ref[0])
    for ref, place in zip((own_ref, r0_ref, r1_ref, r2_ref, r3_ref), places):
        born_ref[pl.ds(place * TILES, TILES), :] = ref[...]
    count = jnp.int32(0)
    for g in range(TILES):
        for k in range(1, 8):
            list_ref[count] = lists_ref[g, k] * 32 + g
            count = count + (k < counts_ref[g]).astype(jnp.int32)
    pad_list(list_ref, count)
    for g in range(TILES):
        column = column_of(own_ref[g : g + 1, :])
        column_ref[g] = column
        inverse_ref[g] = (-0.25 * LOG2E) / column
    column_ref[TILES] = column_ref[0]
    inverse_ref[TILES] = inverse_ref[0]

    buffers = (buf0, buf1, buf2, buf3)

    def produce(w, g):
        return softened(left_ref, blocks_ref, g, w)

    def consume(w, slot, buffer, first=False):
        charge = blocks_ref[w, 4:5, :]
        partner = born_ref[pl.ds(w, 1), :]
        backward = 1.0 / partner
        for v in range(8):
            rows = slice(16 * v, 16 * v + 16)
            squared = buffer[rows, :] - 1.0
            product = column_ref[slot, rows, :] * partner
            decay = jnp.exp2(squared * (inverse_ref[slot, rows, :] * backward))
            term = charge * lax.rsqrt(squared + product * decay)
            if first:
                acc_ref[slot, rows, :] = term
            else:
                acc_ref[slot, rows, :] += term

    run_list(
        TILES,
        lambda index: (2 * TILES + jnp.minimum(index, TILES - 1), index),
        buffers,
        produce,
        lambda w, slot, buffer: consume(w, slot, buffer, True),
    )
    run_list(count, entry_in(list_ref), buffers, produce, consume)
    for g in range(TILES):
        energy_ref[g : g + 1, :] = jnp.sum(acc_ref[g].T, axis=0, keepdims=True)
        charge_ref[g : g + 1, :] = blocks_ref[2 * TILES + g, 4:5, :]
    energy = -0.5 * charge_ref[...] * energy_ref[...]
    energy_ref[...] = energy
    share = jnp.sum(jnp.sum(energy, axis=0, keepdims=True), axis=1, keepdims=True)
    share_ref[...] = jnp.broadcast_to(share[None], share_ref.shape)


def shards(coords, charges, radii, screens, tile_lists, tile_counts, slab_fill):
    f32 = jnp.float32
    count = lax.axis_size(SLAB)
    smem = pl.BlockSpec(memory_space=pltpu.SMEM)
    vmem = pl.BlockSpec(memory_space=pltpu.VMEM)
    slab = lax.axis_index(SLAB).astype(jnp.int32)[None]
    charges, radii, screens = (v.reshape(TILES, 128) for v in (charges, radii, screens))
    packed = pl.pallas_call(
        prep_kernel,
        out_shape=jax.ShapeDtypeStruct((ROWS, 128), f32),
        in_specs=[smem, smem] + [vmem] * 4,
        out_specs=vmem,
        name="prep",
    )(slab, slab_fill, coords, charges, radii, screens)
    around = neighbours(packed)
    square = pltpu.VMEM((128, 128), f32)
    stack = pltpu.VMEM((TILES + 1, 128, 128), f32)
    blocks, left, born, send = pl.pallas_call(
        born_kernel,
        out_shape=(
            jax.ShapeDtypeStruct((5 * TILES, 8, 128), f32),
            jax.ShapeDtypeStruct((TILES, 128, 48), jnp.bfloat16),
            jax.ShapeDtypeStruct((TILES, 128), f32),
            jax.ShapeDtypeStruct((TILES, 128), f32),
        ),
        in_specs=[smem] * 4 + [vmem] * 6,
        out_specs=(vmem,) * 4,
        scratch_shapes=[stack, stack, square, square, square, square]
        + [pltpu.SMEM((144,), jnp.int32)] * 2
        + [pltpu.SMEM((5, 8, 128), f32), pltpu.VMEM((TILES, 128), f32), pltpu.SemaphoreType.DMA((5,))],
        name="born",
    )(slab, slab_fill, tile_lists, tile_counts, packed, *around, radii)
    far_born = neighbours(send)
    energy, share = pl.pallas_call(
        energy_kernel,
        out_shape=(
            jax.ShapeDtypeStruct((TILES, 128), f32),
            jax.ShapeDtypeStruct((count, 1, 128), f32),
        ),
        in_specs=[smem] * 3 + [vmem] * 7,
        out_specs=(vmem,) * 2,
        scratch_shapes=[pltpu.VMEM((5 * TILES, 128), f32), stack, stack, stack, square, square, square, square]
        + [pltpu.SMEM((144,), jnp.int32), pltpu.VMEM((TILES, 128), f32)],
        name="energy",
    )(slab, tile_lists, tile_counts, blocks, left, send, *far_born)
    shares = lax.all_to_all(share, SLAB, 0, 0, tiled=True)
    total = jnp.sum(shares[:, 0, 0])
    return (born.reshape(-1), energy.reshape(-1), total)


def solution(mesh):
    torus = Mesh(mesh.devices.reshape(4, 8, 4, 2), SLAB)
    placed = (P(None, SLAB), P(SLAB), P(SLAB), P(SLAB), P(SLAB, None), P(SLAB), P(SLAB))
    return jax.shard_map(
        shards, mesh=torus, in_specs=placed, out_specs=(P(SLAB), P(SLAB), P()), check_vma=False
    )
```

time: 164 us -> 68.9 us (0.42)
  other arithmetic: 82.8 us -> 0.87 us
  blocking collectives: 45.5 us -> 23.9 us
  Pallas kernels: 0 us -> 16.8 us
  local copies, waits for them, and re-layouts: 10.9 us -> 2.13 us
    reduce_sum x9 -> x1, other arithmetic: 79.4 us -> 0.87 us  [shards(): total = jnp.sum(shares[:, 0, 0])]
    psum x4 -> x0, blocking collectives: 45.5 us -> none  [by_axis(): shard = lax.psum(shard, axis)]
    all_to_all x0 -> x1, blocking collectives: none -> 23.9 us  [shards(): shares = lax.all_to_all(share, SLAB, 0, 0, tiled=True)]
    pallas_call x0 -> x3, Pallas kernels: none -> 16.8 us  [the longest x1 9.41 us: shards(): pl.pallas_call(born_kernel, out_shape=(jax.ShapeDtypeStruct((5 * TILES, 8...]
    gather x12 -> x0, local copies, waits for them, and re-layouts: 6.98 us -> none  [the longest x8 4.68 us: one_block(): partner_atoms = jnp.take(tiled, list_block, axis=1)]
where the time goes in v1:
time: 68.9 us; the launch traced here: 69.4 us
  blocking collectives  23.9 us (35%)
  starting transfers between devices  23 us (33%)
  Pallas kernels  16.8 us (24%)
  local copies, waits for them, and re-layouts  2.13 us (3%)
  waiting for transfers between devices  1.4 us (2%)
  between operations  1.37 us (2%)
  other arithmetic  0.87 us (1%)
    all_to_all x1, blocking collectives, shards(): shares = lax.all_to_all(share, SLAB, 0, 0, tiled=True)  23.9 us
    ppermute x8, starting transfers between devices, neighbours(): lax.ppermute(value, SLAB, pairs)  23 us
    pallas_call x1, Pallas kernels, shards(): pl.pallas_call(born_kernel, out_shape=(jax.ShapeDtypeStruct((5 * TILES, 8...  9.41 us
    pallas_call x1, Pallas kernels, shards(): pl.pallas_call(energy_kernel, out_shape=(jax.ShapeDtypeStruct((TILES, 128...  5.92 us
    unnamed x19, local copies, waits for them, and re-layouts  2.13 us
    pallas_call x1, Pallas kernels, shards(): pl.pallas_call(prep_kernel, out_shape=jax.ShapeDtypeStruct((ROWS, 128), f...  1.51 us
    ppermute x8, waiting for transfers between devices, neighbours(): lax.ppermute(value, SLAB, pairs)  1.4 us
  transfers between devices with their start and end apart: 8, of which 2 were waited for; matrix products, arithmetic and copies ran while one was open for 1% of the time, Pallas kernels for 0%

profile of v1, /device:TPU:1, one launch (start us, length us, event | category | flops | bytes accessed | tf_op | source)
XLA Modules:
  0.0 69.4 jit_solution(11631306604768872073)
XLA Ops:
  1.3 0.0 copy-start.8
  1.3 1.5 %prep.1.own_ref = f32[88,128]{1,0:T(8,128)} custom-call(s32[1]{0:T(128)} %bitcast.slab_ref, s32[1]{0:T(128)S(6)} %copy.12.fill_ref, f32[3,2048]{1,0:T(4,128)} %coords_ref.1, f32[16,128]{1,0:T(8,128)} %bitcast.8, f32[16,128]{1,0:T(8,128)} %bitcast.6, f32[16,128]{1,0:T(8,128)} %bitcast.9), custom_call_target="tpu_custom_call" | custom-call | tf_op jit(solution)/shard_map/prep/pallas_call | solution.py:324
  2.8 3.2 %collective-permute-start.3 = (f32[88,128]{1,0:T(8,128)}, f32[88,128]{1,0:T(8,128)S(1)}, u32[]{:S(2)}, u32[]{:S(2)}) collective-permute-start(f32[88,128]{1,0:T(8,128)} %prep.1.own_ref), channel_id=1, source_target_pairs={{0,1},{1,0},{2,4},{3,5},{4,2},{5,3},{6,8},{7,9},{8,6},{9,7},{10,12... | collective-permute-start | bytes 135176 | tf_op jit(solution)/shard_map/ppermute | solution.py:36
  6.0 0.2 collective-permute-start.2
  6.2 1.4 %collective-permute-start.1 = (f32[88,128]{1,0:T(8,128)}, f32[88,128]{1,0:T(8,128)S(1)}, u32[]{:S(2)}, u32[]{:S(2)}) collective-permute-start(f32[88,128]{1,0:T(8,128)} %prep.1.own_ref), channel_id=1, source_target_pairs={{0,255},{1,2},{2,1},{3,4},{4,3},{5,6},{6,5},{7,8},{8,7},{9,10},{10... | collective-permute-start | bytes 135176 | tf_op jit(solution)/shard_map/ppermute | solution.py:36
  7.6 7.3 %collective-permute-start = (f32[88,128]{1,0:T(8,128)}, f32[88,128]{1,0:T(8,128)S(1)}, u32[]{:S(2)}, u32[]{:S(2)}) collective-permute-start(f32[88,128]{1,0:T(8,128)} %prep.1.own_ref), channel_id=1, source_target_pairs={{0,1},{1,0},{2,3},{3,2},{4,5},{5,4},{6,7},{7,6},{8,9},{9,8},{10,11... | collective-permute-start | bytes 135176 | tf_op jit(solution)/shard_map/ppermute | solution.py:36
  14.9 0.0 copy-done.8
  14.9 0.7 copy.10.lists_ref
  15.6 0.0 collective-permute-done.3.p3_ref
  15.6 0.0 copy-start
  15.6 0.0 collective-permute-done.2.p2_ref
  15.6 0.0 copy-start.1
  15.6 0.0 collective-permute-done.1.p1_ref
  15.6 0.0 copy-start.2
  15.6 0.4 collective-permute-done.p0_ref
  16.0 0.2 copy-done
  16.2 0.0 copy-done.1
  16.2 0.0 copy-done.2
  16.3 0.0 copy-start.3
  16.3 0.6 copy-done.3
  16.9 9.4 %born.1 = (f32[80,8,128]{2,1,0:T(8,128)}, bf16[16,128,48]{2,1,0:T(8,128)(2,1)}, f32[16,128]{1,0:T(8,128)}, f32[16,128]{1,0:T(8,128)}) custom-call(s32[1]{0:T(128)} %bitcast.slab_ref, s32[1]{0:T(128)S(6)} %copy.12.fill_ref, s32[16,8]{1,0:T(8,128)} %copy.10.lists_ref, s32[16]{0:T(128)} %counts_ref.3, f32[88,128]{1,0:T(8,128)} %prep.1.own_ref, ...), custom_call_target="tpu_custom_call" | custom-call | tf_op jit(solution)/shard_map/born/pallas_call | solution.py:334
  26.3 2.9 %collective-permute-start.7 = (f32[16,128]{1,0:T(8,128)}, f32[16,128]{1,0:T(8,128)S(1)}, u32[]{:S(2)}, u32[]{:S(2)}) collective-permute-start(f32[16,128]{1,0:T(8,128)} %get-tuple-element.12.own_ref), channel_id=1, source_target_pairs={{0,1},{1,0},{2,4},{3,5},{4,2},{5,3},{6,8},{7,9},{8,6},{9,7},{10,12... | collective-permute-start | bytes 24584 | tf_op jit(solution)/shard_map/ppermute | solution.py:36
  29.2 0.0 collective-permute-start.6
  29.2 1.7 %collective-permute-start.5 = (f32[16,128]{1,0:T(8,128)}, f32[16,128]{1,0:T(8,128)S(1)}, u32[]{:S(2)}, u32[]{:S(2)}) collective-permute-start(f32[16,128]{1,0:T(8,128)} %get-tuple-element.12.own_ref), channel_id=1, source_target_pairs={{0,255},{1,2},{2,1},{3,4},{4,3},{5,6},{6,5},{7,8},{8,7},{9,10},{10... | collective-permute-start | bytes 24584 | tf_op jit(solution)/shard_map/ppermute | solution.py:36
  31.0 6.2 %collective-permute-start.4 = (f32[16,128]{1,0:T(8,128)}, f32[16,128]{1,0:T(8,128)S(1)}, u32[]{:S(2)}, u32[]{:S(2)}) collective-permute-start(f32[16,128]{1,0:T(8,128)} %get-tuple-element.12.own_ref), channel_id=1, source_target_pairs={{0,1},{1,0},{2,3},{3,2},{4,5},{5,4},{6,7},{7,6},{8,9},{9,8},{10,11... | collective-permute-start | bytes 24584 | tf_op jit(solution)/shard_map/ppermute | solution.py:36
  37.2 0.0 collective-permute-done.7.r3_ref
  37.2 0.0 copy-start.4
  37.2 0.0 collective-permute-done.6.r2_ref
  37.2 0.0 copy-start.5
  37.2 0.0 collective-permute-done.5.r1_ref
  37.2 0.0 copy-start.6
  37.2 1.0 %collective-permute-done.4.r0_ref = f32[16,128]{1,0:T(8,128)S(1)} collective-permute-done((f32[16,128]{1,0:T(8,128)}, f32[16,128]{1,0:T(8,128)S(1)}, u32[]{:S(2)}, u32[]{:S(2)}) %collective-permute-start.4) | collective-permute-done | bytes 8224 | tf_op jit(solution)/shard_map/ppermute | solution.py:36
  38.2 0.0 copy-start.7
  38.2 0.0 copy-done.4
  38.2 0.0 copy-done.5
  38.2 0.0 copy-done.6
  38.2 0.6 copy-done.7
  38.8 5.9 %energy.1 = (f32[16,128]{1,0:T(8,128)}, f32[256,1,128]{2,1,0:T(1,128)}) custom-call(s32[1]{0:T(128)} %bitcast.slab_ref, s32[16,8]{1,0:T(8,128)} %copy.10.lists_ref, s32[16]{0:T(128)} %counts_ref.3, f32[80,8,128]{2,1,0:T(8,128)} %get-tuple-element.10.blocks_ref, bf16[16,128,48]{2,1,0:T(8,128)(2,1)} %get-tuple-element.11.left_ref, ...), custom_call_target="tpu_custom_call" | custom-call | tf_op jit(solution)/shard_map/energy/pallas_call | solution.py:350
  44.7 23.9 %all_to_all.5 = f32[256,1,128]{2,1,0:T(1,128)S(1)} all-to-all(f32[256,1,128]{2,1,0:T(1,128)} %get-tuple-element.14), channel_id=1, replica_groups=mesh['slab_0'=4,'slab_1'=8,'slab_2'=4,'slab_3'=2] {'slab_0','slab_1','sl..., dimensions={0} | all-to-all | bytes 262144 | tf_op jit(solution)/shard_map/all_to_all | solution.py:362
  68.6 0.9 %slice_reduce_fusion = f32[]{:T(128)} fusion(f32[256,1,128]{2,1,0:T(1,128)S(1)} %all_to_all.5), kind=kLoop, calls=%fused_computation | loop fusion | flops 255 | bytes 1028 | tf_op jit(solution)/shard_map/reduce_sum | solution.py:363
Async XLA Ops:
  1.3 13.6 %copy-start.8 = (s32[16,8]{0,1:T(8,128)S(1)}, s32[16,8]{0,1:T(8,128)}, u32[]{:S(2)}) copy-start(s32[16,8]{0,1:T(8,128)} %param.11) | copy-start | bytes 1540
  2.8 12.8 %collective-permute-start.3 = (f32[88,128]{1,0:T(8,128)}, f32[88,128]{1,0:T(8,128)S(1)}, u32[]{:S(2)}, u32[]{:S(2)}) collective-permute-start(f32[88,128]{1,0:T(8,128)} %prep.1.own_ref), channel_id=1, source_target_pairs={{0,1},{1,0},{2,4},{3,5},{4,2},{5,3},{6,8},{7,9},{8,6},{9,7},{10,12... | collective-permute-start | bytes 135176 | tf_op jit(solution)/shard_map/ppermute | solution.py:36
  6.0 9.6 %collective-permute-start.2 = (f32[88,128]{1,0:T(8,128)}, f32[88,128]{1,0:T(8,128)S(1)}, u32[]{:S(2)}, u32[]{:S(2)}) collective-permute-start(f32[88,128]{1,0:T(8,128)} %prep.1.own_ref), channel_id=1, source_target_pairs={{0,2},{1,3},{2,0},{3,1},{4,6},{5,7},{6,4},{7,5},{8,10},{9,11},{10,... | collective-permute-start | bytes 135176 | tf_op jit(solution)/shard_map/ppermute | solution.py:36
  6.2 9.4 %collective-permute-start.1 = (f32[88,128]{1,0:T(8,128)}, f32[88,128]{1,0:T(8,128)S(1)}, u32[]{:S(2)}, u32[]{:S(2)}) collective-permute-start(f32[88,128]{1,0:T(8,128)} %prep.1.own_ref), channel_id=1, source_target_pairs={{0,255},{1,2},{2,1},{3,4},{4,3},{5,6},{6,5},{7,8},{8,7},{9,10},{10... | collective-permute-start | bytes 135176 | tf_op jit(solution)/shard_map/ppermute | solution.py:36
  7.6 8.4 %collective-permute-start = (f32[88,128]{1,0:T(8,128)}, f32[88,128]{1,0:T(8,128)S(1)}, u32[]{:S(2)}, u32[]{:S(2)}) collective-permute-start(f32[88,128]{1,0:T(8,128)} %prep.1.own_ref), channel_id=1, source_target_pairs={{0,1},{1,0},{2,3},{3,2},{4,5},{5,4},{6,7},{7,6},{8,9},{9,8},{10,11... | collective-permute-start | bytes 135176 | tf_op jit(solution)/shard_map/ppermute | solution.py:36
  15.6 0.6 copy-start
  15.6 0.6 copy-start.1
  15.6 0.6 copy-start.2
  16.3 0.6 copy-start.3
  26.3 10.9 %collective-permute-start.7 = (f32[16,128]{1,0:T(8,128)}, f32[16,128]{1,0:T(8,128)S(1)}, u32[]{:S(2)}, u32[]{:S(2)}) collective-permute-start(f32[16,128]{1,0:T(8,128)} %get-tuple-element.12.own_ref), channel_id=1, source_target_pairs={{0,1},{1,0},{2,4},{3,5},{4,2},{5,3},{6,8},{7,9},{8,6},{9,7},{10,12... | collective-permute-start | bytes 24584 | tf_op jit(solution)/shard_map/ppermute | solution.py:36
  29.2 7.9 %collective-permute-start.6 = (f32[16,128]{1,0:T(8,128)}, f32[16,128]{1,0:T(8,128)S(1)}, u32[]{:S(2)}, u32[]{:S(2)}) collective-permute-start(f32[16,128]{1,0:T(8,128)} %get-tuple-element.12.own_ref), channel_id=1, source_target_pairs={{0,2},{1,3},{2,0},{3,1},{4,6},{5,7},{6,4},{7,5},{8,10},{9,11},{10,... | collective-permute-start | bytes 24584 | tf_op jit(solution)/shard_map/ppermute | solution.py:36
  29.2 7.9 %collective-permute-start.5 = (f32[16,128]{1,0:T(8,128)}, f32[16,128]{1,0:T(8,128)S(1)}, u32[]{:S(2)}, u32[]{:S(2)}) collective-permute-start(f32[16,128]{1,0:T(8,128)} %get-tuple-element.12.own_ref), channel_id=1, source_target_pairs={{0,255},{1,2},{2,1},{3,4},{4,3},{5,6},{6,5},{7,8},{8,7},{9,10},{10... | collective-permute-start | bytes 24584 | tf_op jit(solution)/shard_map/ppermute | solution.py:36
  31.0 7.2 %collective-permute-start.4 = (f32[16,128]{1,0:T(8,128)}, f32[16,128]{1,0:T(8,128)S(1)}, u32[]{:S(2)}, u32[]{:S(2)}) collective-permute-start(f32[16,128]{1,0:T(8,128)} %get-tuple-element.12.own_ref), channel_id=1, source_target_pairs={{0,1},{1,0},{2,3},{3,2},{4,5},{5,4},{6,7},{7,6},{8,9},{9,8},{10,11... | collective-permute-start | bytes 24584 | tf_op jit(solution)/shard_map/ppermute | solution.py:36
  37.2 1.0 %copy-start.4 = (f32[16,128]{1,0:T(8,128)}, f32[16,128]{1,0:T(8,128)S(1)}, u32[]{:S(2)}) copy-start(f32[16,128]{1,0:T(8,128)S(1)} %collective-permute-done.7.r3_ref) | copy-start | bytes 24580
  37.2 1.0 %copy-start.5 = (f32[16,128]{1,0:T(8,128)}, f32[16,128]{1,0:T(8,128)S(1)}, u32[]{:S(2)}) copy-start(f32[16,128]{1,0:T(8,128)S(1)} %collective-permute-done.6.r2_ref) | copy-start | bytes 24580
  37.2 1.0 %copy-start.6 = (f32[16,128]{1,0:T(8,128)}, f32[16,128]{1,0:T(8,128)S(1)}, u32[]{:S(2)}) copy-start(f32[16,128]{1,0:T(8,128)S(1)} %collective-permute-done.5.r1_ref) | copy-start | bytes 24580
  38.2 0.6 copy-start.7

commit v2 on v1

v2 whole, which is shorter than its diff:
```python
import jax
import jax.numpy as jnp
from jax import lax
from jax.experimental import pallas as pl
from jax.experimental.pallas import tpu as pltpu
from jax.sharding import Mesh
from jax.sharding import PartitionSpec as P

SLAB = ("slab_0", "slab_1", "slab_2", "slab_3")
OFFSET = 0.09
LOG2E = 1.4426950408889634
TILES = 16
UNROLL = 8
FAR_GAP = 3.5
ROWS = 88


def swaps(count):
    def chip_swap(odd):
        pairs = []
        for chip in range(count // 2):
            other = ((chip + odd) ^ 1) - odd
            for core in (0, 1):
                if 0 <= other < count // 2:
                    pairs.append((2 * chip + core, 2 * other + core))
                else:
                    pairs.append((2 * chip + core, 2 * chip + 1 - core))
        return pairs

    inner = [(i, i ^ 1) for i in range(count)]
    outer = [(i, (((i + 1) ^ 1) - 1) % count) for i in range(count)]
    return inner, outer, chip_swap(0), chip_swap(1)


def neighbours(value):
    return [lax.ppermute(value, SLAB, pairs) for pairs in swaps(lax.axis_size(SLAB))]


def slots(slab):
    inner = jnp.where(slab % 2 == 0, 3, 1)
    chip = jnp.where((slab // 2) % 2 == 0, 4, 0)
    return inner, 4 - inner, chip, 4 - chip


def rows_of(shape, axis=0):
    return lax.broadcasted_iota(jnp.int32, shape, axis)


def prep_kernel(slab_ref, fill_ref, coords_ref, charges_ref, radii_ref, screens_ref, out_ref):
    fill = fill_ref[0]
    middle = (8 * slab_ref[0] + 4).astype(jnp.float32)
    slot = rows_of((TILES, 128)) * 128 + rows_of((TILES, 128), 1)
    live = slot < fill
    scaled = jnp.where(live, screens_ref[...] * (radii_ref[...] - OFFSET), 0.0)
    charge = jnp.where(live, charges_ref[...], 0.0)
    home = jnp.where(rows_of((3, 128)) == 2, middle, 0.0)
    lane = rows_of((3, 128), 1)
    column = rows_of((1, 128), 1) % TILES
    low = jnp.zeros((1, 128), jnp.float32)
    high = jnp.zeros((1, 128), jnp.float32)
    for t in range(TILES):
        xyz = jnp.where(lane + t * 128 < fill, coords_ref[:, t * 128 : (t + 1) * 128], home)
        out_ref[5 * t : 5 * t + 3, :] = xyz
        out_ref[5 * t + 3 : 5 * t + 4, :] = scaled[t : t + 1]
        out_ref[5 * t + 4 : 5 * t + 5, :] = charge[t : t + 1]
        low = jnp.where(column == t, jnp.min(xyz[2:3], axis=1, keepdims=True), low)
        high = jnp.where(column == t, jnp.max(xyz[2:3], axis=1, keepdims=True), high)
    top = jnp.max(jnp.max(scaled, axis=0, keepdims=True), axis=1, keepdims=True)
    out_ref[80:81, :] = low
    out_ref[81:82, :] = high
    out_ref[82:83, :] = jnp.broadcast_to(top, (1, 128))
    out_ref[83:88, :] = jnp.zeros((5, 128), jnp.float32)


def parts_of(rows):
    first = rows.astype(jnp.bfloat16).astype(jnp.float32)
    rest = rows - first
    second = rest.astype(jnp.bfloat16).astype(jnp.float32)
    third = (rest - second).astype(jnp.bfloat16).astype(jnp.float32)
    return first, second, third


def fill_blocks(blocks_ref, right_ref, packed_ref, base, centre):
    row = rows_of((8, 128))
    shift = jnp.where(row == 2, centre, 0.0)
    tail = jnp.where(row == 6, 1.0, 0.0)
    last = jnp.where(rows_of((16, 128)) == 0, 1.0, 0.0)
    for t in range(TILES):
        block = packed_ref[5 * t : 5 * t + 8, :] - shift
        square = block * block
        norm = square[0:1] + square[1:2] + square[2:3]
        block = jnp.where(row < 5, block, jnp.where(row == 5, norm, tail))
        blocks_ref[base + t] = block
        b1, b2, b3 = parts_of(block)
        stack = jnp.concatenate([b1, b2, b3, b1, b2, b1, last], axis=0)
        right_ref[base + t] = stack.astype(jnp.bfloat16)


def fill_left(left_ref, blocks_ref):
    row = rows_of((8, 128))
    last = jnp.where(rows_of((16, 128)) == 0, 1.0, 0.0)
    for g in range(TILES):
        block = blocks_ref[2 * TILES + g]
        norm = jnp.broadcast_to(block[5:6], (8, 128))
        left = jnp.where(
            row < 3, -2.0 * block, jnp.where(row == 5, 1.0, jnp.where(row == 6, norm, 0.0))
        )
        a1, a2, a3 = parts_of(left)
        stack = jnp.concatenate([a1, a1, a1, a2, a2, a3, last], axis=0)
        left_ref[g] = stack.T.astype(jnp.bfloat16)


def column_of(row):
    return jnp.broadcast_to(row, (128, 128)).T


def squares(left_ref, right_ref, g, w, depth):
    return jnp.dot(
        left_ref[g, :, :depth], right_ref[w, :depth, :], preferred_element_type=jnp.float32
    )


def run_list(count, entry_of, buffers, produce, consume):
    unroll = len(buffers)

    def fetch(base):
        for u, buffer in enumerate(buffers):
            w, slot = entry_of(base + u)
            buffer[...] = produce(w, jnp.minimum(slot, TILES - 1))

    fetch(0)

    @pl.loop(0, (count + unroll - 1) // unroll)
    def _(step):
        base = step * unroll
        for u, buffer in enumerate(buffers):
            w, slot = entry_of(base + u)
            consume(w, slot, buffer)
        fetch(base + unroll)


def own_entry(index):
    return 2 * TILES + jnp.minimum(index, TILES - 1), index


def pad_list(list_ref, count):
    for u in range(2 * UNROLL):
        list_ref[count + u] = 2 * TILES * 32 + TILES


def entry_in(list_ref):
    def entry_of(index):
        entry = list_ref[index]
        return (entry >> 5) & 127, entry & 31

    return entry_of


def plan_of(lists_ref, counts_ref, offset, packed, places, index_ref, plan_ref):
    lane = rows_of((1, 128), 1)
    low = jnp.zeros((1, 128), jnp.float32)
    high = jnp.zeros((1, 128), jnp.float32)
    top = packed[0][82:83, :]
    for ref, place in zip(packed, places):
        low = jnp.where(lane >> 4 == place, ref[80:81, :], low)
        high = jnp.where(lane >> 4 == place, ref[81:82, :], high)
        top = jnp.maximum(top, ref[82:83, :])
    index_ref[...] = jnp.zeros((16, 128), jnp.int32)
    index_ref[0:8, 0:TILES] = lists_ref[...]
    index_ref[8:9, 0:TILES] = counts_ref[...]
    tile = index_ref[0:8, :]
    used = (rows_of((8, 128)) > 0) & (rows_of((8, 128)) < index_ref[8:9, :])

    def picked(row):
        return jnp.take_along_axis(
            jnp.broadcast_to(row, (8, 128)), tile, axis=1, mode="promise_in_bounds"
        )

    gap = jnp.maximum(picked(low) - packed[0][81:82, :], packed[0][80:81, :] - picked(high))
    kind = jnp.where(used, jnp.where(gap >= FAR_GAP, 1 << 17, 1 << 16), 0)
    plan_ref[0:8, :] = tile * 32 + (lane & 15) + kind
    least = jnp.min(jnp.min(offset, axis=0, keepdims=True), axis=1, keepdims=True)
    plan_ref[8:16, :] = jnp.broadcast_to(jnp.where(top - 0.99 >= least, 1, 0), (8, 128))


def born_kernel(
    slab_ref, fill_ref, lists_ref, counts_ref, own_ref, p0_ref, p1_ref, p2_ref, p3_ref, radii_ref,
    blocks_ref, left_ref, right_ref, plan_ref, born_ref, send_ref,
    offsets_ref, acc_ref, buf0, buf1, buf2, buf3, buf4, buf5, buf6, buf7,
    near_ref, far_ref, index_ref, steps_ref, sums_ref, sem,
):
    slab = slab_ref[0]
    places = (2,) + slots(slab)
    packed = (own_ref, p0_ref, p1_ref, p2_ref, p3_ref)
    offset = radii_ref[...] - OFFSET
    plan_of(lists_ref, counts_ref, offset, packed, places, index_ref, plan_ref)
    copy = pltpu.make_async_copy(plan_ref, steps_ref, sem)
    copy.start()
    centre = (8 * slab + 4).astype(jnp.float32)
    for ref, place in zip(packed, places):
        fill_blocks(blocks_ref, right_ref, ref, place * TILES, centre)
    copy.wait()
    near = jnp.int32(0)
    far = jnp.int32(0)
    for g in range(TILES):
        for k in range(1, 8):
            entry = steps_ref[k, g]
            near_ref[near] = entry
            far_ref[far] = entry
            near = near + ((entry >> 16) & 1)
            far = far + (entry >> 17)
    pad_list(near_ref, near)
    pad_list(far_ref, far)
    fill_left(left_ref, blocks_ref)
    for g in range(TILES):
        offsets_ref[g] = column_of(offset[g : g + 1])
    offsets_ref[TILES] = offsets_ref[0]

    buffers = (buf0, buf1, buf2, buf3, buf4, buf5, buf6, buf7)

    def produce(w, g):
        return squares(left_ref, right_ref, g, w, 64)

    def near_term(soft, scaled, offset, inside):
        inverse = lax.rsqrt(soft)
        distance = soft * inverse
        upper = distance + scaled
        gap = distance - scaled
        lower = jnp.minimum(jnp.maximum(offset, jnp.abs(gap)), upper)
        ratio = 1.0 / (lower * upper)
        difference = (upper - lower) * ratio
        total = (upper + lower) * ratio
        weight = gap * upper * inverse
        logs = jnp.log(lower * lower * ratio)
        term = difference * (4.0 - weight * total) + (inverse + inverse) * logs
        if inside:
            term += jnp.where(offset < -gap, 16.0 * (1.0 / offset - 1.0 / lower), 0.0)
        return term

    def consume_near(inside, diagonal):
        def consume(w, slot, buffer):
            scaled = blocks_ref[w, 3:4, :]
            for v in range(8):
                rows = slice(16 * v, 16 * v + 16)
                c = jnp.broadcast_to(scaled, (16, 128))
                if diagonal:
                    same = rows_of((16, 128)) + 16 * v == rows_of((16, 128), 1)
                    c = jnp.where(same, 0.0, c)
                term = near_term(buffer[rows, :], c, offsets_ref[slot, rows, :], inside)
                if diagonal:
                    acc_ref[slot, rows, :] = term
                else:
                    acc_ref[slot, rows, :] += term

        return consume

    def consume_far(w, slot, buffer):
        scaled = blocks_ref[w, 3:4, :]
        for v in range(8):
            rows = slice(16 * v, 16 * v + 16)
            soft = buffer[rows, :]
            inverse = lax.rsqrt(soft)
            gap = soft * inverse - scaled
            ratio = 1.0 / (soft - scaled * scaled)
            logs = jnp.log(gap * gap * ratio)
            acc_ref[slot, rows, :] += (4.0 * scaled) * ratio + (inverse + inverse) * logs

    def near_lists(inside):
        run_list(TILES, own_entry, buffers[:4], produce, consume_near(inside, True))
        run_list(near, entry_in(near_ref), buffers[:4], produce, consume_near(inside, False))

    within = steps_ref[8, 0]
    pl.when(within == 0)(lambda: near_lists(False))
    pl.when(within != 0)(lambda: near_lists(True))
    run_list(far, entry_in(far_ref), buffers, produce, consume_far)

    for g in range(TILES):
        sums_ref[g : g + 1, :] = jnp.sum(acc_ref[g].T, axis=0, keepdims=True)
    slot = rows_of((TILES, 128)) * 128 + rows_of((TILES, 128), 1)
    live = slot < fill_ref[0]
    radius = jnp.where(live, radii_ref[...], 1.5)
    inner = radius - OFFSET
    psi = 0.125 * sums_ref[...] * inner
    bending = jnp.tanh(psi - 0.8 * psi * psi + 4.85 * psi * psi * psi)
    born = 1.0 / (1.0 / inner - bending / radius)
    born_ref[...] = jnp.where(live, born, 0.0)
    send_ref[...] = jnp.where(live, born, 1.0)


def energy_kernel(
    slab_ref, plan_ref, blocks_ref, left_ref, right_ref, own_ref, r0_ref, r1_ref, r2_ref, r3_ref,
    energy_ref, share_ref,
    born_ref, column_ref, inverse_ref, acc_ref, buf0, buf1, buf2, buf3, buf4, buf5, buf6, buf7,
    list_ref, steps_ref, charge_ref, sem,
):
    copy = pltpu.make_async_copy(plan_ref, steps_ref, sem)
    copy.start()
    places = (2,) + slots(slab_ref[0])
    for ref, place in zip((own_ref, r0_ref, r1_ref, r2_ref, r3_ref), places):
        born_ref[pl.ds(place * TILES, TILES), :] = ref[...]
    copy.wait()
    count = jnp.int32(0)
    for g in range(TILES):
        for k in range(1, 8):
            entry = steps_ref[k, g]
            list_ref[count] = entry
            count = count + jnp.minimum(entry >> 16, 1)
    pad_list(list_ref, count)
    for g in range(TILES):
        column = column_of(own_ref[g : g + 1, :])
        column_ref[g] = column
        inverse_ref[g] = (-0.25 * LOG2E) / column
    column_ref[TILES] = column_ref[0]
    inverse_ref[TILES] = inverse_ref[0]

    buffers = (buf0, buf1, buf2, buf3, buf4, buf5, buf6, buf7)

    def produce(w, g):
        return squares(left_ref, right_ref, g, w, 48)

    def consume(first):
        def body(w, slot, buffer):
            charge = blocks_ref[w, 4:5, :]
            partner = born_ref[pl.ds(w, 1), :]
            backward = 1.0 / partner
            for v in range(8):
                rows = slice(16 * v, 16 * v + 16)
                squared = buffer[rows, :]
                product = column_ref[slot, rows, :] * partner
                decay = jnp.exp2(squared * (inverse_ref[slot, rows, :] * backward))
                term = charge * lax.rsqrt(squared + product * decay)
                if first:
                    acc_ref[slot, rows, :] = term
                else:
                    acc_ref[slot, rows, :] += term

        return body

    run_list(TILES, own_entry, buffers, produce, consume(True))
    run_list(count, entry_in(list_ref), buffers, produce, consume(False))
    for g in range(TILES):
        energy_ref[g : g + 1, :] = jnp.sum(acc_ref[g].T, axis=0, keepdims=True)
        charge_ref[g : g + 1, :] = blocks_ref[2 * TILES + g, 4:5, :]
    energy = -0.5 * charge_ref[...] * energy_ref[...]
    energy_ref[...] = energy
    share = jnp.sum(jnp.sum(energy, axis=0, keepdims=True), axis=1, keepdims=True)
    share_ref[...] = jnp.broadcast_to(share[None], share_ref.shape)


def total_kernel(shares_ref, total_ref):
    total = shares_ref[0]
    for i in range(1, shares_ref.shape[0]):
        total = total + shares_ref[i]
    total_ref[0] = total[0, 0]


def shards(coords, charges, radii, screens, tile_lists, tile_counts, slab_fill):
    f32 = jnp.float32
    count = lax.axis_size(SLAB)
    smem = pl.BlockSpec(memory_space=pltpu.SMEM)
    vmem = pl.BlockSpec(memory_space=pltpu.VMEM)

    def near(value):
        return pltpu.with_memory_space_constraint(value, pltpu.VMEM)

    slab = lax.axis_index(SLAB).astype(jnp.int32)[None]
    charges, radii, screens = (v.reshape(TILES, 128) for v in (charges, radii, screens))
    packed = pl.pallas_call(
        prep_kernel,
        out_shape=pltpu.VMEM((ROWS, 128), f32),
        in_specs=[smem, smem] + [vmem] * 4,
        out_specs=vmem,
        name="prep",
    )(slab, slab_fill, coords, charges, radii, screens)
    around = neighbours(packed)
    squares = [pltpu.VMEM((128, 128), f32)] * 8
    stack = pltpu.VMEM((TILES + 1, 128, 128), f32)
    steps = pltpu.SMEM((16, 128), jnp.int32)
    blocks, left, right, plan, born, send = pl.pallas_call(
        born_kernel,
        out_shape=(
            pltpu.VMEM((5 * TILES, 8, 128), f32),
            pltpu.VMEM((TILES, 128, 64), jnp.bfloat16),
            pltpu.VMEM((5 * TILES, 64, 128), jnp.bfloat16),
            pltpu.VMEM((16, 128), jnp.int32),
            jax.ShapeDtypeStruct((TILES, 128), f32),
            pltpu.VMEM((TILES, 128), f32),
        ),
        in_specs=[smem] * 2 + [vmem] * 8,
        out_specs=(vmem,) * 6,
        scratch_shapes=[stack, stack]
        + squares
        + [pltpu.SMEM((144,), jnp.int32)] * 2
        + [pltpu.VMEM((16, 128), jnp.int32), steps, pltpu.VMEM((TILES, 128), f32), pltpu.SemaphoreType.DMA],
        name="born",
    )(
        slab, slab_fill, tile_lists.T, tile_counts.reshape(1, TILES),
        near(packed), *(near(value) for value in around), radii,
    )
    far_born = neighbours(send)
    energy, share = pl.pallas_call(
        energy_kernel,
        out_shape=(jax.ShapeDtypeStruct((TILES, 128), f32), pltpu.VMEM((count, 1, 128), f32)),
        in_specs=[smem] + [vmem] * 9,
        out_specs=(vmem,) * 2,
        scratch_shapes=[pltpu.VMEM((5 * TILES, 128), f32), stack, stack, stack]
        + squares
        + [pltpu.SMEM((144,), jnp.int32), steps, pltpu.VMEM((TILES, 128), f32), pltpu.SemaphoreType.DMA],
        name="energy",
    )(slab, *(near(value) for value in (plan, blocks, left, right, send, *far_born)))
    shares = lax.all_to_all(share, SLAB, 0, 0, tiled=True)
    total = pl.pallas_call(
        total_kernel,
        out_shape=jax.ShapeDtypeStruct((1,), f32),
        in_specs=[vmem],
        out_specs=smem,
        name="total",
    )(near(shares))
    return (born.reshape(-1), energy.reshape(-1), total[0])


def solution(mesh):
    torus = Mesh(mesh.devices.reshape(4, 8, 4, 2), SLAB)
    placed = (P(None, SLAB), P(SLAB), P(SLAB), P(SLAB), P(SLAB, None), P(SLAB), P(SLAB))
    return jax.shard_map(
        shards, mesh=torus, in_specs=placed, out_specs=(P(SLAB), P(SLAB), P()), check_vma=False
    )
```

time: 68.9 us -> 63.8 us (0.926); the launches traced: 69.4 us -> 63.4 us
  starting transfers between devices: 23 us -> 20.5 us
  Pallas kernels: 16.8 us -> 14.5 us
  other arithmetic: 0.87 us -> 0 us
  blocking collectives: 23.9 us -> 23.1 us
    ppermute x8, starting transfers between devices: 23 us -> 20.5 us  [neighbours(): lax.ppermute(value, SLAB, pairs)]
    pallas_call x2 -> x3, Pallas kernels: 10.9 us -> 9.41 us  [the longest x1 7.71 us: shards(): pl.pallas_call(born_kernel, out_shape=(pltpu.VMEM((5 * TILES, 8, 128), f3...]
    pallas_call x1, Pallas kernels: 5.92 us -> 5.05 us  [shards(): pl.pallas_call(energy_kernel, out_shape=(jax.ShapeDtypeStruct((TILES, 128...]
    reduce_sum x1 -> x0, other arithmetic: 0.87 us -> none  [shards(): total = jnp.sum(shares[:, 0, 0])]
    all_to_all x1, blocking collectives: 23.9 us -> 23.1 us  [shards(): shares = lax.all_to_all(share, SLAB, 0, 0, tiled=True)]
    unnamed x19 -> x4, local copies, waits for them, and re-layouts: 2.13 us -> 2.4 us
  transfers between devices with their start and end apart: 8 -> 8, of which waited for: 2 -> 2; matrix products, arithmetic and copies ran while one was open for 1% -> 0% of each run, Pallas kernels for 0% -> 0%
where the time goes in v2:
time: 63.8 us; the launch traced here: 63.4 us
  blocking collectives  23.1 us (36%)
  starting transfers between devices  20.5 us (32%)
  Pallas kernels  14.5 us (23%)
  local copies, waits for them, and re-layouts  2.4 us (4%)
  waiting for transfers between devices  1.7 us (3%)
  between operations  1.33 us (2%)
    all_to_all x1, blocking collectives, shards(): shares = lax.all_to_all(share, SLAB, 0, 0, tiled=True)  23.1 us
    ppermute x8, starting transfers between devices, neighbours(): lax.ppermute(value, SLAB, pairs)  20.5 us
    pallas_call x1, Pallas kernels, shards(): pl.pallas_call(born_kernel, out_shape=(pltpu.VMEM((5 * TILES, 8, 128), f3...  7.71 us
    pallas_call x1, Pallas kernels, shards(): pl.pallas_call(energy_kernel, out_shape=(jax.ShapeDtypeStruct((TILES, 128...  5.05 us
    unnamed x4, local copies, waits for them, and re-layouts  2.4 us
    ppermute x8, waiting for transfers between devices, neighbours(): lax.ppermute(value, SLAB, pairs)  1.7 us
  transfers between devices with their start and end apart: 8, of which 2 were waited for; matrix products, arithmetic and copies ran while one was open for 0% of the time, Pallas kernels for 0%

profile of v2, /device:TPU:1, one launch (start us, length us, event | category | flops | bytes accessed | tf_op | source)
XLA Modules:
  0.0 63.4 jit_solution(3726808550831739797)
XLA Ops:
  1.3 0.9 %prep.1.own_ref = f32[88,128]{1,0:T(8,128)S(1)} custom-call(s32[1]{0:T(128)} %bitcast.slab_ref, s32[1]{0:T(128)S(6)} %copy.10.fill_ref, f32[3,2048]{1,0:T(4,128)} %coords_ref.1, f32[16,128]{1,0:T(8,128)} %bitcast.11, f32[16,128]{1,0:T(8,128)} %bitcast.9, f32[16,128]{1,0:T(8,128)} %bitcast.12), custom_call_target="tpu_custom_call" | custom-call | tf_op jit(solution)/shard_map/prep/pallas_call | solution.py:368
  2.2 3.3 %collective-permute-start.3 = (f32[88,128]{1,0:T(8,128)S(1)}, f32[88,128]{1,0:T(8,128)S(1)}, u32[]{:S(2)}, u32[]{:S(2)}) collective-permute-start(f32[88,128]{1,0:T(8,128)S(1)} %prep.1.own_ref), channel_id=1, source_target_pairs={{0,1},{1,0},{2,4},{3,5},{4,2},{5,3},{6,8},{7,9},{8,6},{9,7},{10,12... | collective-permute-start | bytes 135176 | tf_op jit(solution)/shard_map/ppermute | solution.py:36
  5.5 0.2 collective-permute-start.2
  5.7 1.5 %collective-permute-start.1 = (f32[88,128]{1,0:T(8,128)S(1)}, f32[88,128]{1,0:T(8,128)S(1)}, u32[]{:S(2)}, u32[]{:S(2)}) collective-permute-start(f32[88,128]{1,0:T(8,128)S(1)} %prep.1.own_ref), channel_id=1, source_target_pairs={{0,255},{1,2},{2,1},{3,4},{4,3},{5,6},{6,5},{7,8},{8,7},{9,10},{10... | collective-permute-start | bytes 135176 | tf_op jit(solution)/shard_map/ppermute | solution.py:36
  7.2 7.2 %collective-permute-start = (f32[88,128]{1,0:T(8,128)S(1)}, f32[88,128]{1,0:T(8,128)S(1)}, u32[]{:S(2)}, u32[]{:S(2)}) collective-permute-start(f32[88,128]{1,0:T(8,128)S(1)} %prep.1.own_ref), channel_id=1, source_target_pairs={{0,1},{1,0},{2,3},{3,2},{4,5},{5,4},{6,7},{7,6},{8,9},{9,8},{10,11... | collective-permute-start | bytes 135176 | tf_op jit(solution)/shard_map/ppermute | solution.py:36
  14.4 0.0 collective-permute-done.3.p3_ref
  14.4 0.0 collective-permute-done.2.p2_ref
  14.4 0.0 collective-permute-done.1.p1_ref
  14.4 0.9 %collective-permute-done.p0_ref = f32[88,128]{1,0:T(8,128)S(1)} collective-permute-done((f32[88,128]{1,0:T(8,128)S(1)}, f32[88,128]{1,0:T(8,128)S(1)}, u32[]{:S(2)}, u32[]{:S(2)}) %collective-permute-start) | collective-permute-done | bytes 45088 | tf_op jit(solution)/shard_map/ppermute | solution.py:36
  15.3 7.7 %born.1 = (f32[80,8,128]{2,1,0:T(8,128)S(1)}, bf16[16,128,64]{2,1,0:T(8,128)(2,1)S(1)}, bf16[80,64,128]{2,1,0:T(8,128)(2,1)S(1)}, s32[16,128]{1,0:T(8,128)S(1)},...) custom-call(s32[1]{0:T(128)} %bitcast.slab_ref, s32[1]{0:T(128)S(6)} %copy.10.fill_ref, s32[8,16]{1,0:T(8,128)} %bitcast.13, ...), custom_call_target="tpu_custom_call" | custom-call | tf_op jit(solution)/shard_map/born/pallas_call | solution.py:379
  23.0 0.0 copy-start
  23.0 1.1 %copy-done = bf16[80,64,128]{2,1,0:T(8,128)(2,1)} copy-done((bf16[80,64,128]{2,1,0:T(8,128)(2,1)}, bf16[80,64,128]{2,1,0:T(8,128)(2,1)S(1)}, u32[]{:S(2)}) %copy-start) | copy-done | bytes 1310744
  24.1 1.1 %collective-permute-start.7 = (f32[16,128]{1,0:T(8,128)S(1)}, f32[16,128]{1,0:T(8,128)S(1)}, u32[]{:S(2)}, u32[]{:S(2)}) collective-permute-start(f32[16,128]{1,0:T(8,128)S(1)} %get-tuple-element.16.own_ref), channel_id=1, source_target_pairs={{0,1},{1,0},{2,4},{3,5},{4,2},{5,3},{6,8},{7,9},{8,6},{9,7},{10,12... | collective-permute-start | bytes 24584 | tf_op jit(solution)/shard_map/ppermute | solution.py:36
  25.2 0.0 collective-permute-start.6
  25.2 1.6 %collective-permute-start.5 = (f32[16,128]{1,0:T(8,128)S(1)}, f32[16,128]{1,0:T(8,128)S(1)}, u32[]{:S(2)}, u32[]{:S(2)}) collective-permute-start(f32[16,128]{1,0:T(8,128)S(1)} %get-tuple-element.16.own_ref), channel_id=1, source_target_pairs={{0,255},{1,2},{2,1},{3,4},{4,3},{5,6},{6,5},{7,8},{8,7},{9,10},{10... | collective-permute-start | bytes 24584 | tf_op jit(solution)/shard_map/ppermute | solution.py:36
  26.8 5.5 %collective-permute-start.4 = (f32[16,128]{1,0:T(8,128)S(1)}, f32[16,128]{1,0:T(8,128)S(1)}, u32[]{:S(2)}, u32[]{:S(2)}) collective-permute-start(f32[16,128]{1,0:T(8,128)S(1)} %get-tuple-element.16.own_ref), channel_id=1, source_target_pairs={{0,1},{1,0},{2,3},{3,2},{4,5},{5,4},{6,7},{7,6},{8,9},{9,8},{10,11... | collective-permute-start | bytes 24584 | tf_op jit(solution)/shard_map/ppermute | solution.py:36
  32.3 0.0 collective-permute-done.7.r3_ref
  32.3 0.0 collective-permute-done.6.r2_ref
  32.4 0.0 collective-permute-done.5.r1_ref
  32.4 0.8 %collective-permute-done.4.r0_ref = f32[16,128]{1,0:T(8,128)S(1)} collective-permute-done((f32[16,128]{1,0:T(8,128)S(1)}, f32[16,128]{1,0:T(8,128)S(1)}, u32[]{:S(2)}, u32[]{:S(2)}) %collective-permute-start.4) | collective-permute-done | bytes 8224 | tf_op jit(solution)/shard_map/ppermute | solution.py:36
  33.2 0.0 copy-start.1
  33.2 1.3 %copy-done.1 = bf16[80,64,128]{2,1,0:T(8,128)(2,1)S(1)} copy-done((bf16[80,64,128]{2,1,0:T(8,128)(2,1)S(1)}, bf16[80,64,128]{2,1,0:T(8,128)(2,1)}, u32[]{:S(2)}) %copy-start.1) | copy-done | bytes 1310744
  34.5 5.0 %energy.1 = (f32[16,128]{1,0:T(8,128)}, f32[256,1,128]{2,1,0:T(1,128)S(1)}) custom-call(s32[1]{0:T(128)} %bitcast.slab_ref, s32[16,128]{1,0:T(8,128)S(1)} %get-tuple-element.12.plan_ref, f32[80,8,128]{2,1,0:T(8,128)S(1)} %get-tuple-element.13.blocks_ref, bf16[16,128,64]{2,1,0:T(8,128)(2,1)S(1)} %get-tuple-element.14.left_ref, ...), custom_call_target="tpu_custom_call" | custom-call | tf_op jit(solution)/shard_map/energy/pallas_call | solution.py:401
  39.5 23.1 %all_to_all.5.shares_ref = f32[256,1,128]{2,1,0:T(1,128)S(1)} all-to-all(f32[256,1,128]{2,1,0:T(1,128)S(1)} %get-tuple-element.18), channel_id=1, replica_groups=mesh['slab_0'=4,'slab_1'=8,'slab_2'=4,'slab_3'=2] {'slab_0','slab_1','sl..., dimensions={0} | all-to-all | bytes 262144 | tf_op jit(solution)/shard_map/all_to_all | solution.py:411
  62.6 0.8 %total.1 = f32[1]{0:T(128)} custom-call(f32[256,1,128]{2,1,0:T(1,128)S(1)} %all_to_all.5.shares_ref), custom_call_target="tpu_custom_call" | custom-call | tf_op jit(solution)/shard_map/total/pallas_call | solution.py:412
Async XLA Ops:
  2.2 12.2 %collective-permute-start.3 = (f32[88,128]{1,0:T(8,128)S(1)}, f32[88,128]{1,0:T(8,128)S(1)}, u32[]{:S(2)}, u32[]{:S(2)}) collective-permute-start(f32[88,128]{1,0:T(8,128)S(1)} %prep.1.own_ref), channel_id=1, source_target_pairs={{0,1},{1,0},{2,4},{3,5},{4,2},{5,3},{6,8},{7,9},{8,6},{9,7},{10,12... | collective-permute-start | bytes 135176 | tf_op jit(solution)/shard_map/ppermute | solution.py:36
  5.5 8.9 %collective-permute-start.2 = (f32[88,128]{1,0:T(8,128)S(1)}, f32[88,128]{1,0:T(8,128)S(1)}, u32[]{:S(2)}, u32[]{:S(2)}) collective-permute-start(f32[88,128]{1,0:T(8,128)S(1)} %prep.1.own_ref), channel_id=1, source_target_pairs={{0,2},{1,3},{2,0},{3,1},{4,6},{5,7},{6,4},{7,5},{8,10},{9,11},{10,... | collective-permute-start | bytes 135176 | tf_op jit(solution)/shard_map/ppermute | solution.py:36
  5.7 8.7 %collective-permute-start.1 = (f32[88,128]{1,0:T(8,128)S(1)}, f32[88,128]{1,0:T(8,128)S(1)}, u32[]{:S(2)}, u32[]{:S(2)}) collective-permute-start(f32[88,128]{1,0:T(8,128)S(1)} %prep.1.own_ref), channel_id=1, source_target_pairs={{0,255},{1,2},{2,1},{3,4},{4,3},{5,6},{6,5},{7,8},{8,7},{9,10},{10... | collective-permute-start | bytes 135176 | tf_op jit(solution)/shard_map/ppermute | solution.py:36
  7.2 8.1 %collective-permute-start = (f32[88,128]{1,0:T(8,128)S(1)}, f32[88,128]{1,0:T(8,128)S(1)}, u32[]{:S(2)}, u32[]{:S(2)}) collective-permute-start(f32[88,128]{1,0:T(8,128)S(1)} %prep.1.own_ref), channel_id=1, source_target_pairs={{0,1},{1,0},{2,3},{3,2},{4,5},{5,4},{6,7},{7,6},{8,9},{9,8},{10,11... | collective-permute-start | bytes 135176 | tf_op jit(solution)/shard_map/ppermute | solution.py:36
  23.0 1.1 %copy-start = (bf16[80,64,128]{2,1,0:T(8,128)(2,1)}, bf16[80,64,128]{2,1,0:T(8,128)(2,1)S(1)}, u32[]{:S(2)}) copy-start(bf16[80,64,128]{2,1,0:T(8,128)(2,1)S(1)} %get-tuple-element.15.right_ref) | copy-start | bytes 3932164
  24.1 8.3 %collective-permute-start.7 = (f32[16,128]{1,0:T(8,128)S(1)}, f32[16,128]{1,0:T(8,128)S(1)}, u32[]{:S(2)}, u32[]{:S(2)}) collective-permute-start(f32[16,128]{1,0:T(8,128)S(1)} %get-tuple-element.16.own_ref), channel_id=1, source_target_pairs={{0,1},{1,0},{2,4},{3,5},{4,2},{5,3},{6,8},{7,9},{8,6},{9,7},{10,12... | collective-permute-start | bytes 24584 | tf_op jit(solution)/shard_map/ppermute | solution.py:36
  25.2 7.2 %collective-permute-start.6 = (f32[16,128]{1,0:T(8,128)S(1)}, f32[16,128]{1,0:T(8,128)S(1)}, u32[]{:S(2)}, u32[]{:S(2)}) collective-permute-start(f32[16,128]{1,0:T(8,128)S(1)} %get-tuple-element.16.own_ref), channel_id=1, source_target_pairs={{0,2},{1,3},{2,0},{3,1},{4,6},{5,7},{6,4},{7,5},{8,10},{9,11},{10,... | collective-permute-start | bytes 24584 | tf_op jit(solution)/shard_map/ppermute | solution.py:36
  25.2 7.2 %collective-permute-start.5 = (f32[16,128]{1,0:T(8,128)S(1)}, f32[16,128]{1,0:T(8,128)S(1)}, u32[]{:S(2)}, u32[]{:S(2)}) collective-permute-start(f32[16,128]{1,0:T(8,128)S(1)} %get-tuple-element.16.own_ref), channel_id=1, source_target_pairs={{0,255},{1,2},{2,1},{3,4},{4,3},{5,6},{6,5},{7,8},{8,7},{9,10},{10... | collective-permute-start | bytes 24584 | tf_op jit(solution)/shard_map/ppermute | solution.py:36
  26.8 6.4 %collective-permute-start.4 = (f32[16,128]{1,0:T(8,128)S(1)}, f32[16,128]{1,0:T(8,128)S(1)}, u32[]{:S(2)}, u32[]{:S(2)}) collective-permute-start(f32[16,128]{1,0:T(8,128)S(1)} %get-tuple-element.16.own_ref), channel_id=1, source_target_pairs={{0,1},{1,0},{2,3},{3,2},{4,5},{5,4},{6,7},{7,6},{8,9},{9,8},{10,11... | collective-permute-start | bytes 24584 | tf_op jit(solution)/shard_map/ppermute | solution.py:36
  33.2 1.3 %copy-start.1 = (bf16[80,64,128]{2,1,0:T(8,128)(2,1)S(1)}, bf16[80,64,128]{2,1,0:T(8,128)(2,1)}, u32[]{:S(2)}) copy-start(bf16[80,64,128]{2,1,0:T(8,128)(2,1)} %copy-done) | copy-start | bytes 3932164

commit v3 on v2

--- a/solution.py
+++ b/solution.py
@@ -15,31 +15,48 @@
 ROWS = 88
 
 
-def swaps(count):
-    def chip_swap(odd):
-        pairs = []
-        for chip in range(count // 2):
-            other = ((chip + odd) ^ 1) - odd
-            for core in (0, 1):
-                if 0 <= other < count // 2:
-                    pairs.append((2 * chip + core, 2 * other + core))
-                else:
-                    pairs.append((2 * chip + core, 2 * chip + 1 - core))
-        return pairs
-
-    inner = [(i, i ^ 1) for i in range(count)]
-    outer = [(i, (((i + 1) ^ 1) - 1) % count) for i in range(count)]
-    return inner, outer, chip_swap(0), chip_swap(1)
+def chip_swap(count, odd):
+    pairs = []
+    for chip in range(count // 2):
+        other = ((chip + odd) ^ 1) - odd
+        for core in (0, 1):
+            if 0 <= other < count // 2:
+                pairs.append((2 * chip + core, 2 * other + core))
+            else:
+                pairs.append((2 * chip + core, 2 * chip + 1 - core))
+    return pairs
 
 
 def neighbours(value):
-    return [lax.ppermute(value, SLAB, pairs) for pairs in swaps(lax.axis_size(SLAB))]
-
-
-def slots(slab):
-    inner = jnp.where(slab % 2 == 0, 3, 1)
-    chip = jnp.where((slab // 2) % 2 == 0, 4, 0)
-    return inner, 4 - inner, chip, 4 - chip
+    count = lax.axis_size(SLAB)
+    other = lax.ppermute(value, SLAB, [(i, i ^ 1) for i in range(count)])
+    both = jnp.concatenate([value, other], axis=0)
+    return [other] + [lax.ppermute(both, SLAB, chip_swap(count, odd)) for odd in (0, 1)]
+
+
+class Window:
+    def __init__(self, slab, own, other, even, odd):
+        core = slab % 2
+        ahead = (slab // 2) % 2 == 0
+        height = own.shape[0]
+        near = jnp.where(core == 0, 3, 1)
+        far = jnp.where(ahead, 4, 0)
+        from_even = ahead == (core == 1)
+
+        def crossed(start, size):
+            rows = pl.ds(height + start, size)
+            return jnp.where(from_even, even[rows, :], odd[rows, :])
+
+        def reader(ref):
+            return lambda start, size: ref[pl.ds(start, size), :]
+
+        self.slabs = (
+            (2, reader(own)),
+            (near, reader(other)),
+            (4 - near, crossed),
+            (far, reader(even)),
+            (4 - far, reader(odd)),
+        )
 
 
 def rows_of(shape, axis=0):
@@ -80,20 +97,23 @@
     return first, second, third
 
 
-def fill_blocks(blocks_ref, right_ref, packed_ref, base, centre):
+def fill_blocks(blocks_ref, read, base, centre):
     row = rows_of((8, 128))
     shift = jnp.where(row == 2, centre, 0.0)
     tail = jnp.where(row == 6, 1.0, 0.0)
-    last = jnp.where(rows_of((16, 128)) == 0, 1.0, 0.0)
     for t in range(TILES):
-        block = packed_ref[5 * t : 5 * t + 8, :] - shift
+        block = read(5 * t, 8) - shift
         square = block * block
         norm = square[0:1] + square[1:2] + square[2:3]
-        block = jnp.where(row < 5, block, jnp.where(row == 5, norm, tail))
-        blocks_ref[base + t] = block
-        b1, b2, b3 = parts_of(block)
+        blocks_ref[base + t] = jnp.where(row < 5, block, jnp.where(row == 5, norm, tail))
+
+
+def fill_right(right_ref, blocks_ref):
+    last = jnp.where(rows_of((16, 128)) == 0, 1.0, 0.0)
+    for w in range(5 * TILES):
+        b1, b2, b3 = parts_of(blocks_ref[w])
         stack = jnp.concatenate([b1, b2, b3, b1, b2, b1, last], axis=0)
-        right_ref[base + t] = stack.astype(jnp.bfloat16)
+        right_ref[w] = stack.astype(jnp.bfloat16)
 
 
 def fill_left(left_ref, blocks_ref):
@@ -156,15 +176,17 @@
     return entry_of
 
 
-def plan_of(lists_ref, counts_ref, offset, packed, places, index_ref, plan_ref):
+def plan_of(lists_ref, counts_ref, offset, window, index_ref, plan_ref):
     lane = rows_of((1, 128), 1)
     low = jnp.zeros((1, 128), jnp.float32)
     high = jnp.zeros((1, 128), jnp.float32)
-    top = packed[0][82:83, :]
-    for ref, place in zip(packed, places):
-        low = jnp.where(lane >> 4 == place, ref[80:81, :], low)
-        high = jnp.where(lane >> 4 == place, ref[81:82, :], high)
-        top = jnp.maximum(top, ref[82:83, :])
+    top = jnp.zeros((1, 128), jnp.float32)
+    for place, read in window.slabs:
+        ranges = read(80, 8)
+        low = jnp.where(lane >> 4 == place, ranges[0:1], low)
+        high = jnp.where(lane >> 4 == place, ranges[1:2], high)
+        top = jnp.maximum(top, ranges[2:3])
+    own = window.slabs[0][1](80, 8)
     index_ref[...] = jnp.zeros((16, 128), jnp.int32)
     index_ref[0:8, 0:TILES] = lists_ref[...]
     index_ref[8:9, 0:TILES] = counts_ref[...]
@@ -176,7 +198,7 @@
             jnp.broadcast_to(row, (8, 128)), tile, axis=1, mode="promise_in_bounds"
         )
 
-    gap = jnp.maximum(picked(low) - packed[0][81:82, :], packed[0][80:81, :] - picked(high))
+    gap = jnp.maximum(picked(low) - own[1:2], own[0:1] - picked(high))
     kind = jnp.where(used, jnp.where(gap >= FAR_GAP, 1 << 17, 1 << 16), 0)
     plan_ref[0:8, :] = tile * 32 + (lane & 15) + kind
     least = jnp.min(jnp.min(offset, axis=0, keepdims=True), axis=1, keepdims=True)
@@ -184,21 +206,21 @@
 
 
 def born_kernel(
-    slab_ref, fill_ref, lists_ref, counts_ref, own_ref, p0_ref, p1_ref, p2_ref, p3_ref, radii_ref,
-    blocks_ref, left_ref, right_ref, plan_ref, born_ref, send_ref,
-    offsets_ref, acc_ref, buf0, buf1, buf2, buf3, buf4, buf5, buf6, buf7,
+    slab_ref, fill_ref, lists_ref, counts_ref, own_ref, other_ref, even_ref, odd_ref, radii_ref,
+    blocks_ref, left_ref, plan_ref, born_ref, send_ref,
+    right_ref, offsets_ref, acc_ref, buf0, buf1, buf2, buf3, buf4, buf5, buf6, buf7,
     near_ref, far_ref, index_ref, steps_ref, sums_ref, sem,
 ):
     slab = slab_ref[0]
-    places = (2,) + slots(slab)
-    packed = (own_ref, p0_ref, p1_ref, p2_ref, p3_ref)
+    window = Window(slab, own_ref, other_ref, even_ref, odd_ref)
     offset = radii_ref[...] - OFFSET
-    plan_of(lists_ref, counts_ref, offset, packed, places, index_ref, plan_ref)
+    plan_of(lists_ref, counts_ref, offset, window, index_ref, plan_ref)
     copy = pltpu.make_async_copy(plan_ref, steps_ref, sem)
     copy.start()
     centre = (8 * slab + 4).astype(jnp.float32)
-    for ref, place in zip(packed, places):
-        fill_blocks(blocks_ref, right_ref, ref, place * TILES, centre)
+    for place, read in window.slabs:
+        fill_blocks(blocks_ref, read, place * TILES, centre)
+    fill_right(right_ref, blocks_ref)
     copy.wait()
     near = jnp.int32(0)
     far = jnp.int32(0)
@@ -288,16 +310,17 @@
 
 
 def energy_kernel(
-    slab_ref, plan_ref, blocks_ref, left_ref, right_ref, own_ref, r0_ref, r1_ref, r2_ref, r3_ref,
+    slab_ref, plan_ref, blocks_ref, left_ref, own_ref, other_ref, even_ref, odd_ref,
     energy_ref, share_ref,
-    born_ref, column_ref, inverse_ref, acc_ref, buf0, buf1, buf2, buf3, buf4, buf5, buf6, buf7,
+    right_ref, born_ref, column_ref, inverse_ref, acc_ref, buf0, buf1, buf2, buf3, buf4, buf5, buf6, buf7,
     list_ref, steps_ref, charge_ref, sem,
 ):
     copy = pltpu.make_async_copy(plan_ref, steps_ref, sem)
     copy.start()
-    places = (2,) + slots(slab_ref[0])
-    for ref, place in zip((own_ref, r0_ref, r1_ref, r2_ref, r3_ref), places):
-        born_ref[pl.ds(place * TILES, TILES), :] = ref[...]
+    window = Window(slab_ref[0], own_ref, other_ref, even_ref, odd_ref)
+    for place, read in window.slabs:
+        born_ref[pl.ds(place * TILES, TILES), :] = read(0, TILES)
+    fill_right(right_ref, blocks_ref)
     copy.wait()
     count = jnp.int32(0)
     for g in range(TILES):
@@ -375,20 +398,20 @@
     around = neighbours(packed)
     squares = [pltpu.VMEM((128, 128), f32)] * 8
     stack = pltpu.VMEM((TILES + 1, 128, 128), f32)
+    right = pltpu.VMEM((5 * TILES, 64, 128), jnp.bfloat16)
     steps = pltpu.SMEM((16, 128), jnp.int32)
-    blocks, left, right, plan, born, send = pl.pallas_call(
+    blocks, left, plan, born, send = pl.pallas_call(
         born_kernel,
         out_shape=(
             pltpu.VMEM((5 * TILES, 8, 128), f32),
             pltpu.VMEM((TILES, 128, 64), jnp.bfloat16),
-            pltpu.VMEM((5 * TILES, 64, 128), jnp.bfloat16),
             pltpu.VMEM((16, 128), jnp.int32),
             jax.ShapeDtypeStruct((TILES, 128), f32),
             pltpu.VMEM((TILES, 128), f32),
         ),
-        in_specs=[smem] * 2 + [vmem] * 8,
-        out_specs=(vmem,) * 6,
-        scratch_shapes=[stack, stack]
+        in_specs=[smem] * 2 + [vmem] * 7,
+        out_specs=(vmem,) * 5,
+        scratch_shapes=[right, stack, stack]
         + squares
         + [pltpu.SMEM((144,), jnp.int32)] * 2
         + [pltpu.VMEM((16, 128), jnp.int32), steps, pltpu.VMEM((TILES, 128), f32), pltpu.SemaphoreType.DMA],
@@ -401,13 +424,13 @@
     energy, share = pl.pallas_call(
         energy_kernel,
         out_shape=(jax.ShapeDtypeStruct((TILES, 128), f32), pltpu.VMEM((count, 1, 128), f32)),
-        in_specs=[smem] + [vmem] * 9,
+        in_specs=[smem] + [vmem] * 7,
         out_specs=(vmem,) * 2,
-        scratch_shapes=[pltpu.VMEM((5 * TILES, 128), f32), stack, stack, stack]
+        scratch_shapes=[right, pltpu.VMEM((5 * TILES, 128), f32), stack, stack, stack]
         + squares
         + [pltpu.SMEM((144,), jnp.int32), steps, pltpu.VMEM((TILES, 128), f32), pltpu.SemaphoreType.DMA],
         name="energy",
-    )(slab, *(near(value) for value in (plan, blocks, left, right, send, *far_born)))
+    )(slab, *(near(value) for value in (plan, blocks, left, send, *far_born)))
     shares = lax.all_to_all(share, SLAB, 0, 0, tiled=True)
     total = pl.pallas_call(
         total_kernel,

time: 63.8 us -> 63.3 us (level)
  starting transfers between devices: 20.5 us -> 5.52 us
  blocking collectives: 23.1 us -> 31.7 us
  waiting for transfers between devices: 1.7 us -> 7.14 us
  Pallas kernels: 14.5 us -> 17 us
  local copies, waits for them, and re-layouts: 2.4 us -> 0.01 us
    ppermute x8 -> x6, starting transfers between devices: 20.5 us -> 5.52 us  [the longest x2 3.38 us: neighbours(): other = lax.ppermute(value, SLAB, [(i, i ^ 1) for i in range(count)])]
    all_to_all x1, blocking collectives: 23.1 us -> 31.7 us  [shards(): shares = lax.all_to_all(share, SLAB, 0, 0, tiled=True)]
    ppermute x8 -> x6, waiting for transfers between devices: 1.7 us -> 7.14 us  [the longest x4 5.12 us: neighbours(): lax.ppermute(both, SLAB, chip_swap(count, odd))]
    unnamed x4 -> x1, local copies, waits for them, and re-layouts: 2.4 us -> 0.01 us
    pallas_call x1, Pallas kernels: 7.71 us -> 9.34 us  [shards(): pl.pallas_call(born_kernel, out_shape=(pltpu.VMEM((5 * TILES, 8, 128), f3...]
    pallas_call x1, Pallas kernels: 5.05 us -> 5.98 us  [shards(): pl.pallas_call(energy_kernel, out_shape=(jax.ShapeDtypeStruct((TILES, 128...]
  transfers between devices with their start and end apart: 8 -> 6, of which waited for: 2 -> 5; matrix products, arithmetic and copies ran while one was open for 0% -> 0% of each run, Pallas kernels for 0% -> 0%
where the time goes in v3:
time: 63.3 us; the launch traced here: 62.8 us
  blocking collectives  31.7 us (50%)
  Pallas kernels  17 us (27%)
  waiting for transfers between devices  7.14 us (11%)
  starting transfers between devices  5.52 us (9%)
  between operations  1.33 us (2%)
    all_to_all x1, blocking collectives, shards(): shares = lax.all_to_all(share, SLAB, 0, 0, tiled=True)  31.7 us
    pallas_call x1, Pallas kernels, shards(): pl.pallas_call(born_kernel, out_shape=(pltpu.VMEM((5 * TILES, 8, 128), f3...  9.34 us
    pallas_call x1, Pallas kernels, shards(): pl.pallas_call(energy_kernel, out_shape=(jax.ShapeDtypeStruct((TILES, 128...  5.98 us
    ppermute x4, waiting for transfers between devices, neighbours(): lax.ppermute(both, SLAB, chip_swap(count, odd))  5.12 us
    ppermute x2, starting transfers between devices, neighbours(): other = lax.ppermute(value, SLAB, [(i, i ^ 1) for i in range(count)])  3.38 us
    ppermute x4, starting transfers between devices, neighbours(): lax.ppermute(both, SLAB, chip_swap(count, odd))  2.14 us
    ppermute x2, waiting for transfers between devices, neighbours(): other = lax.ppermute(value, SLAB, [(i, i ^ 1) for i in range(count)])  2.02 us
  transfers between devices with their start and end apart: 6, of which 5 were waited for; matrix products, arithmetic and copies ran while one was open for 0% of the time, Pallas kernels for 0%

profile of v3, /device:TPU:1, one launch (start us, length us, event | category | flops | bytes accessed | tf_op | source)
XLA Modules:
  0.0 62.8 jit_solution(3011791612681741508)
XLA Ops:
  1.3 0.9 %prep.1.own_ref = f32[88,128]{1,0:T(8,128)S(1)} custom-call(s32[1]{0:T(128)} %bitcast.slab_ref, s32[1]{0:T(128)S(6)} %copy.11.fill_ref, f32[3,2048]{1,0:T(4,128)} %coords_ref.1, f32[16,128]{1,0:T(8,128)} %bitcast.11, f32[16,128]{1,0:T(8,128)} %bitcast.9, f32[16,128]{1,0:T(8,128)} %bitcast.12), custom_call_target="tpu_custom_call" | custom-call | tf_op jit(solution)/shard_map/prep/pallas_call | solution.py:391
  2.2 3.3 %collective-permute-start = (f32[88,128]{1,0:T(8,128)S(1)}, f32[88,128]{1,0:T(8,128)S(1)}, u32[]{:S(2)}, u32[]{:S(2)}) collective-permute-start(f32[88,128]{1,0:T(8,128)S(1)} %prep.1.own_ref), channel_id=1, source_target_pairs={{0,1},{1,0},{2,3},{3,2},{4,5},{5,4},{6,7},{7,6},{8,9},{9,8},{10,11... | collective-permute-start | bytes 135176 | tf_op jit(solution)/shard_map/ppermute | solution.py:32
  5.5 0.9 %collective-permute-done.other_ref = f32[88,128]{1,0:T(8,128)S(1)} collective-permute-done((f32[88,128]{1,0:T(8,128)S(1)}, f32[88,128]{1,0:T(8,128)S(1)}, u32[]{:S(2)}, u32[]{:S(2)}) %collective-permute-start) | collective-permute-done | bytes 45088 | tf_op jit(solution)/shard_map/ppermute | solution.py:32
  6.3 0.4 collective-permute-start.2
  6.8 0.5 collective-permute-start.1
  7.2 0.5 collective-permute-done.2.odd_ref
  7.7 3.1 %collective-permute-done.1.even_ref = f32[176,128]{1,0:T(8,128)S(1)} collective-permute-done((f32[176,128]{1,0:T(8,128)S(1)}, f32[176,128]{1,0:T(8,128)S(1)}, u32[]{:S(2)}, u32[]{:S(2)}) %collective-permute-start.1) | collective-permute-done | bytes 90144 | tf_op jit(solution)/shard_map/ppermute | solution.py:34
  10.9 9.3 %born.1 = (f32[80,8,128]{2,1,0:T(8,128)S(1)}, bf16[16,128,64]{2,1,0:T(8,128)(2,1)S(1)}, s32[16,128]{1,0:T(8,128)S(1)}, f32[16,128]{1,0:T(8,128)}, f32[16,128]{1,0:T(8,128)S(1)}) custom-call(s32[1]{0:T(128)} %bitcast.slab_ref, s32[1]{0:T(128)S(6)} %copy.11.fill_ref, s32[8,16]{1,0:T(8,128)} %bitcast.13, s32[1,16]{1,0:T(1,128)} %bitcast.14, ...), custom_call_target="tpu_custom_call" | custom-call | tf_op jit(solution)/shard_map/born/pallas_call | solution.py:403
  20.2 0.1 collective-permute-start.3
  20.3 1.1 %collective-permute-done.3.other_ref = f32[16,128]{1,0:T(8,128)S(1)} collective-permute-done((f32[16,128]{1,0:T(8,128)S(1)}, f32[16,128]{1,0:T(8,128)S(1)}, u32[]{:S(2)}, u32[]{:S(2)}) %collective-permute-start.3) | collective-permute-done | bytes 8224 | tf_op jit(solution)/shard_map/ppermute | solution.py:32
  21.5 0.2 collective-permute-start.5
  21.6 1.1 %collective-permute-start.4 = (f32[32,128]{1,0:T(8,128)S(1)}, f32[32,128]{1,0:T(8,128)S(1)}, u32[]{:S(2)}, u32[]{:S(2)}) collective-permute-start(f32[32,128]{1,0:T(8,128)S(1)} %constant_dynamic-update-slice_fusion), channel_id=1, source_target_pairs={{0,2},{1,3},{2,0},{3,1},{4,6},{5,7},{6,4},{7,5},{8,10},{9,11},{10,... | collective-permute-start | bytes 49160 | tf_op jit(solution)/shard_map/ppermute | solution.py:34
  22.7 0.0 collective-permute-done.5.odd_ref
  22.7 1.5 %collective-permute-done.4.even_ref = f32[32,128]{1,0:T(8,128)S(1)} collective-permute-done((f32[32,128]{1,0:T(8,128)S(1)}, f32[32,128]{1,0:T(8,128)S(1)}, u32[]{:S(2)}, u32[]{:S(2)}) %collective-permute-start.4) | collective-permute-done | bytes 16416 | tf_op jit(solution)/shard_map/ppermute | solution.py:34
  24.2 6.0 %energy.1 = (f32[16,128]{1,0:T(8,128)}, f32[256,1,128]{2,1,0:T(1,128)S(1)}) custom-call(s32[1]{0:T(128)} %bitcast.slab_ref, s32[16,128]{1,0:T(8,128)S(1)} %get-tuple-element.11.plan_ref, f32[80,8,128]{2,1,0:T(8,128)S(1)} %get-tuple-element.12.blocks_ref, bf16[16,128,64]{2,1,0:T(8,128)(2,1)S(1)} %get-tuple-element.13.left_ref, ...), custom_call_target="tpu_custom_call" | custom-call | tf_op jit(solution)/shard_map/energy/pallas_call | solution.py:424
  30.2 31.7 %all_to_all.5.shares_ref = f32[256,1,128]{2,1,0:T(1,128)S(1)} all-to-all(f32[256,1,128]{2,1,0:T(1,128)S(1)} %get-tuple-element.16), channel_id=1, replica_groups=mesh['slab_0'=4,'slab_1'=8,'slab_2'=4,'slab_3'=2] {'slab_0','slab_1','sl..., dimensions={0} | all-to-all | bytes 262144 | tf_op jit(solution)/shard_map/all_to_all | solution.py:434
  61.9 0.8 %total.1 = f32[1]{0:T(128)} custom-call(f32[256,1,128]{2,1,0:T(1,128)S(1)} %all_to_all.5.shares_ref), custom_call_target="tpu_custom_call" | custom-call | tf_op jit(solution)/shard_map/total/pallas_call | solution.py:435
  (3 shorter events, 0.0 us)
Async XLA Ops:
  2.2 4.2 %collective-permute-start = (f32[88,128]{1,0:T(8,128)S(1)}, f32[88,128]{1,0:T(8,128)S(1)}, u32[]{:S(2)}, u32[]{:S(2)}) collective-permute-start(f32[88,128]{1,0:T(8,128)S(1)} %prep.1.own_ref), channel_id=1, source_target_pairs={{0,1},{1,0},{2,3},{3,2},{4,5},{5,4},{6,7},{7,6},{8,9},{9,8},{10,11... | collective-permute-start | bytes 135176 | tf_op jit(solution)/shard_map/ppermute | solution.py:32
  6.3 1.4 %collective-permute-start.2 = (f32[176,128]{1,0:T(8,128)S(1)}, f32[176,128]{1,0:T(8,128)S(1)}, u32[]{:S(2)}, u32[]{:S(2)}) collective-permute-start(f32[176,128]{1,0:T(8,128)S(1)} %pad_maximum_fusion), channel_id=1, source_target_pairs={{0,1},{1,0},{2,4},{3,5},{4,2},{5,3},{6,8},{7,9},{8,6},{9,7},{10,12... | collective-permute-start | bytes 270344 | tf_op jit(solution)/shard_map/ppermute | solution.py:34
  6.8 4.1 %collective-permute-start.1 = (f32[176,128]{1,0:T(8,128)S(1)}, f32[176,128]{1,0:T(8,128)S(1)}, u32[]{:S(2)}, u32[]{:S(2)}) collective-permute-start(f32[176,128]{1,0:T(8,128)S(1)} %pad_maximum_fusion), channel_id=1, source_target_pairs={{0,2},{1,3},{2,0},{3,1},{4,6},{5,7},{6,4},{7,5},{8,10},{9,11},{10,... | collective-permute-start | bytes 270344 | tf_op jit(solution)/shard_map/ppermute | solution.py:34
  20.2 1.3 %collective-permute-start.3 = (f32[16,128]{1,0:T(8,128)S(1)}, f32[16,128]{1,0:T(8,128)S(1)}, u32[]{:S(2)}, u32[]{:S(2)}) collective-permute-start(f32[16,128]{1,0:T(8,128)S(1)} %get-tuple-element.14.own_ref), channel_id=1, source_target_pairs={{0,1},{1,0},{2,3},{3,2},{4,5},{5,4},{6,7},{7,6},{8,9},{9,8},{10,11... | collective-permute-start | bytes 24584 | tf_op jit(solution)/shard_map/ppermute | solution.py:32
  21.5 1.3 %collective-permute-start.5 = (f32[32,128]{1,0:T(8,128)S(1)}, f32[32,128]{1,0:T(8,128)S(1)}, u32[]{:S(2)}, u32[]{:S(2)}) collective-permute-start(f32[32,128]{1,0:T(8,128)S(1)} %constant_dynamic-update-slice_fusion), channel_id=1, source_target_pairs={{0,1},{1,0},{2,4},{3,5},{4,2},{5,3},{6,8},{7,9},{8,6},{9,7},{10,12... | collective-permute-start | bytes 49160 | tf_op jit(solution)/shard_map/ppermute | solution.py:34
  21.6 2.6 %collective-permute-start.4 = (f32[32,128]{1,0:T(8,128)S(1)}, f32[32,128]{1,0:T(8,128)S(1)}, u32[]{:S(2)}, u32[]{:S(2)}) collective-permute-start(f32[32,128]{1,0:T(8,128)S(1)} %constant_dynamic-update-slice_fusion), channel_id=1, source_target_pairs={{0,2},{1,3},{2,0},{3,1},{4,6},{5,7},{6,4},{7,5},{8,10},{9,11},{10,... | collective-permute-start | bytes 49160 | tf_op jit(solution)/shard_map/ppermute | solution.py:34

commit v4 on v2

v4 whole, which is shorter than its diff:
```python
import jax
import jax.numpy as jnp
from jax import lax
from jax.experimental import pallas as pl
from jax.experimental.pallas import tpu as pltpu
from jax.sharding import Mesh
from jax.sharding import PartitionSpec as P

SLAB = ("slab_0", "slab_1", "slab_2", "slab_3")
OFFSET = 0.09
LOG2E = 1.4426950408889634
TILES = 16
UNROLL = 8
FAR_GAP = 3.5
ROWS = 88


def swaps(count):
    def chip_swap(odd):
        pairs = []
        for chip in range(count // 2):
            other = ((chip + odd) ^ 1) - odd
            for core in (0, 1):
                if 0 <= other < count // 2:
                    pairs.append((2 * chip + core, 2 * other + core))
                else:
                    pairs.append((2 * chip + core, 2 * chip + 1 - core))
        return pairs

    inner = [(i, i ^ 1) for i in range(count)]
    outer = [(i, (((i + 1) ^ 1) - 1) % count) for i in range(count)]
    return inner, outer, chip_swap(0), chip_swap(1)


def neighbours(value):
    return [lax.ppermute(value, SLAB, pairs) for pairs in swaps(lax.axis_size(SLAB))]


def slots(slab):
    inner = jnp.where(slab % 2 == 0, 3, 1)
    chip = jnp.where((slab // 2) % 2 == 0, 4, 0)
    return inner, 4 - inner, chip, 4 - chip


def rows_of(shape, axis=0):
    return lax.broadcasted_iota(jnp.int32, shape, axis)


def prep_kernel(slab_ref, fill_ref, coords_ref, charges_ref, radii_ref, screens_ref, out_ref):
    fill = fill_ref[0]
    middle = (8 * slab_ref[0] + 4).astype(jnp.float32)
    slot = rows_of((TILES, 128)) * 128 + rows_of((TILES, 128), 1)
    live = slot < fill
    scaled = jnp.where(live, screens_ref[...] * (radii_ref[...] - OFFSET), 0.0)
    charge = jnp.where(live, charges_ref[...], 0.0)
    home = jnp.where(rows_of((3, 128)) == 2, middle, 0.0)
    lane = rows_of((3, 128), 1)
    column = rows_of((1, 128), 1) % TILES
    low = jnp.zeros((1, 128), jnp.float32)
    high = jnp.zeros((1, 128), jnp.float32)
    for t in range(TILES):
        xyz = jnp.where(lane + t * 128 < fill, coords_ref[:, t * 128 : (t + 1) * 128], home)
        out_ref[5 * t : 5 * t + 3, :] = xyz
        out_ref[5 * t + 3 : 5 * t + 4, :] = scaled[t : t + 1]
        out_ref[5 * t + 4 : 5 * t + 5, :] = charge[t : t + 1]
        low = jnp.where(column == t, jnp.min(xyz[2:3], axis=1, keepdims=True), low)
        high = jnp.where(column == t, jnp.max(xyz[2:3], axis=1, keepdims=True), high)
    top = jnp.max(jnp.max(scaled, axis=0, keepdims=True), axis=1, keepdims=True)
    out_ref[80:81, :] = low
    out_ref[81:82, :] = high
    out_ref[82:83, :] = jnp.broadcast_to(top, (1, 128))
    out_ref[83:88, :] = jnp.zeros((5, 128), jnp.float32)


def parts_of(rows):
    first = rows.astype(jnp.bfloat16).astype(jnp.float32)
    rest = rows - first
    second = rest.astype(jnp.bfloat16).astype(jnp.float32)
    third = (rest - second).astype(jnp.bfloat16).astype(jnp.float32)
    return first, second, third


def fill_blocks(blocks_ref, packed_ref, base, centre):
    row = rows_of((8, 128))
    shift = jnp.where(row == 2, centre, 0.0)
    tail = jnp.where(row == 6, 1.0, 0.0)
    for t in range(TILES):
        block = packed_ref[5 * t : 5 * t + 8, :] - shift
        square = block * block
        norm = square[0:1] + square[1:2] + square[2:3]
        blocks_ref[base + t] = jnp.where(row < 5, block, jnp.where(row == 5, norm, tail))


def fill_right(right_ref, blocks_ref, base):
    last = jnp.where(rows_of((16, 128)) == 0, 1.0, 0.0)
    for t in range(TILES):
        b1, b2, b3 = parts_of(blocks_ref[base + t])
        stack = jnp.concatenate([b1, b2, b3, b1, b2, b1, last], axis=0)
        right_ref[base + t] = stack.astype(jnp.bfloat16)


def fill_left(left_ref, blocks_ref):
    row = rows_of((8, 128))
    last = jnp.where(rows_of((16, 128)) == 0, 1.0, 0.0)
    for g in range(TILES):
        block = blocks_ref[2 * TILES + g]
        norm = jnp.broadcast_to(block[5:6], (8, 128))
        left = jnp.where(
            row < 3, -2.0 * block, jnp.where(row == 5, 1.0, jnp.where(row == 6, norm, 0.0))
        )
        a1, a2, a3 = parts_of(left)
        stack = jnp.concatenate([a1, a1, a1, a2, a2, a3, last], axis=0)
        left_ref[g] = stack.T.astype(jnp.bfloat16)


def column_of(row):
    return jnp.broadcast_to(row, (128, 128)).T


def squares(left_ref, right_ref, g, w, depth):
    return jnp.dot(
        left_ref[g, :, :depth], right_ref[w, :depth, :], preferred_element_type=jnp.float32
    )


def run_list(count, entry_of, buffers, produce, consume):
    unroll = len(buffers)

    def fetch(base):
        for u, buffer in enumerate(buffers):
            w, slot = entry_of(base + u)
            buffer[...] = produce(w, jnp.minimum(slot, TILES - 1))

    fetch(0)

    @pl.loop(0, (count + unroll - 1) // unroll)
    def _(step):
        base = step * unroll
        for u, buffer in enumerate(buffers):
            w, slot = entry_of(base + u)
            consume(w, slot, buffer)
        fetch(base + unroll)


def own_entry(index):
    return 2 * TILES + jnp.minimum(index, TILES - 1), index


def pad_list(list_ref, count):
    for u in range(2 * UNROLL):
        list_ref[count + u] = 2 * TILES * 32 + TILES


def entry_in(list_ref):
    def entry_of(index):
        entry = list_ref[index]
        return (entry >> 5) & 127, entry & 31

    return entry_of


def plan_of(lists_ref, counts_ref, least, sources, index_ref, plan_ref, own_ref):
    lane = rows_of((1, 128), 1)
    low = jnp.zeros((1, 128), jnp.float32)
    high = jnp.zeros((1, 128), jnp.float32)
    top = jnp.zeros((1, 128), jnp.float32)
    index_ref[...] = jnp.zeros((16, 128), jnp.int32)
    index_ref[0:8, 0:TILES] = lists_ref[...]
    index_ref[8:9, 0:TILES] = counts_ref[...]
    tile = index_ref[0:8, :]
    here = jnp.zeros((8, 128), jnp.int32)
    for place, ref in sources:
        low = jnp.where(lane >> 4 == place, ref[80:81, :], low)
        high = jnp.where(lane >> 4 == place, ref[81:82, :], high)
        top = jnp.maximum(top, ref[82:83, :])
        here = jnp.where(tile >> 4 == place, 1, here)
    used = (rows_of((8, 128)) > 0) & (rows_of((8, 128)) < index_ref[8:9, :]) & (here > 0)

    def picked(row):
        return jnp.take_along_axis(
            jnp.broadcast_to(row, (8, 128)), tile, axis=1, mode="promise_in_bounds"
        )

    gap = jnp.maximum(picked(low) - own_ref[81:82, :], own_ref[80:81, :] - picked(high))
    kind = jnp.where(used, jnp.where(gap >= FAR_GAP, 1 << 17, 1 << 16), 0)
    plan_ref[0:8, :] = tile * 32 + (lane & 15) + kind
    plan_ref[8:16, :] = jnp.broadcast_to(jnp.where(top - 0.99 >= least, 1, 0), (8, 128))


def near_term(soft, scaled, offset, inside):
    inverse = lax.rsqrt(soft)
    distance = soft * inverse
    upper = distance + scaled
    gap = distance - scaled
    lower = jnp.minimum(jnp.maximum(offset, jnp.abs(gap)), upper)
    ratio = 1.0 / (lower * upper)
    difference = (upper - lower) * ratio
    total = (upper + lower) * ratio
    weight = gap * upper * inverse
    logs = jnp.log(lower * lower * ratio)
    term = difference * (4.0 - weight * total) + (inverse + inverse) * logs
    if inside:
        term += jnp.where(offset < -gap, 16.0 * (1.0 / offset - 1.0 / lower), 0.0)
    return term


def split_lists(steps_ref, near_ref, far_ref):
    near = jnp.int32(0)
    far = jnp.int32(0)
    for g in range(TILES):
        for k in range(1, 8):
            entry = steps_ref[k, g]
            near_ref[near] = entry
            far_ref[far] = entry
            near = near + ((entry >> 16) & 1)
            far = far + (entry >> 17)
    pad_list(near_ref, near)
    pad_list(far_ref, far)
    return near, far


def sum_pairs(left_ref, right_ref, blocks_ref, offsets_ref, acc_ref, buffers, lists, counts, within, own):
    def produce(w, g):
        return squares(left_ref, right_ref, g, w, 64)

    def consume_near(inside, diagonal):
        def consume(w, slot, buffer):
            scaled = blocks_ref[w, 3:4, :]
            for v in range(8):
                rows = slice(16 * v, 16 * v + 16)
                c = jnp.broadcast_to(scaled, (16, 128))
                if diagonal:
                    same = rows_of((16, 128)) + 16 * v == rows_of((16, 128), 1)
                    c = jnp.where(same, 0.0, c)
                term = near_term(buffer[rows, :], c, offsets_ref[slot, rows, :], inside)
                if diagonal:
                    acc_ref[slot, rows, :] = term
                else:
                    acc_ref[slot, rows, :] += term

        return consume

    def consume_far(w, slot, buffer):
        scaled = blocks_ref[w, 3:4, :]
        for v in range(8):
            rows = slice(16 * v, 16 * v + 16)
            soft = buffer[rows, :]
            inverse = lax.rsqrt(soft)
            gap = soft * inverse - scaled
            ratio = 1.0 / (soft - scaled * scaled)
            logs = jnp.log(gap * gap * ratio)
            acc_ref[slot, rows, :] += (4.0 * scaled) * ratio + (inverse + inverse) * logs

    def near_lists(inside):
        if own:
            run_list(TILES, own_entry, buffers[:4], produce, consume_near(inside, True))
        run_list(counts[0], entry_in(lists[0]), buffers[:4], produce, consume_near(inside, False))

    pl.when(within == 0)(lambda: near_lists(False))
    pl.when(within != 0)(lambda: near_lists(True))
    run_list(counts[1], entry_in(lists[1]), buffers[:4] if own else buffers, produce, consume_far)


def least_of(offset):
    return jnp.min(jnp.min(offset, axis=0, keepdims=True), axis=1, keepdims=True)


def born_own_kernel(
    slab_ref, lists_ref, counts_ref, own_ref, radii_ref,
    blocks_ref, left_ref, right_ref, offsets_ref, acc_ref, plan_ref,
    near_ref, far_ref, index_ref, steps_ref, sem, *buffers,
):
    offset = radii_ref[...] - OFFSET
    plan_of(lists_ref, counts_ref, least_of(offset), ((2, own_ref),), index_ref, plan_ref, own_ref)
    copy = pltpu.make_async_copy(plan_ref, steps_ref, sem)
    copy.start()
    centre = (8 * slab_ref[0] + 4).astype(jnp.float32)
    fill_blocks(blocks_ref, own_ref, 2 * TILES, centre)
    fill_right(right_ref, blocks_ref, 2 * TILES)
    fill_left(left_ref, blocks_ref)
    for g in range(TILES):
        offsets_ref[g] = column_of(offset[g : g + 1])
    offsets_ref[TILES] = offsets_ref[0]
    copy.wait()
    counts = split_lists(steps_ref, near_ref, far_ref)
    sum_pairs(
        left_ref, right_ref, blocks_ref, offsets_ref, acc_ref, buffers,
        (near_ref, far_ref), counts, steps_ref[8, 0], True,
    )


def born_rest_kernel(
    slab_ref, fill_ref, lists_ref, counts_ref, own_ref, p0_ref, p1_ref, p2_ref, p3_ref, radii_ref,
    left_ref, offsets_ref, blocks_in, right_in, acc_in,
    plan_ref, born_ref, send_ref, blocks_ref, right_ref, acc_ref,
    near_ref, far_ref, index_ref, steps_ref, sem, sums_ref, *buffers,
):
    slab = slab_ref[0]
    sources = tuple(zip(slots(slab), (p0_ref, p1_ref, p2_ref, p3_ref)))
    offset = radii_ref[...] - OFFSET
    plan_of(lists_ref, counts_ref, least_of(offset), sources, index_ref, plan_ref, own_ref)
    copy = pltpu.make_async_copy(plan_ref, steps_ref, sem)
    copy.start()
    centre = (8 * slab + 4).astype(jnp.float32)
    for place, ref in sources:
        fill_blocks(blocks_ref, ref, place * TILES, centre)
        fill_right(right_ref, blocks_ref, place * TILES)
    copy.wait()
    counts = split_lists(steps_ref, near_ref, far_ref)
    sum_pairs(
        left_ref, right_ref, blocks_ref, offsets_ref, acc_ref, buffers,
        (near_ref, far_ref), counts, steps_ref[8, 0], False,
    )
    for g in range(TILES):
        sums_ref[g : g + 1, :] = jnp.sum(acc_ref[g].T, axis=0, keepdims=True)
    slot = rows_of((TILES, 128)) * 128 + rows_of((TILES, 128), 1)
    live = slot < fill_ref[0]
    radius = jnp.where(live, radii_ref[...], 1.5)
    inner = radius - OFFSET
    psi = 0.125 * sums_ref[...] * inner
    bending = jnp.tanh(psi - 0.8 * psi * psi + 4.85 * psi * psi * psi)
    born = 1.0 / (1.0 / inner - bending / radius)
    born_ref[...] = jnp.where(live, born, 0.0)
    send_ref[...] = jnp.where(live, born, 1.0)


def energy_list(plan_ref, steps_ref, list_ref, sem):
    copy = pltpu.make_async_copy(plan_ref, steps_ref, sem)
    copy.start()
    copy.wait()
    count = jnp.int32(0)
    for g in range(TILES):
        for k in range(1, 8):
            entry = steps_ref[k, g]
            list_ref[count] = entry
            count = count + jnp.minimum(entry >> 16, 1)
    pad_list(list_ref, count)
    return count


def sum_energy(left_ref, right_ref, blocks_ref, born_ref, column_ref, inverse_ref, acc_ref, buffers, entries, count, first):
    def produce(w, g):
        return squares(left_ref, right_ref, g, w, 48)

    def consume(w, slot, buffer):
        charge = blocks_ref[w, 4:5, :]
        partner = born_ref[pl.ds(w, 1), :]
        backward = 1.0 / partner
        for v in range(8):
            rows = slice(16 * v, 16 * v + 16)
            squared = buffer[rows, :]
            product = column_ref[slot, rows, :] * partner
            decay = jnp.exp2(squared * (inverse_ref[slot, rows, :] * backward))
            term = charge * lax.rsqrt(squared + product * decay)
            if first:
                acc_ref[slot, rows, :] = term
            else:
                acc_ref[slot, rows, :] += term

    run_list(count, entries, buffers, produce, consume)


def energy_own_kernel(
    plan_ref, blocks_ref, left_ref, right_ref, own_ref,
    column_ref, inverse_ref, acc_ref,
    list_ref, steps_ref, born_ref, sem, *buffers,
):
    count = energy_list(plan_ref, steps_ref, list_ref, sem)
    born_ref[2 * TILES : 3 * TILES, :] = own_ref[...]
    for g in range(TILES):
        column = column_of(own_ref[g : g + 1, :])
        column_ref[g] = column
        inverse_ref[g] = (-0.25 * LOG2E) / column
    column_ref[TILES] = column_ref[0]
    inverse_ref[TILES] = inverse_ref[0]
    shared = (left_ref, right_ref, blocks_ref, born_ref, column_ref, inverse_ref, acc_ref)
    sum_energy(*shared, buffers, own_entry, TILES, True)
    sum_energy(*shared, buffers[:4], entry_in(list_ref), count, False)


def energy_rest_kernel(
    slab_ref, plan_ref, blocks_ref, left_ref, right_ref, r0_ref, r1_ref, r2_ref, r3_ref,
    column_ref, inverse_ref, acc_in,
    energy_ref, share_ref, acc_ref,
    list_ref, steps_ref, born_ref, sem, charge_ref, *buffers,
):
    count = energy_list(plan_ref, steps_ref, list_ref, sem)
    for place, ref in zip(slots(slab_ref[0]), (r0_ref, r1_ref, r2_ref, r3_ref)):
        born_ref[pl.ds(place * TILES, TILES), :] = ref[...]
    born_ref[2 * TILES : 3 * TILES, :] = jnp.ones((TILES, 128), jnp.float32)
    sum_energy(
        left_ref, right_ref, blocks_ref, born_ref, column_ref, inverse_ref, acc_ref, buffers,
        entry_in(list_ref), count, False,
    )
    for g in range(TILES):
        energy_ref[g : g + 1, :] = jnp.sum(acc_ref[g].T, axis=0, keepdims=True)
        charge_ref[g : g + 1, :] = blocks_ref[2 * TILES + g, 4:5, :]
    energy = -0.5 * charge_ref[...] * energy_ref[...]
    energy_ref[...] = energy
    share = jnp.sum(jnp.sum(energy, axis=0, keepdims=True), axis=1, keepdims=True)
    share_ref[...] = jnp.broadcast_to(share[None], share_ref.shape)


def total_kernel(shares_ref, total_ref):
    total = shares_ref[0]
    for i in range(1, shares_ref.shape[0]):
        total = total + shares_ref[i]
    total_ref[0] = total[0, 0]


def shards(coords, charges, radii, screens, tile_lists, tile_counts, slab_fill):
    f32 = jnp.float32
    count = lax.axis_size(SLAB)
    smem = pl.BlockSpec(memory_space=pltpu.SMEM)
    vmem = pl.BlockSpec(memory_space=pltpu.VMEM)

    def near(*values):
        return tuple(pltpu.with_memory_space_constraint(value, pltpu.VMEM) for value in values)

    def call(kernel, name, outs, scalars, arrays, scratch, aliases=None, out_specs=None, flops=0):
        return pl.pallas_call(
            kernel,
            out_shape=outs,
            in_specs=[smem] * len(scalars) + [vmem] * len(arrays),
            out_specs=out_specs or (vmem,) * len(outs),
            scratch_shapes=scratch,
            input_output_aliases=aliases or {},
            cost_estimate=pl.CostEstimate(flops=flops, transcendentals=0, bytes_accessed=0),
            compiler_params=pltpu.CompilerParams(vmem_limit_bytes=20 << 20),
            name=name,
        )(*scalars, *arrays)

    stack = pltpu.VMEM((TILES + 1, 128, 128), f32)
    blocks_type = pltpu.VMEM((5 * TILES, 8, 128), f32)
    right_type = pltpu.VMEM((5 * TILES, 64, 128), jnp.bfloat16)
    left_type = pltpu.VMEM((TILES, 128, 64), jnp.bfloat16)
    plan_type = pltpu.VMEM((16, 128), jnp.int32)
    slab_type = pltpu.VMEM((TILES, 128), f32)
    entries = pltpu.SMEM((144,), jnp.int32)
    steps = pltpu.SMEM((16, 128), jnp.int32)
    squares = [pltpu.VMEM((128, 128), f32)] * 8
    sem = pltpu.SemaphoreType.DMA

    slab = lax.axis_index(SLAB).astype(jnp.int32)[None]
    charges, radii, screens = (v.reshape(TILES, 128) for v in (charges, radii, screens))
    lists, counts = tile_lists.T, tile_counts.reshape(1, TILES)
    coords, charges, radii, screens, lists, counts = (
        pltpu.with_memory_space_constraint(value, pltpu.HBM)
        for value in (coords, charges, radii, screens, lists, counts)
    )
    (packed,) = call(
        prep_kernel, "prep", (pltpu.VMEM((ROWS, 128), f32),),
        (slab, slab_fill), (coords, charges, radii, screens), [],
    )
    around = neighbours(packed)
    (packed,) = near(packed)
    blocks, left, right, offsets, acc, own_plan = call(
        born_own_kernel, "born_own",
        (blocks_type, left_type, right_type, stack, stack, plan_type),
        (slab,), (lists, counts, packed, radii),
        [entries, entries, plan_type, steps, sem] + squares, flops=1 << 27,
    )
    plan, born, send, blocks, right, acc = call(
        born_rest_kernel, "born_rest",
        (plan_type, jax.ShapeDtypeStruct((TILES, 128), f32), slab_type, blocks_type, right_type, stack),
        (slab, slab_fill),
        (lists, counts, packed, *near(*around), radii, *near(left, offsets, blocks, right, acc)),
        [entries, entries, plan_type, steps, sem, slab_type] + squares,
        aliases={12: 3, 13: 4, 14: 5},
    )
    far_born = neighbours(send)
    column, inverse, acc = call(
        energy_own_kernel, "energy_own", (stack,) * 3,
        (), near(own_plan, blocks, left, right, send),
        [entries, steps, pltpu.VMEM((5 * TILES, 128), f32), sem] + squares, flops=1 << 27,
    )
    energy, share, acc = call(
        energy_rest_kernel, "energy_rest",
        (jax.ShapeDtypeStruct((TILES, 128), f32), pltpu.VMEM((count, 1, 128), f32), stack),
        (slab,), near(plan, blocks, left, right, *far_born, column, inverse, acc),
        [entries, steps, pltpu.VMEM((5 * TILES, 128), f32), sem, slab_type] + squares,
        aliases={11: 2},
    )
    shares = lax.all_to_all(share, SLAB, 0, 0, tiled=True)
    (total,) = call(
        total_kernel, "total", (jax.ShapeDtypeStruct((1,), f32),), (), near(shares), [], out_specs=(smem,)
    )
    return (born.reshape(-1), energy.reshape(-1), total[0])


def solution(mesh):
    torus = Mesh(mesh.devices.reshape(4, 8, 4, 2), SLAB)
    placed = (P(None, SLAB), P(SLAB), P(SLAB), P(SLAB), P(SLAB, None), P(SLAB), P(SLAB))
    return jax.shard_map(
        shards, mesh=torus, in_specs=placed, out_specs=(P(SLAB), P(SLAB), P()), check_vma=False
    )
```

time: 63.8 us -> 62.7 us (0.983)
  blocking collectives: 23.1 us -> 25.9 us
  local copies, waits for them, and re-layouts: 2.4 us -> 0 us
  Pallas kernels: 14.5 us -> 16.8 us
  starting transfers between devices: 20.5 us -> 18.2 us
  waiting for transfers between devices: 1.7 us -> 0.02 us
    all_to_all x1, blocking collectives: 23.1 us -> 25.9 us  [shards(): shares = lax.all_to_all(share, SLAB, 0, 0, tiled=True)]
    unnamed x4 -> x0, local copies, waits for them, and re-layouts: 2.4 us -> none
    pallas_call x4 -> x6, Pallas kernels: 14.5 us -> 16.8 us  [call(): pl.pallas_call(kernel, out_shape=outs, in_specs=[smem] * len(scalars) + [...]
    ppermute x8, starting transfers between devices: 20.5 us -> 18.2 us  [neighbours(): lax.ppermute(value, SLAB, pairs)]
    ppermute x8, waiting for transfers between devices: 1.7 us -> 0.02 us  [neighbours(): lax.ppermute(value, SLAB, pairs)]
  transfers between devices with their start and end apart: 8 -> 8, of which waited for: 2 -> 0; matrix products, arithmetic and copies ran while one was open for 0% -> 0% of each run, Pallas kernels for 0% -> 11%
where the time goes in v4:
time: 62.7 us; the launch traced here: 62.4 us
  blocking collectives  25.9 us (41%)
  starting transfers between devices  18.2 us (29%)
  Pallas kernels  16.8 us (27%)
  between operations  1.39 us (2%)
    all_to_all x1, blocking collectives, shards(): shares = lax.all_to_all(share, SLAB, 0, 0, tiled=True)  25.9 us
    ppermute x8, starting transfers between devices, neighbours(): lax.ppermute(value, SLAB, pairs)  18.2 us
    pallas_call x6, Pallas kernels, call(): pl.pallas_call(kernel, out_shape=outs, in_specs=[smem] * len(scalars) + [...  16.8 us
  transfers between devices with their start and end apart: 8, of which 0 were waited for; matrix products, arithmetic and copies ran while one was open for 0% of the time, Pallas kernels for 11%

profile of v4, /device:TPU:1, one launch (start us, length us, event | category | flops | bytes accessed | tf_op | source)
XLA Modules:
  0.0 62.4 jit_solution(12332823214903532448)
XLA Ops:
  1.3 0.9 %prep.1.own_ref = f32[88,128]{1,0:T(8,128)S(1)} custom-call(s32[1]{0:T(128)} %bitcast.slab_ref, s32[1]{0:T(128)S(6)} %copy.18.fill_ref, f32[3,2048]{1,0:T(4,128)} %coords_ref.1, f32[16,128]{1,0:T(8,128)} %bitcast.12, f32[16,128]{1,0:T(8,128)} %bitcast.9, f32[16,128]{1,0:T(8,128)} %bitcast.13), custom_call_target="tpu_custom_call" | custom-call | tf_op jit(solution)/shard_map/prep/pallas_call | solution.py:421
  2.2 3.3 %collective-permute-start.3 = (f32[88,128]{1,0:T(8,128)S(1)}, f32[88,128]{1,0:T(8,128)S(1)}, u32[]{:S(2)}, u32[]{:S(2)}) collective-permute-start(f32[88,128]{1,0:T(8,128)S(1)} %prep.1.own_ref), channel_id=1, source_target_pairs={{0,1},{1,0},{2,4},{3,5},{4,2},{5,3},{6,8},{7,9},{8,6},{9,7},{10,12... | collective-permute-start | bytes 135176 | tf_op jit(solution)/shard_map/ppermute | solution.py:36
  5.5 0.2 collective-permute-start.2
  5.7 1.5 %collective-permute-start.1 = (f32[88,128]{1,0:T(8,128)S(1)}, f32[88,128]{1,0:T(8,128)S(1)}, u32[]{:S(2)}, u32[]{:S(2)}) collective-permute-start(f32[88,128]{1,0:T(8,128)S(1)} %prep.1.own_ref), channel_id=1, source_target_pairs={{0,255},{1,2},{2,1},{3,4},{4,3},{5,6},{6,5},{7,8},{8,7},{9,10},{10... | collective-permute-start | bytes 135176 | tf_op jit(solution)/shard_map/ppermute | solution.py:36
  7.2 7.2 %collective-permute-start = (f32[88,128]{1,0:T(8,128)S(1)}, f32[88,128]{1,0:T(8,128)S(1)}, u32[]{:S(2)}, u32[]{:S(2)}) collective-permute-start(f32[88,128]{1,0:T(8,128)S(1)} %prep.1.own_ref), channel_id=1, source_target_pairs={{0,1},{1,0},{2,3},{3,2},{4,5},{5,4},{6,7},{7,6},{8,9},{9,8},{10,11... | collective-permute-start | bytes 135176 | tf_op jit(solution)/shard_map/ppermute | solution.py:36
  14.4 4.6 %born_own.1 = (f32[80,8,128]{2,1,0:T(8,128)S(1)}, bf16[16,128,64]{2,1,0:T(8,128)(2,1)S(1)}, bf16[80,64,128]{2,1,0:T(8,128)(2,1)S(1)}, f32[17,128,128]{2,1,0:T(8,...) custom-call(s32[1]{0:T(128)} %bitcast.slab_ref, s32[8,16]{1,0:T(8,128)} %bitcast.14, s32[1,16]{1,0:T(1,128)} %bitcast.16, ...), custom_call_target="tpu_custom_call" | custom-call | flops 134217728 | tf_op jit(solution)/shard_map/born_own/pallas_call | solution.py:421
  19.0 0.0 collective-permute-done.3.p3_ref
  19.0 0.0 collective-permute-done.2.p2_ref
  19.0 0.0 collective-permute-done.1.p1_ref
  19.0 0.0 collective-permute-done.p0_ref
  19.1 5.1 %born_rest.1 = (s32[16,128]{1,0:T(8,128)S(1)}, f32[16,128]{1,0:T(8,128)}, f32[16,128]{1,0:T(8,128)S(1)}, f32[80,8,128]{2,1,0:T(8,128)S(1)}, bf16[80,64,128]{2,1,...) custom-call(s32[1]{0:T(128)} %bitcast.slab_ref, ...), custom_call_target="tpu_custom_call", output_to_operand_aliasing={{3}: (12, {}), {4}: (13, {}), {5}: (14, {})} | custom-call | tf_op jit(solution)/shard_map/born_rest/pallas_call | solution.py:421
  24.2 1.5 %collective-permute-start.7 = (f32[16,128]{1,0:T(8,128)S(1)}, f32[16,128]{1,0:T(8,128)S(1)}, u32[]{:S(2)}, u32[]{:S(2)}) collective-permute-start(f32[16,128]{1,0:T(8,128)S(1)} %get-tuple-element.28.own_ref), channel_id=1, source_target_pairs={{0,1},{1,0},{2,4},{3,5},{4,2},{5,3},{6,8},{7,9},{8,6},{9,7},{10,12... | collective-permute-start | bytes 24584 | tf_op jit(solution)/shard_map/ppermute | solution.py:36
  25.6 0.0 collective-permute-start.6
  25.6 1.7 %collective-permute-start.5 = (f32[16,128]{1,0:T(8,128)S(1)}, f32[16,128]{1,0:T(8,128)S(1)}, u32[]{:S(2)}, u32[]{:S(2)}) collective-permute-start(f32[16,128]{1,0:T(8,128)S(1)} %get-tuple-element.28.own_ref), channel_id=1, source_target_pairs={{0,255},{1,2},{2,1},{3,4},{4,3},{5,6},{6,5},{7,8},{8,7},{9,10},{10... | collective-permute-start | bytes 24584 | tf_op jit(solution)/shard_map/ppermute | solution.py:36
  27.4 2.8 %collective-permute-start.4 = (f32[16,128]{1,0:T(8,128)S(1)}, f32[16,128]{1,0:T(8,128)S(1)}, u32[]{:S(2)}, u32[]{:S(2)}) collective-permute-start(f32[16,128]{1,0:T(8,128)S(1)} %get-tuple-element.28.own_ref), channel_id=1, source_target_pairs={{0,1},{1,0},{2,3},{3,2},{4,5},{5,4},{6,7},{7,6},{8,9},{9,8},{10,11... | collective-permute-start | bytes 24584 | tf_op jit(solution)/shard_map/ppermute | solution.py:36
  30.2 2.2 %energy_own.1 = (f32[17,128,128]{2,1,0:T(8,128)S(1)}, f32[17,128,128]{2,1,0:T(8,128)S(1)}, f32[17,128,128]{2,1,0:T(8,128)S(1)}) custom-call(s32[16,128]{1,0:T(8,128)S(1)} %get-tuple-element.29.plan_ref, f32[80,8,128]{2,1,0:T(8,128)S(1)} %get-tuple-element.26.blocks_ref, bf16[16,128,64]{2,1,0:T(8,128)(2,1)S(1)} %get-tuple-element.19.left_ref, ...), custom_call_target="tpu_custom_call" | custom-call | flops 134217728 | tf_op jit(solution)/shard_map/energy_own/pallas_call | solution.py:421
  32.4 0.0 collective-permute-done.7.r3_ref
  32.4 0.0 collective-permute-done.6.r2_ref
  32.4 0.0 collective-permute-done.5.r1_ref
  32.5 0.0 collective-permute-done.4.r0_ref
  32.5 3.2 %energy_rest.1 = (f32[16,128]{1,0:T(8,128)}, f32[256,1,128]{2,1,0:T(1,128)S(1)}, f32[17,128,128]{2,1,0:T(8,128)S(1)}) custom-call(s32[1]{0:T(128)} %bitcast.slab_ref, s32[16,128]{1,0:T(8,128)S(1)} %get-tuple-element.25.plan_ref, f32[80,8,128]{2,1,0:T(8,128)S(1)} %get-tuple-element.26.blocks_ref, ...), custom_call_target="tpu_custom_call", output_to_operand_aliasing={{2}: (11, {})} | custom-call | tf_op jit(solution)/shard_map/energy_rest/pallas_call | solution.py:421
  35.7 25.9 %all_to_all.5.shares_ref = f32[256,1,128]{2,1,0:T(1,128)S(1)} all-to-all(f32[256,1,128]{2,1,0:T(1,128)S(1)} %get-tuple-element.34), channel_id=1, replica_groups=mesh['slab_0'=4,'slab_1'=8,'slab_2'=4,'slab_3'=2] {'slab_0','slab_1','sl..., dimensions={0} | all-to-all | bytes 262144 | tf_op jit(solution)/shard_map/all_to_all | solution.py:484
  61.6 0.8 %total.1 = f32[1]{0:T(128)} custom-call(f32[256,1,128]{2,1,0:T(1,128)S(1)} %all_to_all.5.shares_ref), custom_call_target="tpu_custom_call" | custom-call | tf_op jit(solution)/shard_map/total/pallas_call | solution.py:421
Async XLA Ops:
  2.2 16.8 %collective-permute-start.3 = (f32[88,128]{1,0:T(8,128)S(1)}, f32[88,128]{1,0:T(8,128)S(1)}, u32[]{:S(2)}, u32[]{:S(2)}) collective-permute-start(f32[88,128]{1,0:T(8,128)S(1)} %prep.1.own_ref), channel_id=1, source_target_pairs={{0,1},{1,0},{2,4},{3,5},{4,2},{5,3},{6,8},{7,9},{8,6},{9,7},{10,12... | collective-permute-start | bytes 135176 | tf_op jit(solution)/shard_map/ppermute | solution.py:36
  5.5 13.6 %collective-permute-start.2 = (f32[88,128]{1,0:T(8,128)S(1)}, f32[88,128]{1,0:T(8,128)S(1)}, u32[]{:S(2)}, u32[]{:S(2)}) collective-permute-start(f32[88,128]{1,0:T(8,128)S(1)} %prep.1.own_ref), channel_id=1, source_target_pairs={{0,2},{1,3},{2,0},{3,1},{4,6},{5,7},{6,4},{7,5},{8,10},{9,11},{10,... | collective-permute-start | bytes 135176 | tf_op jit(solution)/shard_map/ppermute | solution.py:36
  5.7 13.4 %collective-permute-start.1 = (f32[88,128]{1,0:T(8,128)S(1)}, f32[88,128]{1,0:T(8,128)S(1)}, u32[]{:S(2)}, u32[]{:S(2)}) collective-permute-start(f32[88,128]{1,0:T(8,128)S(1)} %prep.1.own_ref), channel_id=1, source_target_pairs={{0,255},{1,2},{2,1},{3,4},{4,3},{5,6},{6,5},{7,8},{8,7},{9,10},{10... | collective-permute-start | bytes 135176 | tf_op jit(solution)/shard_map/ppermute | solution.py:36
  7.2 11.9 %collective-permute-start = (f32[88,128]{1,0:T(8,128)S(1)}, f32[88,128]{1,0:T(8,128)S(1)}, u32[]{:S(2)}, u32[]{:S(2)}) collective-permute-start(f32[88,128]{1,0:T(8,128)S(1)} %prep.1.own_ref), channel_id=1, source_target_pairs={{0,1},{1,0},{2,3},{3,2},{4,5},{5,4},{6,7},{7,6},{8,9},{9,8},{10,11... | collective-permute-start | bytes 135176 | tf_op jit(solution)/shard_map/ppermute | solution.py:36
  24.2 8.3 %collective-permute-start.7 = (f32[16,128]{1,0:T(8,128)S(1)}, f32[16,128]{1,0:T(8,128)S(1)}, u32[]{:S(2)}, u32[]{:S(2)}) collective-permute-start(f32[16,128]{1,0:T(8,128)S(1)} %get-tuple-element.28.own_ref), channel_id=1, source_target_pairs={{0,1},{1,0},{2,4},{3,5},{4,2},{5,3},{6,8},{7,9},{8,6},{9,7},{10,12... | collective-permute-start | bytes 24584 | tf_op jit(solution)/shard_map/ppermute | solution.py:36
  25.6 6.8 %collective-permute-start.6 = (f32[16,128]{1,0:T(8,128)S(1)}, f32[16,128]{1,0:T(8,128)S(1)}, u32[]{:S(2)}, u32[]{:S(2)}) collective-permute-start(f32[16,128]{1,0:T(8,128)S(1)} %get-tuple-element.28.own_ref), channel_id=1, source_target_pairs={{0,2},{1,3},{2,0},{3,1},{4,6},{5,7},{6,4},{7,5},{8,10},{9,11},{10,... | collective-permute-start | bytes 24584 | tf_op jit(solution)/shard_map/ppermute | solution.py:36
  25.6 6.8 %collective-permute-start.5 = (f32[16,128]{1,0:T(8,128)S(1)}, f32[16,128]{1,0:T(8,128)S(1)}, u32[]{:S(2)}, u32[]{:S(2)}) collective-permute-start(f32[16,128]{1,0:T(8,128)S(1)} %get-tuple-element.28.own_ref), channel_id=1, source_target_pairs={{0,255},{1,2},{2,1},{3,4},{4,3},{5,6},{6,5},{7,8},{8,7},{9,10},{10... | collective-permute-start | bytes 24584 | tf_op jit(solution)/shard_map/ppermute | solution.py:36
  27.4 5.1 %collective-permute-start.4 = (f32[16,128]{1,0:T(8,128)S(1)}, f32[16,128]{1,0:T(8,128)S(1)}, u32[]{:S(2)}, u32[]{:S(2)}) collective-permute-start(f32[16,128]{1,0:T(8,128)S(1)} %get-tuple-element.28.own_ref), channel_id=1, source_target_pairs={{0,1},{1,0},{2,3},{3,2},{4,5},{5,4},{6,7},{7,6},{8,9},{9,8},{10,11... | collective-permute-start | bytes 24584 | tf_op jit(solution)/shard_map/ppermute | solution.py:36

commit v5 on v4

--- a/solution.py
+++ b/solution.py
@@ -15,31 +15,43 @@
 ROWS = 88
 
 
-def swaps(count):
-    def chip_swap(odd):
-        pairs = []
-        for chip in range(count // 2):
-            other = ((chip + odd) ^ 1) - odd
-            for core in (0, 1):
-                if 0 <= other < count // 2:
-                    pairs.append((2 * chip + core, 2 * other + core))
-                else:
-                    pairs.append((2 * chip + core, 2 * chip + 1 - core))
-        return pairs
-
-    inner = [(i, i ^ 1) for i in range(count)]
-    outer = [(i, (((i + 1) ^ 1) - 1) % count) for i in range(count)]
-    return inner, outer, chip_swap(0), chip_swap(1)
+def chip_swap(count, odd):
+    pairs = []
+    for chip in range(count // 2):
+        other = ((chip + odd) ^ 1) - odd
+        for core in (0, 1):
+            if 0 <= other < count // 2:
+                pairs.append((2 * chip + core, 2 * other + core))
+            else:
+                pairs.append((2 * chip + core, 2 * chip + 1 - core))
+    return pairs
 
 
 def neighbours(value):
-    return [lax.ppermute(value, SLAB, pairs) for pairs in swaps(lax.axis_size(SLAB))]
-
-
-def slots(slab):
-    inner = jnp.where(slab % 2 == 0, 3, 1)
-    chip = jnp.where((slab // 2) % 2 == 0, 4, 0)
-    return inner, 4 - inner, chip, 4 - chip
+    count = lax.axis_size(SLAB)
+    other = lax.ppermute(value, SLAB, [(i, i ^ 1) for i in range(count)])
+    both = jnp.concatenate([value, other], axis=0)
+    return [other] + [lax.ppermute(both, SLAB, chip_swap(count, odd)) for odd in (0, 1)]
+
+
+def rows_in(ref):
+    return lambda start, size: ref[pl.ds(start, size), :]
+
+
+def inner_slot(slab):
+    return jnp.where(slab % 2 == 0, 3, 1)
+
+
+def outer_slabs(slab, even, odd, height):
+    ahead = (slab // 2) % 2 == 0
+    far = jnp.where(ahead, 4, 0)
+    from_even = ahead == (slab % 2 == 1)
+
+    def crossed(start, size):
+        rows = pl.ds(height + start, size)
+        return jnp.where(from_even, even[rows, :], odd[rows, :])
+
+    return ((4 - inner_slot(slab), crossed), (far, rows_in(even)), (4 - far, rows_in(odd)))
 
 
 def rows_of(shape, axis=0):
@@ -80,12 +92,12 @@
     return first, second, third
 
 
-def fill_blocks(blocks_ref, packed_ref, base, centre):
+def fill_blocks(blocks_ref, read, base, centre):
     row = rows_of((8, 128))
     shift = jnp.where(row == 2, centre, 0.0)
     tail = jnp.where(row == 6, 1.0, 0.0)
     for t in range(TILES):
-        block = packed_ref[5 * t : 5 * t + 8, :] - shift
+        block = read(5 * t, 8) - shift
         square = block * block
         norm = square[0:1] + square[1:2] + square[2:3]
         blocks_ref[base + t] = jnp.where(row < 5, block, jnp.where(row == 5, norm, tail))
@@ -169,10 +181,11 @@
     index_ref[8:9, 0:TILES] = counts_ref[...]
     tile = index_ref[0:8, :]
     here = jnp.zeros((8, 128), jnp.int32)
-    for place, ref in sources:
-        low = jnp.where(lane >> 4 == place, ref[80:81, :], low)
-        high = jnp.where(lane >> 4 == place, ref[81:82, :], high)
-        top = jnp.maximum(top, ref[82:83, :])
+    for place, read in sources:
+        ranges = read(80, 8)
+        low = jnp.where(lane >> 4 == place, ranges[0:1], low)
+        high = jnp.where(lane >> 4 == place, ranges[1:2], high)
+        top = jnp.maximum(top, ranges[2:3])
         here = jnp.where(tile >> 4 == place, 1, here)
     used = (rows_of((8, 128)) > 0) & (rows_of((8, 128)) < index_ref[8:9, :]) & (here > 0)
 
@@ -258,7 +271,7 @@
 
     pl.when(within == 0)(lambda: near_lists(False))
     pl.when(within != 0)(lambda: near_lists(True))
-    run_list(counts[1], entry_in(lists[1]), buffers[:4] if own else buffers, produce, consume_far)
+    run_list(counts[1], entry_in(lists[1]), buffers, produce, consume_far)
 
 
 def least_of(offset):
@@ -266,17 +279,19 @@
 
 
 def born_own_kernel(
-    slab_ref, lists_ref, counts_ref, own_ref, radii_ref,
+    slab_ref, lists_ref, counts_ref, own_ref, other_ref, radii_ref,
     blocks_ref, left_ref, right_ref, offsets_ref, acc_ref, plan_ref,
     near_ref, far_ref, index_ref, steps_ref, sem, *buffers,
 ):
     offset = radii_ref[...] - OFFSET
-    plan_of(lists_ref, counts_ref, least_of(offset), ((2, own_ref),), index_ref, plan_ref, own_ref)
+    sources = ((2, rows_in(own_ref)), (inner_slot(slab_ref[0]), rows_in(other_ref)))
+    plan_of(lists_ref, counts_ref, least_of(offset), sources, index_ref, plan_ref, own_ref)
     copy = pltpu.make_async_copy(plan_ref, steps_ref, sem)
     copy.start()
     centre = (8 * slab_ref[0] + 4).astype(jnp.float32)
-    fill_blocks(blocks_ref, own_ref, 2 * TILES, centre)
-    fill_right(right_ref, blocks_ref, 2 * TILES)
+    for place, read in sources:
+        fill_blocks(blocks_ref, read, place * TILES, centre)
+        fill_right(right_ref, blocks_ref, place * TILES)
     fill_left(left_ref, blocks_ref)
     for g in range(TILES):
         offsets_ref[g] = column_of(offset[g : g + 1])
@@ -290,20 +305,20 @@
 
 
 def born_rest_kernel(
-    slab_ref, fill_ref, lists_ref, counts_ref, own_ref, p0_ref, p1_ref, p2_ref, p3_ref, radii_ref,
+    slab_ref, fill_ref, lists_ref, counts_ref, own_ref, even_ref, odd_ref, radii_ref,
     left_ref, offsets_ref, blocks_in, right_in, acc_in,
     plan_ref, born_ref, send_ref, blocks_ref, right_ref, acc_ref,
     near_ref, far_ref, index_ref, steps_ref, sem, sums_ref, *buffers,
 ):
     slab = slab_ref[0]
-    sources = tuple(zip(slots(slab), (p0_ref, p1_ref, p2_ref, p3_ref)))
+    sources = outer_slabs(slab, even_ref, odd_ref, ROWS)
     offset = radii_ref[...] - OFFSET
     plan_of(lists_ref, counts_ref, least_of(offset), sources, index_ref, plan_ref, own_ref)
     copy = pltpu.make_async_copy(plan_ref, steps_ref, sem)
     copy.start()
     centre = (8 * slab + 4).astype(jnp.float32)
-    for place, ref in sources:
-        fill_blocks(blocks_ref, ref, place * TILES, centre)
+    for place, read in sources:
+        fill_blocks(blocks_ref, read, place * TILES, centre)
         fill_right(right_ref, blocks_ref, place * TILES)
     copy.wait()
     counts = split_lists(steps_ref, near_ref, far_ref)
@@ -361,12 +376,13 @@
 
 
 def energy_own_kernel(
-    plan_ref, blocks_ref, left_ref, right_ref, own_ref,
+    slab_ref, plan_ref, blocks_ref, left_ref, right_ref, own_ref, other_ref,
     column_ref, inverse_ref, acc_ref,
     list_ref, steps_ref, born_ref, sem, *buffers,
 ):
     count = energy_list(plan_ref, steps_ref, list_ref, sem)
     born_ref[2 * TILES : 3 * TILES, :] = own_ref[...]
+    born_ref[pl.ds(inner_slot(slab_ref[0]) * TILES, TILES), :] = other_ref[...]
     for g in range(TILES):
         column = column_of(own_ref[g : g + 1, :])
         column_ref[g] = column
@@ -375,18 +391,18 @@
     inverse_ref[TILES] = inverse_ref[0]
     shared = (left_ref, right_ref, blocks_ref, born_ref, column_ref, inverse_ref, acc_ref)
     sum_energy(*shared, buffers, own_entry, TILES, True)
-    sum_energy(*shared, buffers[:4], entry_in(list_ref), count, False)
+    sum_energy(*shared, buffers, entry_in(list_ref), count, False)
 
 
 def energy_rest_kernel(
-    slab_ref, plan_ref, blocks_ref, left_ref, right_ref, r0_ref, r1_ref, r2_ref, r3_ref,
+    slab_ref, plan_ref, blocks_ref, left_ref, right_ref, even_ref, odd_ref,
     column_ref, inverse_ref, acc_in,
     energy_ref, share_ref, acc_ref,
     list_ref, steps_ref, born_ref, sem, charge_ref, *buffers,
 ):
     count = energy_list(plan_ref, steps_ref, list_ref, sem)
-    for place, ref in zip(slots(slab_ref[0]), (r0_ref, r1_ref, r2_ref, r3_ref)):
-        born_ref[pl.ds(place * TILES, TILES), :] = ref[...]
+    for place, read in outer_slabs(slab_ref[0], even_ref, odd_ref, TILES):
+        born_ref[pl.ds(place * TILES, TILES), :] = read(0, TILES)
     born_ref[2 * TILES : 3 * TILES, :] = jnp.ones((TILES, 128), jnp.float32)
     sum_energy(
         left_ref, right_ref, blocks_ref, born_ref, column_ref, inverse_ref, acc_ref, buffers,
@@ -452,34 +468,34 @@
         prep_kernel, "prep", (pltpu.VMEM((ROWS, 128), f32),),
         (slab, slab_fill), (coords, charges, radii, screens), [],
     )
-    around = neighbours(packed)
-    (packed,) = near(packed)
+    other, even, odd = neighbours(packed)
+    packed, other, even, odd = near(packed, other, even, odd)
     blocks, left, right, offsets, acc, own_plan = call(
         born_own_kernel, "born_own",
         (blocks_type, left_type, right_type, stack, stack, plan_type),
-        (slab,), (lists, counts, packed, radii),
+        (slab,), (lists, counts, packed, other, radii),
         [entries, entries, plan_type, steps, sem] + squares, flops=1 << 27,
     )
     plan, born, send, blocks, right, acc = call(
         born_rest_kernel, "born_rest",
         (plan_type, jax.ShapeDtypeStruct((TILES, 128), f32), slab_type, blocks_type, right_type, stack),
         (slab, slab_fill),
-        (lists, counts, packed, *near(*around), radii, *near(left, offsets, blocks, right, acc)),
+        (lists, counts, packed, even, odd, radii, *near(left, offsets, blocks, right, acc)),
         [entries, entries, plan_type, steps, sem, slab_type] + squares,
-        aliases={12: 3, 13: 4, 14: 5},
-    )
-    far_born = neighbours(send)
+        aliases={10: 3, 11: 4, 12: 5},
+    )
+    born_other, born_even, born_odd = neighbours(send)
     column, inverse, acc = call(
         energy_own_kernel, "energy_own", (stack,) * 3,
-        (), near(own_plan, blocks, left, right, send),
+        (slab,), near(own_plan, blocks, left, right, send, born_other),
         [entries, steps, pltpu.VMEM((5 * TILES, 128), f32), sem] + squares, flops=1 << 27,
     )
     energy, share, acc = call(
         energy_rest_kernel, "energy_rest",
         (jax.ShapeDtypeStruct((TILES, 128), f32), pltpu.VMEM((count, 1, 128), f32), stack),
-        (slab,), near(plan, blocks, left, right, *far_born, column, inverse, acc),
+        (slab,), near(plan, blocks, left, right, born_even, born_odd, column, inverse, acc),
         [entries, steps, pltpu.VMEM((5 * TILES, 128), f32), sem, slab_type] + squares,
-        aliases={11: 2},
+        aliases={9: 2},
     )
     shares = lax.all_to_all(share, SLAB, 0, 0, tiled=True)
     (total,) = call(

time: 62.7 us -> 57.9 us (0.923)
  starting transfers between devices: 18.2 us -> 6.87 us
  Pallas kernels: 16.8 us -> 19.2 us
  waiting for transfers between devices: 0.02 us -> 2.03 us
  blocking collectives: 25.9 us -> 27.9 us
    ppermute x8 -> x6, starting transfers between devices: 18.2 us -> 6.87 us  [the longest x4 3.49 us: neighbours(): lax.ppermute(both, SLAB, chip_swap(count, odd))]
    pallas_call x6, Pallas kernels: 16.8 us -> 19.2 us  [call(): pl.pallas_call(kernel, out_shape=outs, in_specs=[smem] * len(scalars) + [...]
    ppermute x8 -> x6, waiting for transfers between devices: 0.02 us -> 2.03 us  [the longest x2 2.02 us: neighbours(): other = lax.ppermute(value, SLAB, [(i, i ^ 1) for i in range(count)])]
    all_to_all x1, blocking collectives: 25.9 us -> 27.9 us  [shards(): shares = lax.all_to_all(share, SLAB, 0, 0, tiled=True)]
  transfers between devices with their start and end apart: 8 -> 6, of which waited for: 0 -> 2; matrix products, arithmetic and copies ran while one was open for 0% -> 0% of each run, Pallas kernels for 11% -> 16%
where the time goes in v5:
time: 57.9 us; the launch traced here: 57.3 us
  blocking collectives  27.9 us (48%)
  Pallas kernels  19.2 us (33%)
  starting transfers between devices  6.87 us (12%)
  waiting for transfers between devices  2.03 us (4%)
  between operations  1.38 us (2%)
    all_to_all x1, blocking collectives, shards(): shares = lax.all_to_all(share, SLAB, 0, 0, tiled=True)  27.9 us
    pallas_call x6, Pallas kernels, call(): pl.pallas_call(kernel, out_shape=outs, in_specs=[smem] * len(scalars) + [...  19.2 us
    ppermute x4, starting transfers between devices, neighbours(): lax.ppermute(both, SLAB, chip_swap(count, odd))  3.49 us
    ppermute x2, starting transfers between devices, neighbours(): other = lax.ppermute(value, SLAB, [(i, i ^ 1) for i in range(count)])  3.38 us
    ppermute x2, waiting for transfers between devices, neighbours(): other = lax.ppermute(value, SLAB, [(i, i ^ 1) for i in range(count)])  2.02 us
  transfers between devices with their start and end apart: 6, of which 2 were waited for; matrix products, arithmetic and copies ran while one was open for 0% of the time, Pallas kernels for 16%

profile of v5, /device:TPU:1, one launch (start us, length us, event | category | flops | bytes accessed | tf_op | source)
XLA Modules:
  0.0 57.3 jit_solution(472063573587788911)
XLA Ops:
  1.3 0.9 %prep.1.own_ref = f32[88,128]{1,0:T(8,128)S(1)} custom-call(s32[1]{0:T(128)} %bitcast.slab_ref, s32[1]{0:T(128)S(6)} %copy.19.fill_ref, f32[3,2048]{1,0:T(4,128)} %coords_ref.1, f32[16,128]{1,0:T(8,128)} %bitcast.12, f32[16,128]{1,0:T(8,128)} %bitcast.9, f32[16,128]{1,0:T(8,128)} %bitcast.13), custom_call_target="tpu_custom_call" | custom-call | tf_op jit(solution)/shard_map/prep/pallas_call | solution.py:437
  2.2 3.3 %collective-permute-start = (f32[88,128]{1,0:T(8,128)S(1)}, f32[88,128]{1,0:T(8,128)S(1)}, u32[]{:S(2)}, u32[]{:S(2)}) collective-permute-start(f32[88,128]{1,0:T(8,128)S(1)} %prep.1.own_ref), channel_id=1, source_target_pairs={{0,1},{1,0},{2,3},{3,2},{4,5},{5,4},{6,7},{7,6},{8,9},{9,8},{10,11... | collective-permute-start | bytes 135176 | tf_op jit(solution)/shard_map/ppermute | solution.py:32
  5.5 0.9 %collective-permute-done.other_ref = f32[88,128]{1,0:T(8,128)S(1)} collective-permute-done((f32[88,128]{1,0:T(8,128)S(1)}, f32[88,128]{1,0:T(8,128)S(1)}, u32[]{:S(2)}, u32[]{:S(2)}) %collective-permute-start) | collective-permute-done | bytes 45088 | tf_op jit(solution)/shard_map/ppermute | solution.py:32
  6.3 0.4 collective-permute-start.2
  6.8 0.5 collective-permute-start.1
  7.2 5.9 %born_own.1 = (f32[80,8,128]{2,1,0:T(8,128)S(1)}, bf16[16,128,64]{2,1,0:T(8,128)(2,1)S(1)}, bf16[80,64,128]{2,1,0:T(8,128)(2,1)S(1)}, f32[17,128,128]{2,1,0:T(8,...) custom-call(s32[1]{0:T(128)} %bitcast.slab_ref, s32[8,16]{1,0:T(8,128)} %bitcast.14, s32[1,16]{1,0:T(1,128)} %bitcast.16, ...), custom_call_target="tpu_custom_call" | custom-call | flops 134217728 | tf_op jit(solution)/shard_map/born_own/pallas_call | solution.py:437
  13.2 0.0 collective-permute-done.2.odd_ref
  13.2 0.0 collective-permute-done.1.even_ref
  13.2 5.1 %born_rest.1 = (s32[16,128]{1,0:T(8,128)S(1)}, f32[16,128]{1,0:T(8,128)}, f32[16,128]{1,0:T(8,128)S(1)}, f32[80,8,128]{2,1,0:T(8,128)S(1)}, bf16[80,64,128]{2,1,...) custom-call(s32[1]{0:T(128)} %bitcast.slab_ref, ...), custom_call_target="tpu_custom_call", output_to_operand_aliasing={{3}: (10, {}), {4}: (11, {}), {5}: (12, {})} | custom-call | tf_op jit(solution)/shard_map/born_rest/pallas_call | solution.py:437
  18.3 0.1 collective-permute-start.3
  18.4 1.1 %collective-permute-done.3.other_ref = f32[16,128]{1,0:T(8,128)S(1)} collective-permute-done((f32[16,128]{1,0:T(8,128)S(1)}, f32[16,128]{1,0:T(8,128)S(1)}, u32[]{:S(2)}, u32[]{:S(2)}) %collective-permute-start.3) | collective-permute-done | bytes 8224 | tf_op jit(solution)/shard_map/ppermute | solution.py:32
  19.5 0.2 collective-permute-start.5
  19.7 2.4 %collective-permute-start.4 = (f32[32,128]{1,0:T(8,128)S(1)}, f32[32,128]{1,0:T(8,128)S(1)}, u32[]{:S(2)}, u32[]{:S(2)}) collective-permute-start(f32[32,128]{1,0:T(8,128)S(1)} %constant_dynamic-update-slice_fusion), channel_id=1, source_target_pairs={{0,2},{1,3},{2,0},{3,1},{4,6},{5,7},{6,4},{7,5},{8,10},{9,11},{10,... | collective-permute-start | bytes 49160 | tf_op jit(solution)/shard_map/ppermute | solution.py:34
  22.1 3.2 %energy_own.1 = (f32[17,128,128]{2,1,0:T(8,128)S(1)}, f32[17,128,128]{2,1,0:T(8,128)S(1)}, f32[17,128,128]{2,1,0:T(8,128)S(1)}) custom-call(s32[1]{0:T(128)} %bitcast.slab_ref, s32[16,128]{1,0:T(8,128)S(1)} %get-tuple-element.29.plan_ref, f32[80,8,128]{2,1,0:T(8,128)S(1)} %get-tuple-element.26.blocks_ref, ...), custom_call_target="tpu_custom_call" | custom-call | flops 134217728 | tf_op jit(solution)/shard_map/energy_own/pallas_call | solution.py:437
  25.4 0.0 collective-permute-done.5.odd_ref
  25.4 0.0 collective-permute-done.4.even_ref
  25.4 3.2 %energy_rest.1 = (f32[16,128]{1,0:T(8,128)}, f32[256,1,128]{2,1,0:T(1,128)S(1)}, f32[17,128,128]{2,1,0:T(8,128)S(1)}) custom-call(s32[1]{0:T(128)} %bitcast.slab_ref, s32[16,128]{1,0:T(8,128)S(1)} %get-tuple-element.25.plan_ref, f32[80,8,128]{2,1,0:T(8,128)S(1)} %get-tuple-element.26.blocks_ref, ...), custom_call_target="tpu_custom_call", output_to_operand_aliasing={{2}: (9, {})} | custom-call | tf_op jit(solution)/shard_map/energy_rest/pallas_call | solution.py:437
  28.6 27.9 %all_to_all.5.shares_ref = f32[256,1,128]{2,1,0:T(1,128)S(1)} all-to-all(f32[256,1,128]{2,1,0:T(1,128)S(1)} %get-tuple-element.34), channel_id=1, replica_groups=mesh['slab_0'=4,'slab_1'=8,'slab_2'=4,'slab_3'=2] {'slab_0','slab_1','sl..., dimensions={0} | all-to-all | bytes 262144 | tf_op jit(solution)/shard_map/all_to_all | solution.py:500
  56.5 0.8 %total.1 = f32[1]{0:T(128)} custom-call(f32[256,1,128]{2,1,0:T(1,128)S(1)} %all_to_all.5.shares_ref), custom_call_target="tpu_custom_call" | custom-call | tf_op jit(solution)/shard_map/total/pallas_call | solution.py:437
  (3 shorter events, 0.0 us)
Async XLA Ops:
  2.2 4.2 %collective-permute-start = (f32[88,128]{1,0:T(8,128)S(1)}, f32[88,128]{1,0:T(8,128)S(1)}, u32[]{:S(2)}, u32[]{:S(2)}) collective-permute-start(f32[88,128]{1,0:T(8,128)S(1)} %prep.1.own_ref), channel_id=1, source_target_pairs={{0,1},{1,0},{2,3},{3,2},{4,5},{5,4},{6,7},{7,6},{8,9},{9,8},{10,11... | collective-permute-start | bytes 135176 | tf_op jit(solution)/shard_map/ppermute | solution.py:32
  6.3 6.8 %collective-permute-start.2 = (f32[176,128]{1,0:T(8,128)S(1)}, f32[176,128]{1,0:T(8,128)S(1)}, u32[]{:S(2)}, u32[]{:S(2)}) collective-permute-start(f32[176,128]{1,0:T(8,128)S(1)} %pad_maximum_fusion), channel_id=1, source_target_pairs={{0,1},{1,0},{2,4},{3,5},{4,2},{5,3},{6,8},{7,9},{8,6},{9,7},{10,12... | collective-permute-start | bytes 270344 | tf_op jit(solution)/shard_map/ppermute | solution.py:34
  6.8 6.4 %collective-permute-start.1 = (f32[176,128]{1,0:T(8,128)S(1)}, f32[176,128]{1,0:T(8,128)S(1)}, u32[]{:S(2)}, u32[]{:S(2)}) collective-permute-start(f32[176,128]{1,0:T(8,128)S(1)} %pad_maximum_fusion), channel_id=1, source_target_pairs={{0,2},{1,3},{2,0},{3,1},{4,6},{5,7},{6,4},{7,5},{8,10},{9,11},{10,... | collective-permute-start | bytes 270344 | tf_op jit(solution)/shard_map/ppermute | solution.py:34
  18.3 1.3 %collective-permute-start.3 = (f32[16,128]{1,0:T(8,128)S(1)}, f32[16,128]{1,0:T(8,128)S(1)}, u32[]{:S(2)}, u32[]{:S(2)}) collective-permute-start(f32[16,128]{1,0:T(8,128)S(1)} %get-tuple-element.28.own_ref), channel_id=1, source_target_pairs={{0,1},{1,0},{2,3},{3,2},{4,5},{5,4},{6,7},{7,6},{8,9},{9,8},{10,11... | collective-permute-start | bytes 24584 | tf_op jit(solution)/shard_map/ppermute | solution.py:32
  19.5 5.8 %collective-permute-start.5 = (f32[32,128]{1,0:T(8,128)S(1)}, f32[32,128]{1,0:T(8,128)S(1)}, u32[]{:S(2)}, u32[]{:S(2)}) collective-permute-start(f32[32,128]{1,0:T(8,128)S(1)} %constant_dynamic-update-slice_fusion), channel_id=1, source_target_pairs={{0,1},{1,0},{2,4},{3,5},{4,2},{5,3},{6,8},{7,9},{8,6},{9,7},{10,12... | collective-permute-start | bytes 49160 | tf_op jit(solution)/shard_map/ppermute | solution.py:34
  19.7 5.7 %collective-permute-start.4 = (f32[32,128]{1,0:T(8,128)S(1)}, f32[32,128]{1,0:T(8,128)S(1)}, u32[]{:S(2)}, u32[]{:S(2)}) collective-permute-start(f32[32,128]{1,0:T(8,128)S(1)} %constant_dynamic-update-slice_fusion), channel_id=1, source_target_pairs={{0,2},{1,3},{2,0},{3,1},{4,6},{5,7},{6,4},{7,5},{8,10},{9,11},{10,... | collective-permute-start | bytes 49160 | tf_op jit(solution)/shard_map/ppermute | solution.py:34

commit v6 on v5

--- a/solution.py
+++ b/solution.py
@@ -58,7 +58,16 @@
     return lax.broadcasted_iota(jnp.int32, shape, axis)
 
 
-def prep_kernel(slab_ref, fill_ref, coords_ref, charges_ref, radii_ref, screens_ref, out_ref):
+def prep_kernel(
+    slab_ref, fill_ref, coords_ref, charges_ref, radii_ref, screens_ref, lists_ref, counts_ref,
+    out_ref, index_ref, kept_ref,
+):
+    index_ref[...] = jnp.zeros((8, 128), jnp.int32)
+    for k in range(8):
+        lanes = slice(TILES * k, TILES * k + TILES)
+        index_ref[0:1, lanes] = lists_ref[k : k + 1, :]
+        index_ref[1:2, lanes] = counts_ref[...]
+    kept_ref[...] = radii_ref[...]
     fill = fill_ref[0]
     middle = (8 * slab_ref[0] + 4).astype(jnp.float32)
     slot = rows_of((TILES, 128)) * 128 + rows_of((TILES, 128), 1)
@@ -171,33 +180,36 @@
     return entry_of
 
 
-def plan_of(lists_ref, counts_ref, least, sources, index_ref, plan_ref, own_ref):
+def plan_of(index_ref, least, sources, own_ref, plan_ref):
     lane = rows_of((1, 128), 1)
     low = jnp.zeros((1, 128), jnp.float32)
     high = jnp.zeros((1, 128), jnp.float32)
     top = jnp.zeros((1, 128), jnp.float32)
-    index_ref[...] = jnp.zeros((16, 128), jnp.int32)
-    index_ref[0:8, 0:TILES] = lists_ref[...]
-    index_ref[8:9, 0:TILES] = counts_ref[...]
-    tile = index_ref[0:8, :]
-    here = jnp.zeros((8, 128), jnp.int32)
+    tile = index_ref[0:1, :]
+    here = jnp.zeros((1, 128), jnp.int32)
     for place, read in sources:
         ranges = read(80, 8)
         low = jnp.where(lane >> 4 == place, ranges[0:1], low)
         high = jnp.where(lane >> 4 == place, ranges[1:2], high)
         top = jnp.maximum(top, ranges[2:3])
         here = jnp.where(tile >> 4 == place, 1, here)
-    used = (rows_of((8, 128)) > 0) & (rows_of((8, 128)) < index_ref[8:9, :]) & (here > 0)
+    used = (lane >> 4 > 0) & (lane >> 4 < index_ref[1:2, :]) & (here > 0)
 
     def picked(row):
-        return jnp.take_along_axis(
-            jnp.broadcast_to(row, (8, 128)), tile, axis=1, mode="promise_in_bounds"
+        wide = jnp.take_along_axis(
+            jnp.broadcast_to(row, (8, 128)),
+            jnp.broadcast_to(tile, (8, 128)),
+            axis=1,
+            mode="promise_in_bounds",
         )
+        return wide[0:1]
 
     gap = jnp.maximum(picked(low) - own_ref[81:82, :], own_ref[80:81, :] - picked(high))
     kind = jnp.where(used, jnp.where(gap >= FAR_GAP, 1 << 17, 1 << 16), 0)
-    plan_ref[0:8, :] = tile * 32 + (lane & 15) + kind
-    plan_ref[8:16, :] = jnp.broadcast_to(jnp.where(top - 0.99 >= least, 1, 0), (8, 128))
+    within = jnp.where(top - 0.99 >= least, 1, 0)
+    row = rows_of((8, 128))
+    plan = jnp.broadcast_to(tile * 32 + (lane & 15) + kind, (8, 128))
+    plan_ref[...] = jnp.where(row == 0, plan, jnp.broadcast_to(within, (8, 128)))
 
 
 def near_term(soft, scaled, offset, inside):
@@ -222,7 +234,7 @@
     far = jnp.int32(0)
     for g in range(TILES):
         for k in range(1, 8):
-            entry = steps_ref[k, g]
+            entry = steps_ref[0, TILES * k + g]
             near_ref[near] = entry
             far_ref[far] = entry
             near = near + ((entry >> 16) & 1)
@@ -279,52 +291,53 @@
 
 
 def born_own_kernel(
-    slab_ref, lists_ref, counts_ref, own_ref, other_ref, radii_ref,
+    slab_ref, index_ref, own_ref, other_ref, radii_ref,
     blocks_ref, left_ref, right_ref, offsets_ref, acc_ref, plan_ref,
-    near_ref, far_ref, index_ref, steps_ref, sem, *buffers,
+    near_ref, far_ref, steps_ref, sem, *buffers,
 ):
     offset = radii_ref[...] - OFFSET
     sources = ((2, rows_in(own_ref)), (inner_slot(slab_ref[0]), rows_in(other_ref)))
-    plan_of(lists_ref, counts_ref, least_of(offset), sources, index_ref, plan_ref, own_ref)
+    plan_of(index_ref, least_of(offset), sources, own_ref, plan_ref)
     copy = pltpu.make_async_copy(plan_ref, steps_ref, sem)
     copy.start()
     centre = (8 * slab_ref[0] + 4).astype(jnp.float32)
     for place, read in sources:
         fill_blocks(blocks_ref, read, place * TILES, centre)
         fill_right(right_ref, blocks_ref, place * TILES)
+    copy.wait()
+    counts = split_lists(steps_ref, near_ref, far_ref)
     fill_left(left_ref, blocks_ref)
     for g in range(TILES):
         offsets_ref[g] = column_of(offset[g : g + 1])
     offsets_ref[TILES] = offsets_ref[0]
-    copy.wait()
-    counts = split_lists(steps_ref, near_ref, far_ref)
     sum_pairs(
         left_ref, right_ref, blocks_ref, offsets_ref, acc_ref, buffers,
-        (near_ref, far_ref), counts, steps_ref[8, 0], True,
+        (near_ref, far_ref), counts, steps_ref[1, 0], True,
     )
 
 
 def born_rest_kernel(
-    slab_ref, fill_ref, lists_ref, counts_ref, own_ref, even_ref, odd_ref, radii_ref,
+    slab_ref, fill_ref, index_ref, own_ref, even_ref, odd_ref, radii_ref,
     left_ref, offsets_ref, blocks_in, right_in, acc_in,
     plan_ref, born_ref, send_ref, blocks_ref, right_ref, acc_ref,
-    near_ref, far_ref, index_ref, steps_ref, sem, sums_ref, *buffers,
+    near_ref, far_ref, steps_ref, sem, sums_ref, *buffers,
 ):
     slab = slab_ref[0]
     sources = outer_slabs(slab, even_ref, odd_ref, ROWS)
     offset = radii_ref[...] - OFFSET
-    plan_of(lists_ref, counts_ref, least_of(offset), sources, index_ref, plan_ref, own_ref)
+    plan_of(index_ref, least_of(offset), sources, own_ref, plan_ref)
     copy = pltpu.make_async_copy(plan_ref, steps_ref, sem)
     copy.start()
     centre = (8 * slab + 4).astype(jnp.float32)
-    for place, read in sources:
+    for i, (place, read) in enumerate(sources):
+        if i == 1:
+            copy.wait()
+            counts = split_lists(steps_ref, near_ref, far_ref)
         fill_blocks(blocks_ref, read, place * TILES, centre)
         fill_right(right_ref, blocks_ref, place * TILES)
-    copy.wait()
-    counts = split_lists(steps_ref, near_ref, far_ref)
     sum_pairs(
         left_ref, right_ref, blocks_ref, offsets_ref, acc_ref, buffers,
-        (near_ref, far_ref), counts, steps_ref[8, 0], False,
+        (near_ref, far_ref), counts, steps_ref[1, 0], False,
     )
     for g in range(TILES):
         sums_ref[g : g + 1, :] = jnp.sum(acc_ref[g].T, axis=0, keepdims=True)
@@ -339,14 +352,11 @@
     send_ref[...] = jnp.where(live, born, 1.0)
 
 
-def energy_list(plan_ref, steps_ref, list_ref, sem):
-    copy = pltpu.make_async_copy(plan_ref, steps_ref, sem)
-    copy.start()
-    copy.wait()
+def energy_list(steps_ref, list_ref):
     count = jnp.int32(0)
     for g in range(TILES):
         for k in range(1, 8):
-            entry = steps_ref[k, g]
+            entry = steps_ref[0, TILES * k + g]
             list_ref[count] = entry
             count = count + jnp.minimum(entry >> 16, 1)
     pad_list(list_ref, count)
@@ -380,10 +390,14 @@
     column_ref, inverse_ref, acc_ref,
     list_ref, steps_ref, born_ref, sem, *buffers,
 ):
-    count = energy_list(plan_ref, steps_ref, list_ref, sem)
+    copy = pltpu.make_async_copy(plan_ref, steps_ref, sem)
+    copy.start()
     born_ref[2 * TILES : 3 * TILES, :] = own_ref[...]
     born_ref[pl.ds(inner_slot(slab_ref[0]) * TILES, TILES), :] = other_ref[...]
     for g in range(TILES):
+        if g == 6:
+            copy.wait()
+            count = energy_list(steps_ref, list_ref)
         column = column_of(own_ref[g : g + 1, :])
         column_ref[g] = column
         inverse_ref[g] = (-0.25 * LOG2E) / column
@@ -400,17 +414,21 @@
     energy_ref, share_ref, acc_ref,
     list_ref, steps_ref, born_ref, sem, charge_ref, *buffers,
 ):
-    count = energy_list(plan_ref, steps_ref, list_ref, sem)
+    copy = pltpu.make_async_copy(plan_ref, steps_ref, sem)
+    copy.start()
     for place, read in outer_slabs(slab_ref[0], even_ref, odd_ref, TILES):
         born_ref[pl.ds(place * TILES, TILES), :] = read(0, TILES)
     born_ref[2 * TILES : 3 * TILES, :] = jnp.ones((TILES, 128), jnp.float32)
+    for g in range(TILES):
+        charge_ref[g : g + 1, :] = blocks_ref[2 * TILES + g, 4:5, :]
+    copy.wait()
+    count = energy_list(steps_ref, list_ref)
     sum_energy(
         left_ref, right_ref, blocks_ref, born_ref, column_ref, inverse_ref, acc_ref, buffers,
         entry_in(list_ref), count, False,
     )
     for g in range(TILES):
         energy_ref[g : g + 1, :] = jnp.sum(acc_ref[g].T, axis=0, keepdims=True)
-        charge_ref[g : g + 1, :] = blocks_ref[2 * TILES + g, 4:5, :]
     energy = -0.5 * charge_ref[...] * energy_ref[...]
     energy_ref[...] = energy
     share = jnp.sum(jnp.sum(energy, axis=0, keepdims=True), axis=1, keepdims=True)
@@ -450,10 +468,10 @@
     blocks_type = pltpu.VMEM((5 * TILES, 8, 128), f32)
     right_type = pltpu.VMEM((5 * TILES, 64, 128), jnp.bfloat16)
     left_type = pltpu.VMEM((TILES, 128, 64), jnp.bfloat16)
-    plan_type = pltpu.VMEM((16, 128), jnp.int32)
+    plan_type = pltpu.VMEM((8, 128), jnp.int32)
     slab_type = pltpu.VMEM((TILES, 128), f32)
     entries = pltpu.SMEM((144,), jnp.int32)
-    steps = pltpu.SMEM((16, 128), jnp.int32)
+    steps = pltpu.SMEM((8, 128), jnp.int32)
     squares = [pltpu.VMEM((128, 128), f32)] * 8
     sem = pltpu.SemaphoreType.DMA
 
@@ -464,25 +482,25 @@
         pltpu.with_memory_space_constraint(value, pltpu.HBM)
         for value in (coords, charges, radii, screens, lists, counts)
     )
-    (packed,) = call(
-        prep_kernel, "prep", (pltpu.VMEM((ROWS, 128), f32),),
-        (slab, slab_fill), (coords, charges, radii, screens), [],
+    packed, index, kept = call(
+        prep_kernel, "prep", (pltpu.VMEM((ROWS, 128), f32), plan_type, slab_type),
+        (slab, slab_fill), (coords, charges, radii, screens, lists, counts), [],
     )
     other, even, odd = neighbours(packed)
-    packed, other, even, odd = near(packed, other, even, odd)
+    packed, other, even, odd, index, kept = near(packed, other, even, odd, index, kept)
     blocks, left, right, offsets, acc, own_plan = call(
         born_own_kernel, "born_own",
         (blocks_type, left_type, right_type, stack, stack, plan_type),
-        (slab,), (lists, counts, packed, other, radii),
-        [entries, entries, plan_type, steps, sem] + squares, flops=1 << 27,
+        (slab,), (index, packed, other, kept),
+        [entries, entries, steps, sem] + squares, flops=1 << 27,
     )
     plan, born, send, blocks, right, acc = call(
         born_rest_kernel, "born_rest",
-        (plan_type, jax.ShapeDtypeStruct((TILES, 128), f32), slab_type, blocks_type, right_type, stack),
+        (plan_type, slab_type, slab_type, blocks_type, right_type, stack),
         (slab, slab_fill),
-        (lists, counts, packed, even, odd, radii, *near(left, offsets, blocks, right, acc)),
-        [entries, entries, plan_type, steps, sem, slab_type] + squares,
-        aliases={10: 3, 11: 4, 12: 5},
+        (index, packed, even, odd, kept, *near(left, offsets, blocks, right, acc)),
+        [entries, entries, steps, sem, slab_type] + squares,
+        aliases={9: 3, 10: 4, 11: 5},
     )
     born_other, born_even, born_odd = neighbours(send)
     column, inverse, acc = call(
@@ -492,7 +510,7 @@
     )
     energy, share, acc = call(
         energy_rest_kernel, "energy_rest",
-        (jax.ShapeDtypeStruct((TILES, 128), f32), pltpu.VMEM((count, 1, 128), f32), stack),
+        (slab_type, pltpu.VMEM((count, 1, 128), f32), stack),
         (slab,), near(plan, blocks, left, right, born_even, born_odd, column, inverse, acc),
         [entries, steps, pltpu.VMEM((5 * TILES, 128), f32), sem, slab_type] + squares,
         aliases={9: 2},

time: 57.9 us -> 57 us (0.984)
  blocking collectives: 27.9 us -> 0 us
  starting transfers between devices: 6.87 us -> 20.7 us
  waiting for transfers between devices: 2.03 us -> 13.7 us
  local copies, waits for them, and re-layouts: 0.01 us -> 1.21 us
    all_to_all x1 -> x0, blocking collectives: 27.9 us -> none  [shards(): shares = lax.all_to_all(share, SLAB, 0, 0, tiled=True)]
    all_to_all x0 -> x1, starting transfers between devices: none -> 14.2 us  [shards(): shares = lax.all_to_all(share, SLAB, 0, 0, tiled=True)]
    all_to_all x0 -> x1, waiting for transfers between devices: none -> 11.7 us  [shards(): shares = lax.all_to_all(share, SLAB, 0, 0, tiled=True)]
    unnamed x1 -> x4, local copies, waits for them, and re-layouts: 0.01 us -> 1.21 us
  transfers between devices with their start and end apart: 6 -> 7, of which waited for: 2 -> 3; matrix products, arithmetic and copies ran while one was open for 0% -> 2% of each run, Pallas kernels for 16% -> 16%
where the time goes in v6:
time: 57 us; the launch traced here: 56.3 us
  starting transfers between devices  20.7 us (36%)
  Pallas kernels  19.3 us (34%)
  waiting for transfers between devices  13.7 us (24%)
  between operations  1.39 us (2%)
  local copies, waits for them, and re-layouts  1.21 us (2%)
    pallas_call x6, Pallas kernels, call(): pl.pallas_call(kernel, out_shape=outs, in_specs=[smem] * len(scalars) + [...  19.3 us
    all_to_all x1, starting transfers between devices, shards(): shares = lax.all_to_all(share, SLAB, 0, 0, tiled=True)  14.2 us
    all_to_all x1, waiting for transfers between devices, shards(): shares = lax.all_to_all(share, SLAB, 0, 0, tiled=True)  11.7 us
    ppermute x2, starting transfers between devices, neighbours(): other = lax.ppermute(value, SLAB, [(i, i ^ 1) for i in range(count)])  3.38 us
    ppermute x4, starting transfers between devices, neighbours(): lax.ppermute(both, SLAB, chip_swap(count, odd))  3.09 us
    ppermute x2, waiting for transfers between devices, neighbours(): other = lax.ppermute(value, SLAB, [(i, i ^ 1) for i in range(count)])  2.02 us
    unnamed x4, local copies, waits for them, and re-layouts  1.21 us
  transfers between devices with their start and end apart: 7, of which 3 were waited for; matrix products, arithmetic and copies ran while one was open for 2% of the time, Pallas kernels for 16%

profile of v6, /device:TPU:1, one launch (start us, length us, event | category | flops | bytes accessed | tf_op | source)
XLA Modules:
  0.0 56.3 jit_solution(15422532558528493339)
XLA Ops:
  1.3 0.9 %prep.1 = (f32[88,128]{1,0:T(8,128)S(1)}, s32[8,128]{1,0:T(8,128)S(1)}, f32[16,128]{1,0:T(8,128)S(1)}) custom-call(s32[1]{0:T(128)} %bitcast.slab_ref, s32[1]{0:T(128)S(6)} %copy.22.fill_ref, f32[3,2048]{1,0:T(4,128)} %coords_ref.1, f32[16,128]{1,0:T(8,128)} %bitcast.11, f32[16,128]{1,0:T(8,128)} %bitcast.12, f32[16,128]{1,0:T(8,128)} %bitcast.13, ...), custom_call_target="tpu_custom_call" | custom-call | tf_op jit(solution)/shard_map/prep/pallas_call | solution.py:455
  2.2 3.3 %collective-permute-start = (f32[88,128]{1,0:T(8,128)S(1)}, f32[88,128]{1,0:T(8,128)S(1)}, u32[]{:S(2)}, u32[]{:S(2)}) collective-permute-start(f32[88,128]{1,0:T(8,128)S(1)} %get-tuple-element.23.own_ref), channel_id=1, source_target_pairs={{0,1},{1,0},{2,3},{3,2},{4,5},{5,4},{6,7},{7,6},{8,9},{9,8},{10,11... | collective-permute-start | bytes 135176 | tf_op jit(solution)/shard_map/ppermute | solution.py:32
  5.5 0.9 %collective-permute-done.other_ref = f32[88,128]{1,0:T(8,128)S(1)} collective-permute-done((f32[88,128]{1,0:T(8,128)S(1)}, f32[88,128]{1,0:T(8,128)S(1)}, u32[]{:S(2)}, u32[]{:S(2)}) %collective-permute-start) | collective-permute-done | bytes 45088 | tf_op jit(solution)/shard_map/ppermute | solution.py:32
  6.4 0.3 collective-permute-start.2
  6.8 0.5 collective-permute-start.1
  7.3 5.9 %born_own.1 = (f32[80,8,128]{2,1,0:T(8,128)S(1)}, bf16[16,128,64]{2,1,0:T(8,128)(2,1)S(1)}, bf16[80,64,128]{2,1,0:T(8,128)(2,1)S(1)}, f32[17,128,128]{2,1,0:T(8,...) custom-call(s32[1]{0:T(128)} %bitcast.slab_ref, s32[8,128]{1,0:T(8,128)S(1)} %get-tuple-element.22.index_ref, ...), custom_call_target="tpu_custom_call" | custom-call | flops 134217728 | tf_op jit(solution)/shard_map/born_own/pallas_call | solution.py:455
  13.2 0.0 collective-permute-done.2.odd_ref
  13.2 0.0 collective-permute-done.1.even_ref
  13.2 4.4 %born_rest.1 = (s32[8,128]{1,0:T(8,128)S(1)}, f32[16,128]{1,0:T(8,128)S(1)}, f32[16,128]{1,0:T(8,128)S(1)}, f32[80,8,128]{2,1,0:T(8,128)S(1)}, bf16[80,64,128]{2...) custom-call(s32[1]{0:T(128)} %bitcast.slab_ref, ...), custom_call_target="tpu_custom_call", output_to_operand_aliasing={{3}: (9, {}), {4}: (10, {}), {5}: (11, {})} | custom-call | tf_op jit(solution)/shard_map/born_rest/pallas_call | solution.py:455
  17.5 0.1 collective-permute-start.3
  17.7 1.1 %collective-permute-done.3.other_ref = f32[16,128]{1,0:T(8,128)S(1)} collective-permute-done((f32[16,128]{1,0:T(8,128)S(1)}, f32[16,128]{1,0:T(8,128)S(1)}, u32[]{:S(2)}, u32[]{:S(2)}) %collective-permute-start.3) | collective-permute-done | bytes 8224 | tf_op jit(solution)/shard_map/ppermute | solution.py:32
  18.8 0.2 collective-permute-start.5
  19.0 2.0 %collective-permute-start.4 = (f32[32,128]{1,0:T(8,128)S(1)}, f32[32,128]{1,0:T(8,128)S(1)}, u32[]{:S(2)}, u32[]{:S(2)}) collective-permute-start(f32[32,128]{1,0:T(8,128)S(1)} %constant_dynamic-update-slice_fusion.2), channel_id=1, source_target_pairs={{0,2},{1,3},{2,0},{3,1},{4,6},{5,7},{6,4},{7,5},{8,10},{9,11},{10,... | collective-permute-start | bytes 49160 | tf_op jit(solution)/shard_map/ppermute | solution.py:34
  21.0 3.4 %energy_own.1 = (f32[17,128,128]{2,1,0:T(8,128)S(1)}, f32[17,128,128]{2,1,0:T(8,128)S(1)}, f32[17,128,128]{2,1,0:T(8,128)S(1)}) custom-call(s32[1]{0:T(128)} %bitcast.slab_ref, s32[8,128]{1,0:T(8,128)S(1)} %get-tuple-element.35.plan_ref, f32[80,8,128]{2,1,0:T(8,128)S(1)} %get-tuple-element.32.blocks_ref, ...), custom_call_target="tpu_custom_call" | custom-call | flops 134217728 | tf_op jit(solution)/shard_map/energy_own/pallas_call | solution.py:455
  24.4 0.0 collective-permute-done.5.odd_ref
  24.4 0.0 collective-permute-done.4.even_ref
  24.4 4.0 %energy_rest.1 = (f32[16,128]{1,0:T(8,128)S(1)}, f32[256,1,128]{2,1,0:T(1,128)}, f32[17,128,128]{2,1,0:T(8,128)S(1)}) custom-call(s32[1]{0:T(128)} %bitcast.slab_ref, s32[8,128]{1,0:T(8,128)S(1)} %get-tuple-element.31.plan_ref, f32[80,8,128]{2,1,0:T(8,128)S(1)} %get-tuple-element.32.blocks_ref, ...), custom_call_target="tpu_custom_call", output_to_operand_aliasing={{2}: (9, {})} | custom-call | tf_op jit(solution)/shard_map/energy_rest/pallas_call | solution.py:455
  28.4 14.2 %all-to-all-start = ((f32[256,1,128]{2,1,0:T(1,128)}), f32[256,1,128]{2,1,0:T(1,128)S(1)}, u32[]{:S(2)}, u32[]{:S(2)}) async-start(f32[256,1,128]{2,1,0:T(1,128)} %get-tuple-element.40), calls=%async_computation | async-start | bytes 262144 | tf_op jit(solution)/shard_map/all_to_all | solution.py:518
  42.6 0.6 %copy.20 = f32[2048]{0:T(1024)} copy(f32[2048]{0:T(1024)S(1)} %bitcast.9) | data formatting | bytes 16384
  43.2 0.6 %copy.21 = f32[2048]{0:T(1024)} copy(f32[2048]{0:T(1024)S(1)} %bitcast.10) | data formatting | bytes 16384
  43.8 11.7 %all-to-all-done.shares_ref = f32[256,1,128]{2,1,0:T(1,128)S(1)} async-done(((f32[256,1,128]{2,1,0:T(1,128)}), f32[256,1,128]{2,1,0:T(1,128)S(1)}, u32[]{:S(2)}, u32[]{:S(2)}) %all-to-all-start) | async-done | bytes 131104 | tf_op jit(solution)/shard_map/all_to_all | solution.py:518
  55.5 0.8 %total.1 = f32[1]{0:T(128)} custom-call(f32[256,1,128]{2,1,0:T(1,128)S(1)} %all-to-all-done.shares_ref), custom_call_target="tpu_custom_call" | custom-call | tf_op jit(solution)/shard_map/total/pallas_call | solution.py:455
  (4 shorter events, 0.0 us)
Async XLA Ops:
  2.2 4.2 %collective-permute-start = (f32[88,128]{1,0:T(8,128)S(1)}, f32[88,128]{1,0:T(8,128)S(1)}, u32[]{:S(2)}, u32[]{:S(2)}) collective-permute-start(f32[88,128]{1,0:T(8,128)S(1)} %get-tuple-element.23.own_ref), channel_id=1, source_target_pairs={{0,1},{1,0},{2,3},{3,2},{4,5},{5,4},{6,7},{7,6},{8,9},{9,8},{10,11... | collective-permute-start | bytes 135176 | tf_op jit(solution)/shard_map/ppermute | solution.py:32
  6.4 6.8 %collective-permute-start.2 = (f32[176,128]{1,0:T(8,128)S(1)}, f32[176,128]{1,0:T(8,128)S(1)}, u32[]{:S(2)}, u32[]{:S(2)}) collective-permute-start(f32[176,128]{1,0:T(8,128)S(1)} %constant_dynamic-update-slice_fusion), channel_id=1, source_target_pairs={{0,1},{1,0},{2,4},{3,5},{4,2},{5,3},{6,8},{7,9},{8,6},{9,7},{10,12... | collective-permute-start | bytes 270344 | tf_op jit(solution)/shard_map/ppermute | solution.py:34
  6.8 6.4 %collective-permute-start.1 = (f32[176,128]{1,0:T(8,128)S(1)}, f32[176,128]{1,0:T(8,128)S(1)}, u32[]{:S(2)}, u32[]{:S(2)}) collective-permute-start(f32[176,128]{1,0:T(8,128)S(1)} %constant_dynamic-update-slice_fusion), channel_id=1, source_target_pairs={{0,2},{1,3},{2,0},{3,1},{4,6},{5,7},{6,4},{7,5},{8,10},{9,11},{10,... | collective-permute-start | bytes 270344 | tf_op jit(solution)/shard_map/ppermute | solution.py:34
  17.5 1.3 %collective-permute-start.3 = (f32[16,128]{1,0:T(8,128)S(1)}, f32[16,128]{1,0:T(8,128)S(1)}, u32[]{:S(2)}, u32[]{:S(2)}) collective-permute-start(f32[16,128]{1,0:T(8,128)S(1)} %get-tuple-element.34.own_ref), channel_id=1, source_target_pairs={{0,1},{1,0},{2,3},{3,2},{4,5},{5,4},{6,7},{7,6},{8,9},{9,8},{10,11... | collective-permute-start | bytes 24584 | tf_op jit(solution)/shard_map/ppermute | solution.py:32
  18.8 5.6 %collective-permute-start.5 = (f32[32,128]{1,0:T(8,128)S(1)}, f32[32,128]{1,0:T(8,128)S(1)}, u32[]{:S(2)}, u32[]{:S(2)}) collective-permute-start(f32[32,128]{1,0:T(8,128)S(1)} %constant_dynamic-update-slice_fusion.2), channel_id=1, source_target_pairs={{0,1},{1,0},{2,4},{3,5},{4,2},{5,3},{6,8},{7,9},{8,6},{9,7},{10,12... | collective-permute-start | bytes 49160 | tf_op jit(solution)/shard_map/ppermute | solution.py:34
  19.0 5.4 %collective-permute-start.4 = (f32[32,128]{1,0:T(8,128)S(1)}, f32[32,128]{1,0:T(8,128)S(1)}, u32[]{:S(2)}, u32[]{:S(2)}) collective-permute-start(f32[32,128]{1,0:T(8,128)S(1)} %constant_dynamic-update-slice_fusion.2), channel_id=1, source_target_pairs={{0,2},{1,3},{2,0},{3,1},{4,6},{5,7},{6,4},{7,5},{8,10},{9,11},{10,... | collective-permute-start | bytes 49160 | tf_op jit(solution)/shard_map/ppermute | solution.py:34
  28.4 27.1 %all-to-all-start = ((f32[256,1,128]{2,1,0:T(1,128)}), f32[256,1,128]{2,1,0:T(1,128)S(1)}, u32[]{:S(2)}, u32[]{:S(2)}) async-start(f32[256,1,128]{2,1,0:T(1,128)} %get-tuple-element.40), calls=%async_computation | async-start | bytes 262144 | tf_op jit(solution)/shard_map/all_to_all | solution.py:518

commit v7 on v6

--- a/solution.py
+++ b/solution.py
@@ -386,10 +386,12 @@
 
 
 def energy_own_kernel(
-    slab_ref, plan_ref, blocks_ref, left_ref, right_ref, own_ref, other_ref,
-    column_ref, inverse_ref, acc_ref,
-    list_ref, steps_ref, born_ref, sem, *buffers,
+    slab_ref, plan_ref, blocks_ref, left_ref, right_ref, own_ref, other_ref, radii_ref,
+    column_ref, inverse_ref, acc_ref, result_ref,
+    list_ref, steps_ref, born_ref, sem, result_sem, *buffers,
 ):
+    result = pltpu.make_async_copy(radii_ref, result_ref, result_sem)
+    result.start()
     copy = pltpu.make_async_copy(plan_ref, steps_ref, sem)
     copy.start()
     born_ref[2 * TILES : 3 * TILES, :] = own_ref[...]
@@ -406,6 +408,7 @@
     shared = (left_ref, right_ref, blocks_ref, born_ref, column_ref, inverse_ref, acc_ref)
     sum_energy(*shared, buffers, own_entry, TILES, True)
     sum_energy(*shared, buffers, entry_in(list_ref), count, False)
+    result.wait()
 
 
 def energy_rest_kernel(
@@ -435,11 +438,14 @@
     share_ref[...] = jnp.broadcast_to(share[None], share_ref.shape)
 
 
-def total_kernel(shares_ref, total_ref):
+def total_kernel(shares_ref, energy_ref, total_ref, result_ref, sem):
+    result = pltpu.make_async_copy(energy_ref, result_ref, sem)
+    result.start()
     total = shares_ref[0]
     for i in range(1, shares_ref.shape[0]):
         total = total + shares_ref[i]
     total_ref[0] = total[0, 0]
+    result.wait()
 
 
 def shards(coords, charges, radii, screens, tile_lists, tile_counts, slab_fill):
@@ -470,6 +476,8 @@
     left_type = pltpu.VMEM((TILES, 128, 64), jnp.bfloat16)
     plan_type = pltpu.VMEM((8, 128), jnp.int32)
     slab_type = pltpu.VMEM((TILES, 128), f32)
+    result_type = pltpu.HBM((TILES, 128), f32)
+    hbm = pl.BlockSpec(memory_space=pltpu.HBM)
     entries = pltpu.SMEM((144,), jnp.int32)
     steps = pltpu.SMEM((8, 128), jnp.int32)
     squares = [pltpu.VMEM((128, 128), f32)] * 8
@@ -503,10 +511,11 @@
         aliases={9: 3, 10: 4, 11: 5},
     )
     born_other, born_even, born_odd = neighbours(send)
-    column, inverse, acc = call(
-        energy_own_kernel, "energy_own", (stack,) * 3,
-        (slab,), near(own_plan, blocks, left, right, send, born_other),
-        [entries, steps, pltpu.VMEM((5 * TILES, 128), f32), sem] + squares, flops=1 << 27,
+    column, inverse, acc, born = call(
+        energy_own_kernel, "energy_own", (stack, stack, stack, result_type),
+        (slab,), near(own_plan, blocks, left, right, send, born_other, born),
+        [entries, steps, pltpu.VMEM((5 * TILES, 128), f32), sem, sem] + squares,
+        out_specs=(vmem, vmem, vmem, hbm), flops=1 << 27,
     )
     energy, share, acc = call(
         energy_rest_kernel, "energy_rest",
@@ -516,8 +525,9 @@
         aliases={9: 2},
     )
     shares = lax.all_to_all(share, SLAB, 0, 0, tiled=True)
-    (total,) = call(
-        total_kernel, "total", (jax.ShapeDtypeStruct((1,), f32),), (), near(shares), [], out_specs=(smem,)
+    total, energy = call(
+        total_kernel, "total", (jax.ShapeDtypeStruct((1,), f32), result_type), (),
+        near(shares, energy), [sem], out_specs=(smem, hbm),
     )
     return (born.reshape(-1), energy.reshape(-1), total[0])
 

time: 57 us -> 56.2 us (0.986); the launches traced: 56.3 us -> 56.6 us
  blocking collectives: 0 us -> 30.5 us
  starting transfers between devices: 20.7 us -> 8.29 us
  waiting for transfers between devices: 13.7 us -> 1.71 us
  Pallas kernels: 19.3 us -> 14.7 us
  local copies, waits for them, and re-layouts: 1.21 us -> 0.01 us
    all_to_all x0 -> x1, blocking collectives: none -> 30.5 us  [shards(): shares = lax.all_to_all(share, SLAB, 0, 0, tiled=True)]
    all_to_all x1 -> x0, starting transfers between devices: 14.2 us -> none  [shards(): shares = lax.all_to_all(share, SLAB, 0, 0, tiled=True)]
    all_to_all x1 -> x0, waiting for transfers between devices: 11.7 us -> none  [shards(): shares = lax.all_to_all(share, SLAB, 0, 0, tiled=True)]
    pallas_call x6, Pallas kernels: 19.3 us -> 14.7 us  [call(): pl.pallas_call(kernel, out_shape=outs, in_specs=[smem] * len(scalars) + [...]
    ppermute x2, starting transfers between devices: 3.38 us -> 6.85 us  [neighbours(): other = lax.ppermute(value, SLAB, [(i, i ^ 1) for i in range(count)])]
    ppermute x4, starting transfers between devices: 3.09 us -> 1.44 us  [neighbours(): lax.ppermute(both, SLAB, chip_swap(count, odd))]
    unnamed x4 -> x2, local copies, waits for them, and re-layouts: 1.21 us -> 0.01 us
  transfers between devices with their start and end apart: 7 -> 6, of which waited for: 3 -> 2; matrix products, arithmetic and copies ran while one was open for 2% -> 0% of each run, Pallas kernels for 16% -> 12%
where the time goes in v7:
time: 56.2 us; the launch traced here: 56.6 us
  blocking collectives  30.5 us (54%)
  Pallas kernels  14.7 us (26%)
  starting transfers between devices  8.29 us (15%)
  waiting for transfers between devices  1.71 us (3%)
  between operations  1.37 us (2%)
    all_to_all x1, blocking collectives, shards(): shares = lax.all_to_all(share, SLAB, 0, 0, tiled=True)  30.5 us
    pallas_call x6, Pallas kernels, call(): pl.pallas_call(kernel, out_shape=outs, in_specs=[smem] * len(scalars) + [...  14.7 us
    ppermute x2, starting transfers between devices, neighbours(): other = lax.ppermute(value, SLAB, [(i, i ^ 1) for i in range(count)])  6.85 us
    ppermute x2, waiting for transfers between devices, neighbours(): other = lax.ppermute(value, SLAB, [(i, i ^ 1) for i in range(count)])  1.7 us
    ppermute x4, starting transfers between devices, neighbours(): lax.ppermute(both, SLAB, chip_swap(count, odd))  1.44 us
  transfers between devices with their start and end apart: 6, of which 2 were waited for; matrix products, arithmetic and copies ran while one was open for 0% of the time, Pallas kernels for 12%

profile of v7, /device:TPU:1, one launch (start us, length us, event | category | flops | bytes accessed | tf_op | source)
XLA Modules:
  0.0 56.6 jit_solution(12113975260469347265)
XLA Ops:
  1.3 0.9 %prep.1 = (f32[88,128]{1,0:T(8,128)S(1)}, s32[8,128]{1,0:T(8,128)S(1)}, f32[16,128]{1,0:T(8,128)S(1)}) custom-call(s32[1]{0:T(128)} %bitcast.slab_ref, s32[1]{0:T(128)S(6)} %copy.20.fill_ref, f32[3,2048]{1,0:T(4,128)} %coords_ref.1, f32[16,128]{1,0:T(8,128)} %bitcast.9, f32[16,128]{1,0:T(8,128)} %bitcast.10, f32[16,128]{1,0:T(8,128)} %bitcast.11, ...), custom_call_target="tpu_custom_call" | custom-call | tf_op jit(solution)/shard_map/prep/pallas_call | solution.py:461
  2.2 3.3 %collective-permute-start = (f32[88,128]{1,0:T(8,128)S(1)}, f32[88,128]{1,0:T(8,128)S(1)}, u32[]{:S(2)}, u32[]{:S(2)}) collective-permute-start(f32[88,128]{1,0:T(8,128)S(1)} %get-tuple-element.26.own_ref), channel_id=1, source_target_pairs={{0,1},{1,0},{2,3},{3,2},{4,5},{5,4},{6,7},{7,6},{8,9},{9,8},{10,11... | collective-permute-start | bytes 135176 | tf_op jit(solution)/shard_map/ppermute | solution.py:32
  5.5 0.9 %collective-permute-done.other_ref = f32[88,128]{1,0:T(8,128)S(1)} collective-permute-done((f32[88,128]{1,0:T(8,128)S(1)}, f32[88,128]{1,0:T(8,128)S(1)}, u32[]{:S(2)}, u32[]{:S(2)}) %collective-permute-start) | collective-permute-done | bytes 45088 | tf_op jit(solution)/shard_map/ppermute | solution.py:32
  6.4 0.3 collective-permute-start.2
  6.8 0.5 collective-permute-start.1
  7.3 4.5 %born_own.1 = (f32[80,8,128]{2,1,0:T(8,128)S(1)}, bf16[16,128,64]{2,1,0:T(8,128)(2,1)S(1)}, bf16[80,64,128]{2,1,0:T(8,128)(2,1)S(1)}, f32[17,128,128]{2,1,0:T(8,...) custom-call(s32[1]{0:T(128)} %bitcast.slab_ref, s32[8,128]{1,0:T(8,128)S(1)} %get-tuple-element.25.index_ref, ...), custom_call_target="tpu_custom_call" | custom-call | flops 134217728 | tf_op jit(solution)/shard_map/born_own/pallas_call | solution.py:461
  11.8 0.0 collective-permute-done.2.odd_ref
  11.8 0.0 collective-permute-done.1.even_ref
  11.8 3.3 %born_rest.1 = (s32[8,128]{1,0:T(8,128)S(1)}, f32[16,128]{1,0:T(8,128)S(1)}, f32[16,128]{1,0:T(8,128)S(1)}, f32[80,8,128]{2,1,0:T(8,128)S(1)}, bf16[80,64,128]{2...) custom-call(s32[1]{0:T(128)} %bitcast.slab_ref, ...), custom_call_target="tpu_custom_call", output_to_operand_aliasing={{3}: (9, {}), {4}: (10, {}), {5}: (11, {})} | custom-call | tf_op jit(solution)/shard_map/born_rest/pallas_call | solution.py:461
  15.2 3.6 %collective-permute-start.3 = (f32[16,128]{1,0:T(8,128)S(1)}, f32[16,128]{1,0:T(8,128)S(1)}, u32[]{:S(2)}, u32[]{:S(2)}) collective-permute-start(f32[16,128]{1,0:T(8,128)S(1)} %get-tuple-element.36.own_ref), channel_id=1, source_target_pairs={{0,1},{1,0},{2,3},{3,2},{4,5},{5,4},{6,7},{7,6},{8,9},{9,8},{10,11... | collective-permute-start | bytes 24584 | tf_op jit(solution)/shard_map/ppermute | solution.py:32
  18.7 0.8 %collective-permute-done.3.other_ref = f32[16,128]{1,0:T(8,128)S(1)} collective-permute-done((f32[16,128]{1,0:T(8,128)S(1)}, f32[16,128]{1,0:T(8,128)S(1)}, u32[]{:S(2)}, u32[]{:S(2)}) %collective-permute-start.3) | collective-permute-done | bytes 8224 | tf_op jit(solution)/shard_map/ppermute | solution.py:32
  19.6 0.3 collective-permute-start.5
  19.9 0.2 collective-permute-start.4
  20.1 2.4 %energy_own.1 = (f32[17,128,128]{2,1,0:T(8,128)S(1)}, f32[17,128,128]{2,1,0:T(8,128)S(1)}, f32[17,128,128]{2,1,0:T(8,128)S(1)}, f32[16,128]{1,0:T(8,128)}) custom-call(s32[1]{0:T(128)} %bitcast.slab_ref, s32[8,128]{1,0:T(8,128)S(1)} %get-tuple-element.28.plan_ref, f32[80,8,128]{2,1,0:T(8,128)S(1)} %get-tuple-element.34.blocks_ref, ...), custom_call_target="tpu_custom_call" | custom-call | flops 134217728 | tf_op jit(solution)/shard_map/energy_own/pallas_call | solution.py:461
  22.6 0.0 collective-permute-done.5.odd_ref
  22.6 0.0 collective-permute-done.4.even_ref
  22.6 2.4 %energy_rest.1 = (f32[16,128]{1,0:T(8,128)S(1)}, f32[256,1,128]{2,1,0:T(1,128)S(1)}, f32[17,128,128]{2,1,0:T(8,128)S(1)}) custom-call(s32[1]{0:T(128)} %bitcast.slab_ref, s32[8,128]{1,0:T(8,128)S(1)} %get-tuple-element.39.plan_ref, f32[80,8,128]{2,1,0:T(8,128)S(1)} %get-tuple-element.34.blocks_ref, ...), custom_call_target="tpu_custom_call", output_to_operand_aliasing={{2}: (9, {})} | custom-call | tf_op jit(solution)/shard_map/energy_rest/pallas_call | solution.py:461
  25.0 30.5 %all_to_all.5.shares_ref = f32[256,1,128]{2,1,0:T(1,128)S(1)} all-to-all(f32[256,1,128]{2,1,0:T(1,128)S(1)} %get-tuple-element.43), channel_id=1, replica_groups=mesh['slab_0'=4,'slab_1'=8,'slab_2'=4,'slab_3'=2] {'slab_0','slab_1','sl..., dimensions={0} | all-to-all | bytes 262144 | tf_op jit(solution)/shard_map/all_to_all | solution.py:527
  55.5 1.1 %total.1 = (f32[1]{0:T(128)}, f32[16,128]{1,0:T(8,128)}) custom-call(f32[256,1,128]{2,1,0:T(1,128)S(1)} %all_to_all.5.shares_ref, f32[16,128]{1,0:T(8,128)S(1)} %get-tuple-element.44.energy_ref), custom_call_target="tpu_custom_call" | custom-call | tf_op jit(solution)/shard_map/total/pallas_call | solution.py:461
  (4 shorter events, 0.0 us)
Async XLA Ops:
  2.2 4.2 %collective-permute-start = (f32[88,128]{1,0:T(8,128)S(1)}, f32[88,128]{1,0:T(8,128)S(1)}, u32[]{:S(2)}, u32[]{:S(2)}) collective-permute-start(f32[88,128]{1,0:T(8,128)S(1)} %get-tuple-element.26.own_ref), channel_id=1, source_target_pairs={{0,1},{1,0},{2,3},{3,2},{4,5},{5,4},{6,7},{7,6},{8,9},{9,8},{10,11... | collective-permute-start | bytes 135176 | tf_op jit(solution)/shard_map/ppermute | solution.py:32
  6.4 5.4 %collective-permute-start.2 = (f32[176,128]{1,0:T(8,128)S(1)}, f32[176,128]{1,0:T(8,128)S(1)}, u32[]{:S(2)}, u32[]{:S(2)}) collective-permute-start(f32[176,128]{1,0:T(8,128)S(1)} %constant_dynamic-update-slice_fusion), channel_id=1, source_target_pairs={{0,1},{1,0},{2,4},{3,5},{4,2},{5,3},{6,8},{7,9},{8,6},{9,7},{10,12... | collective-permute-start | bytes 270344 | tf_op jit(solution)/shard_map/ppermute | solution.py:34
  6.8 5.1 %collective-permute-start.1 = (f32[176,128]{1,0:T(8,128)S(1)}, f32[176,128]{1,0:T(8,128)S(1)}, u32[]{:S(2)}, u32[]{:S(2)}) collective-permute-start(f32[176,128]{1,0:T(8,128)S(1)} %constant_dynamic-update-slice_fusion), channel_id=1, source_target_pairs={{0,2},{1,3},{2,0},{3,1},{4,6},{5,7},{6,4},{7,5},{8,10},{9,11},{10,... | collective-permute-start | bytes 270344 | tf_op jit(solution)/shard_map/ppermute | solution.py:34
  15.2 4.4 %collective-permute-start.3 = (f32[16,128]{1,0:T(8,128)S(1)}, f32[16,128]{1,0:T(8,128)S(1)}, u32[]{:S(2)}, u32[]{:S(2)}) collective-permute-start(f32[16,128]{1,0:T(8,128)S(1)} %get-tuple-element.36.own_ref), channel_id=1, source_target_pairs={{0,1},{1,0},{2,3},{3,2},{4,5},{5,4},{6,7},{7,6},{8,9},{9,8},{10,11... | collective-permute-start | bytes 24584 | tf_op jit(solution)/shard_map/ppermute | solution.py:32
  19.6 3.0 %collective-permute-start.5 = (f32[32,128]{1,0:T(8,128)S(1)}, f32[32,128]{1,0:T(8,128)S(1)}, u32[]{:S(2)}, u32[]{:S(2)}) collective-permute-start(f32[32,128]{1,0:T(8,128)S(1)} %constant_dynamic-update-slice_fusion.2), channel_id=1, source_target_pairs={{0,1},{1,0},{2,4},{3,5},{4,2},{5,3},{6,8},{7,9},{8,6},{9,7},{10,12... | collective-permute-start | bytes 49160 | tf_op jit(solution)/shard_map/ppermute | solution.py:34
  19.9 2.7 %collective-permute-start.4 = (f32[32,128]{1,0:T(8,128)S(1)}, f32[32,128]{1,0:T(8,128)S(1)}, u32[]{:S(2)}, u32[]{:S(2)}) collective-permute-start(f32[32,128]{1,0:T(8,128)S(1)} %constant_dynamic-update-slice_fusion.2), channel_id=1, source_target_pairs={{0,2},{1,3},{2,0},{3,1},{4,6},{5,7},{6,4},{7,5},{8,10},{9,11},{10,... | collective-permute-start | bytes 49160 | tf_op jit(solution)/shard_map/ppermute | solution.py:34

commit v8 on v7

--- a/solution.py
+++ b/solution.py
@@ -223,9 +223,9 @@
     total = (upper + lower) * ratio
     weight = gap * upper * inverse
     logs = jnp.log(lower * lower * ratio)
-    term = difference * (4.0 - weight * total) + (inverse + inverse) * logs
+    term = difference * (2.0 - 0.5 * (weight * total)) + inverse * logs
     if inside:
-        term += jnp.where(offset < -gap, 16.0 * (1.0 / offset - 1.0 / lower), 0.0)
+        term += jnp.where(offset < -gap, 8.0 * (1.0 / offset - 1.0 / lower), 0.0)
     return term
 
 
@@ -274,11 +274,11 @@
             gap = soft * inverse - scaled
             ratio = 1.0 / (soft - scaled * scaled)
             logs = jnp.log(gap * gap * ratio)
-            acc_ref[slot, rows, :] += (4.0 * scaled) * ratio + (inverse + inverse) * logs
+            acc_ref[slot, rows, :] += (2.0 * scaled) * ratio + inverse * logs
 
     def near_lists(inside):
         if own:
-            run_list(TILES, own_entry, buffers[:4], produce, consume_near(inside, True))
+            run_list(TILES, own_entry, buffers, produce, consume_near(inside, True))
         run_list(counts[0], entry_in(lists[0]), buffers[:4], produce, consume_near(inside, False))
 
     pl.when(within == 0)(lambda: near_lists(False))
@@ -345,7 +345,7 @@
     live = slot < fill_ref[0]
     radius = jnp.where(live, radii_ref[...], 1.5)
     inner = radius - OFFSET
-    psi = 0.125 * sums_ref[...] * inner
+    psi = 0.25 * sums_ref[...] * inner
     bending = jnp.tanh(psi - 0.8 * psi * psi + 4.85 * psi * psi * psi)
     born = 1.0 / (1.0 / inner - bending / radius)
     born_ref[...] = jnp.where(live, born, 0.0)

time: 56.2 us -> 57 us (1.014); the launches traced: 56.6 us -> 56.5 us
  starting transfers between devices: 8.29 us -> 5.87 us
  Pallas kernels: 14.7 us -> 16.1 us
  blocking collectives: 30.5 us -> 31.5 us
    ppermute x2, starting transfers between devices: 6.85 us -> 4.32 us  [neighbours(): other = lax.ppermute(value, SLAB, [(i, i ^ 1) for i in range(count)])]
    pallas_call x6, Pallas kernels: 14.7 us -> 16.1 us  [call(): pl.pallas_call(kernel, out_shape=outs, in_specs=[smem] * len(scalars) + [...]
    all_to_all x1, blocking collectives: 30.5 us -> 31.5 us  [shards(): shares = lax.all_to_all(share, SLAB, 0, 0, tiled=True)]
  transfers between devices with their start and end apart: 6 -> 6, of which waited for: 2 -> 2; matrix products, arithmetic and copies ran while one was open for 0% -> 0% of each run, Pallas kernels for 12% -> 14%
where the time goes in v8:
time: 57 us; the launch traced here: 56.5 us
  blocking collectives  31.5 us (55%)
  Pallas kernels  16.1 us (28%)
  starting transfers between devices  5.87 us (10%)
  waiting for transfers between devices  1.71 us (3%)
  between operations  1.37 us (2%)
    all_to_all x1, blocking collectives, shards(): shares = lax.all_to_all(share, SLAB, 0, 0, tiled=True)  31.5 us
    pallas_call x6, Pallas kernels, call(): pl.pallas_call(kernel, out_shape=outs, in_specs=[smem] * len(scalars) + [...  16.1 us
    ppermute x2, starting transfers between devices, neighbours(): other = lax.ppermute(value, SLAB, [(i, i ^ 1) for i in range(count)])  4.32 us
    ppermute x2, waiting for transfers between devices, neighbours(): other = lax.ppermute(value, SLAB, [(i, i ^ 1) for i in range(count)])  1.7 us
    ppermute x4, starting transfers between devices, neighbours(): lax.ppermute(both, SLAB, chip_swap(count, odd))  1.55 us
  transfers between devices with their start and end apart: 6, of which 2 were waited for; matrix products, arithmetic and copies ran while one was open for 0% of the time, Pallas kernels for 14%

profile of v8, /device:TPU:1, one launch (start us, length us, event | category | flops | bytes accessed | tf_op | source)
XLA Modules:
  0.0 56.5 jit_solution(16400305751075898718)
XLA Ops:
  1.3 0.9 %prep.1 = (f32[88,128]{1,0:T(8,128)S(1)}, s32[8,128]{1,0:T(8,128)S(1)}, f32[16,128]{1,0:T(8,128)S(1)}) custom-call(s32[1]{0:T(128)} %bitcast.slab_ref, s32[1]{0:T(128)S(6)} %copy.20.fill_ref, f32[3,2048]{1,0:T(4,128)} %coords_ref.1, f32[16,128]{1,0:T(8,128)} %bitcast.9, f32[16,128]{1,0:T(8,128)} %bitcast.10, f32[16,128]{1,0:T(8,128)} %bitcast.11, ...), custom_call_target="tpu_custom_call" | custom-call | tf_op jit(solution)/shard_map/prep/pallas_call | solution.py:461
  2.2 3.3 %collective-permute-start = (f32[88,128]{1,0:T(8,128)S(1)}, f32[88,128]{1,0:T(8,128)S(1)}, u32[]{:S(2)}, u32[]{:S(2)}) collective-permute-start(f32[88,128]{1,0:T(8,128)S(1)} %get-tuple-element.26.own_ref), channel_id=1, source_target_pairs={{0,1},{1,0},{2,3},{3,2},{4,5},{5,4},{6,7},{7,6},{8,9},{9,8},{10,11... | collective-permute-start | bytes 135176 | tf_op jit(solution)/shard_map/ppermute | solution.py:32
  5.5 0.9 %collective-permute-done.other_ref = f32[88,128]{1,0:T(8,128)S(1)} collective-permute-done((f32[88,128]{1,0:T(8,128)S(1)}, f32[88,128]{1,0:T(8,128)S(1)}, u32[]{:S(2)}, u32[]{:S(2)}) %collective-permute-start) | collective-permute-done | bytes 45088 | tf_op jit(solution)/shard_map/ppermute | solution.py:32
  6.4 0.3 collective-permute-start.2
  6.8 0.5 collective-permute-start.1
  7.3 5.0 %born_own.1 = (f32[80,8,128]{2,1,0:T(8,128)S(1)}, bf16[16,128,64]{2,1,0:T(8,128)(2,1)S(1)}, bf16[80,64,128]{2,1,0:T(8,128)(2,1)S(1)}, f32[17,128,128]{2,1,0:T(8,...) custom-call(s32[1]{0:T(128)} %bitcast.slab_ref, s32[8,128]{1,0:T(8,128)S(1)} %get-tuple-element.25.index_ref, ...), custom_call_target="tpu_custom_call" | custom-call | flops 134217728 | tf_op jit(solution)/shard_map/born_own/pallas_call | solution.py:461
  12.3 0.0 collective-permute-done.2.odd_ref
  12.3 0.0 collective-permute-done.1.even_ref
  12.3 3.6 %born_rest.1 = (s32[8,128]{1,0:T(8,128)S(1)}, f32[16,128]{1,0:T(8,128)S(1)}, f32[16,128]{1,0:T(8,128)S(1)}, f32[80,8,128]{2,1,0:T(8,128)S(1)}, bf16[80,64,128]{2...) custom-call(s32[1]{0:T(128)} %bitcast.slab_ref, ...), custom_call_target="tpu_custom_call", output_to_operand_aliasing={{3}: (9, {}), {4}: (10, {}), {5}: (11, {})} | custom-call | tf_op jit(solution)/shard_map/born_rest/pallas_call | solution.py:461
  15.9 1.0 %collective-permute-start.3 = (f32[16,128]{1,0:T(8,128)S(1)}, f32[16,128]{1,0:T(8,128)S(1)}, u32[]{:S(2)}, u32[]{:S(2)}) collective-permute-start(f32[16,128]{1,0:T(8,128)S(1)} %get-tuple-element.36.own_ref), channel_id=1, source_target_pairs={{0,1},{1,0},{2,3},{3,2},{4,5},{5,4},{6,7},{7,6},{8,9},{9,8},{10,11... | collective-permute-start | bytes 24584 | tf_op jit(solution)/shard_map/ppermute | solution.py:32
  17.0 0.8 %collective-permute-done.3.other_ref = f32[16,128]{1,0:T(8,128)S(1)} collective-permute-done((f32[16,128]{1,0:T(8,128)S(1)}, f32[16,128]{1,0:T(8,128)S(1)}, u32[]{:S(2)}, u32[]{:S(2)}) %collective-permute-start.3) | collective-permute-done | bytes 8224 | tf_op jit(solution)/shard_map/ppermute | solution.py:32
  17.8 0.3 collective-permute-start.5
  18.1 0.3 collective-permute-start.4
  18.5 2.7 %energy_own.1 = (f32[17,128,128]{2,1,0:T(8,128)S(1)}, f32[17,128,128]{2,1,0:T(8,128)S(1)}, f32[17,128,128]{2,1,0:T(8,128)S(1)}, f32[16,128]{1,0:T(8,128)}) custom-call(s32[1]{0:T(128)} %bitcast.slab_ref, s32[8,128]{1,0:T(8,128)S(1)} %get-tuple-element.28.plan_ref, f32[80,8,128]{2,1,0:T(8,128)S(1)} %get-tuple-element.34.blocks_ref, ...), custom_call_target="tpu_custom_call" | custom-call | flops 134217728 | tf_op jit(solution)/shard_map/energy_own/pallas_call | solution.py:461
  21.2 0.0 collective-permute-done.5.odd_ref
  21.2 0.0 collective-permute-done.4.even_ref
  21.2 2.7 %energy_rest.1 = (f32[16,128]{1,0:T(8,128)S(1)}, f32[256,1,128]{2,1,0:T(1,128)S(1)}, f32[17,128,128]{2,1,0:T(8,128)S(1)}) custom-call(s32[1]{0:T(128)} %bitcast.slab_ref, s32[8,128]{1,0:T(8,128)S(1)} %get-tuple-element.39.plan_ref, f32[80,8,128]{2,1,0:T(8,128)S(1)} %get-tuple-element.34.blocks_ref, ...), custom_call_target="tpu_custom_call", output_to_operand_aliasing={{2}: (9, {})} | custom-call | tf_op jit(solution)/shard_map/energy_rest/pallas_call | solution.py:461
  23.9 31.5 %all_to_all.5.shares_ref = f32[256,1,128]{2,1,0:T(1,128)S(1)} all-to-all(f32[256,1,128]{2,1,0:T(1,128)S(1)} %get-tuple-element.43), channel_id=1, replica_groups=mesh['slab_0'=4,'slab_1'=8,'slab_2'=4,'slab_3'=2] {'slab_0','slab_1','sl..., dimensions={0} | all-to-all | bytes 262144 | tf_op jit(solution)/shard_map/all_to_all | solution.py:527
  55.4 1.1 %total.1 = (f32[1]{0:T(128)}, f32[16,128]{1,0:T(8,128)}) custom-call(f32[256,1,128]{2,1,0:T(1,128)S(1)} %all_to_all.5.shares_ref, f32[16,128]{1,0:T(8,128)S(1)} %get-tuple-element.44.energy_ref), custom_call_target="tpu_custom_call" | custom-call | tf_op jit(solution)/shard_map/total/pallas_call | solution.py:461
  (4 shorter events, 0.0 us)
Async XLA Ops:
  2.2 4.2 %collective-permute-start = (f32[88,128]{1,0:T(8,128)S(1)}, f32[88,128]{1,0:T(8,128)S(1)}, u32[]{:S(2)}, u32[]{:S(2)}) collective-permute-start(f32[88,128]{1,0:T(8,128)S(1)} %get-tuple-element.26.own_ref), channel_id=1, source_target_pairs={{0,1},{1,0},{2,3},{3,2},{4,5},{5,4},{6,7},{7,6},{8,9},{9,8},{10,11... | collective-permute-start | bytes 135176 | tf_op jit(solution)/shard_map/ppermute | solution.py:32
  6.4 5.9 %collective-permute-start.2 = (f32[176,128]{1,0:T(8,128)S(1)}, f32[176,128]{1,0:T(8,128)S(1)}, u32[]{:S(2)}, u32[]{:S(2)}) collective-permute-start(f32[176,128]{1,0:T(8,128)S(1)} %constant_dynamic-update-slice_fusion), channel_id=1, source_target_pairs={{0,1},{1,0},{2,4},{3,5},{4,2},{5,3},{6,8},{7,9},{8,6},{9,7},{10,12... | collective-permute-start | bytes 270344 | tf_op jit(solution)/shard_map/ppermute | solution.py:34
  6.8 5.6 %collective-permute-start.1 = (f32[176,128]{1,0:T(8,128)S(1)}, f32[176,128]{1,0:T(8,128)S(1)}, u32[]{:S(2)}, u32[]{:S(2)}) collective-permute-start(f32[176,128]{1,0:T(8,128)S(1)} %constant_dynamic-update-slice_fusion), channel_id=1, source_target_pairs={{0,2},{1,3},{2,0},{3,1},{4,6},{5,7},{6,4},{7,5},{8,10},{9,11},{10,... | collective-permute-start | bytes 270344 | tf_op jit(solution)/shard_map/ppermute | solution.py:34
  15.9 1.9 %collective-permute-start.3 = (f32[16,128]{1,0:T(8,128)S(1)}, f32[16,128]{1,0:T(8,128)S(1)}, u32[]{:S(2)}, u32[]{:S(2)}) collective-permute-start(f32[16,128]{1,0:T(8,128)S(1)} %get-tuple-element.36.own_ref), channel_id=1, source_target_pairs={{0,1},{1,0},{2,3},{3,2},{4,5},{5,4},{6,7},{7,6},{8,9},{9,8},{10,11... | collective-permute-start | bytes 24584 | tf_op jit(solution)/shard_map/ppermute | solution.py:32
  17.8 3.4 %collective-permute-start.5 = (f32[32,128]{1,0:T(8,128)S(1)}, f32[32,128]{1,0:T(8,128)S(1)}, u32[]{:S(2)}, u32[]{:S(2)}) collective-permute-start(f32[32,128]{1,0:T(8,128)S(1)} %constant_dynamic-update-slice_fusion.2), channel_id=1, source_target_pairs={{0,1},{1,0},{2,4},{3,5},{4,2},{5,3},{6,8},{7,9},{8,6},{9,7},{10,12... | collective-permute-start | bytes 49160 | tf_op jit(solution)/shard_map/ppermute | solution.py:34
  18.1 3.0 %collective-permute-start.4 = (f32[32,128]{1,0:T(8,128)S(1)}, f32[32,128]{1,0:T(8,128)S(1)}, u32[]{:S(2)}, u32[]{:S(2)}) collective-permute-start(f32[32,128]{1,0:T(8,128)S(1)} %constant_dynamic-update-slice_fusion.2), channel_id=1, source_target_pairs={{0,2},{1,3},{2,0},{3,1},{4,6},{5,7},{6,4},{7,5},{8,10},{9,11},{10,... | collective-permute-start | bytes 49160 | tf_op jit(solution)/shard_map/ppermute | solution.py:34

commit v9 on v8

--- a/solution.py
+++ b/solution.py
@@ -278,7 +278,7 @@
 
     def near_lists(inside):
         if own:
-            run_list(TILES, own_entry, buffers, produce, consume_near(inside, True))
+            run_list(TILES, own_entry, buffers[:4], produce, consume_near(inside, True))
         run_list(counts[0], entry_in(lists[0]), buffers[:4], produce, consume_near(inside, False))
 
     pl.when(within == 0)(lambda: near_lists(False))

time: 57 us -> 56.4 us (0.989)
  starting transfers between devices: 5.87 us -> 9.14 us
  Pallas kernels: 16.1 us -> 14 us
  blocking collectives: 31.5 us -> 29.7 us
    ppermute x2, starting transfers between devices: 4.32 us -> 6.84 us  [neighbours(): other = lax.ppermute(value, SLAB, [(i, i ^ 1) for i in range(count)])]
    pallas_call x6, Pallas kernels: 16.1 us -> 14 us  [call(): pl.pallas_call(kernel, out_shape=outs, in_specs=[smem] * len(scalars) + [...]
    all_to_all x1, blocking collectives: 31.5 us -> 29.7 us  [shards(): shares = lax.all_to_all(share, SLAB, 0, 0, tiled=True)]
    ppermute x4, starting transfers between devices: 1.55 us -> 2.31 us  [neighbours(): lax.ppermute(both, SLAB, chip_swap(count, odd))]
  transfers between devices with their start and end apart: 6 -> 6, of which waited for: 2 -> 2; matrix products, arithmetic and copies ran while one was open for 0% -> 0% of each run, Pallas kernels for 14% -> 12%
where the time goes in v9:
time: 56.4 us; the launch traced here: 55.9 us
  blocking collectives  29.7 us (53%)
  Pallas kernels  14 us (25%)
  starting transfers between devices  9.14 us (16%)
  waiting for transfers between devices  1.71 us (3%)
  between operations  1.37 us (2%)
    all_to_all x1, blocking collectives, shards(): shares = lax.all_to_all(share, SLAB, 0, 0, tiled=True)  29.7 us
    pallas_call x6, Pallas kernels, call(): pl.pallas_call(kernel, out_shape=outs, in_specs=[smem] * len(scalars) + [...  14 us
    ppermute x2, starting transfers between devices, neighbours(): other = lax.ppermute(value, SLAB, [(i, i ^ 1) for i in range(count)])  6.84 us
    ppermute x4, starting transfers between devices, neighbours(): lax.ppermute(both, SLAB, chip_swap(count, odd))  2.31 us
    ppermute x2, waiting for transfers between devices, neighbours(): other = lax.ppermute(value, SLAB, [(i, i ^ 1) for i in range(count)])  1.7 us
  transfers between devices with their start and end apart: 6, of which 2 were waited for; matrix products, arithmetic and copies ran while one was open for 0% of the time, Pallas kernels for 12%

profile of v9, /device:TPU:1, one launch (start us, length us, event | category | flops | bytes accessed | tf_op | source)
XLA Modules:
  0.0 55.9 jit_solution(12400293163046664202)
XLA Ops:
  1.3 0.9 %prep.1 = (f32[88,128]{1,0:T(8,128)S(1)}, s32[8,128]{1,0:T(8,128)S(1)}, f32[16,128]{1,0:T(8,128)S(1)}) custom-call(s32[1]{0:T(128)} %bitcast.slab_ref, s32[1]{0:T(128)S(6)} %copy.20.fill_ref, f32[3,2048]{1,0:T(4,128)} %coords_ref.1, f32[16,128]{1,0:T(8,128)} %bitcast.9, f32[16,128]{1,0:T(8,128)} %bitcast.10, f32[16,128]{1,0:T(8,128)} %bitcast.11, ...), custom_call_target="tpu_custom_call" | custom-call | tf_op jit(solution)/shard_map/prep/pallas_call | solution.py:461
  2.2 3.3 %collective-permute-start = (f32[88,128]{1,0:T(8,128)S(1)}, f32[88,128]{1,0:T(8,128)S(1)}, u32[]{:S(2)}, u32[]{:S(2)}) collective-permute-start(f32[88,128]{1,0:T(8,128)S(1)} %get-tuple-element.26.own_ref), channel_id=1, source_target_pairs={{0,1},{1,0},{2,3},{3,2},{4,5},{5,4},{6,7},{7,6},{8,9},{9,8},{10,11... | collective-permute-start | bytes 135176 | tf_op jit(solution)/shard_map/ppermute | solution.py:32
  5.5 0.9 %collective-permute-done.other_ref = f32[88,128]{1,0:T(8,128)S(1)} collective-permute-done((f32[88,128]{1,0:T(8,128)S(1)}, f32[88,128]{1,0:T(8,128)S(1)}, u32[]{:S(2)}, u32[]{:S(2)}) %collective-permute-start) | collective-permute-done | bytes 45088 | tf_op jit(solution)/shard_map/ppermute | solution.py:32
  6.4 0.3 collective-permute-start.2
  6.8 0.5 collective-permute-start.1
  7.3 4.2 %born_own.1 = (f32[80,8,128]{2,1,0:T(8,128)S(1)}, bf16[16,128,64]{2,1,0:T(8,128)(2,1)S(1)}, bf16[80,64,128]{2,1,0:T(8,128)(2,1)S(1)}, f32[17,128,128]{2,1,0:T(8,...) custom-call(s32[1]{0:T(128)} %bitcast.slab_ref, s32[8,128]{1,0:T(8,128)S(1)} %get-tuple-element.25.index_ref, ...), custom_call_target="tpu_custom_call" | custom-call | flops 134217728 | tf_op jit(solution)/shard_map/born_own/pallas_call | solution.py:461
  11.5 0.0 collective-permute-done.2.odd_ref
  11.5 0.0 collective-permute-done.1.even_ref
  11.5 2.9 %born_rest.1 = (s32[8,128]{1,0:T(8,128)S(1)}, f32[16,128]{1,0:T(8,128)S(1)}, f32[16,128]{1,0:T(8,128)S(1)}, f32[80,8,128]{2,1,0:T(8,128)S(1)}, bf16[80,64,128]{2...) custom-call(s32[1]{0:T(128)} %bitcast.slab_ref, ...), custom_call_target="tpu_custom_call", output_to_operand_aliasing={{3}: (9, {}), {4}: (10, {}), {5}: (11, {})} | custom-call | tf_op jit(solution)/shard_map/born_rest/pallas_call | solution.py:461
  14.4 3.5 %collective-permute-start.3 = (f32[16,128]{1,0:T(8,128)S(1)}, f32[16,128]{1,0:T(8,128)S(1)}, u32[]{:S(2)}, u32[]{:S(2)}) collective-permute-start(f32[16,128]{1,0:T(8,128)S(1)} %get-tuple-element.36.own_ref), channel_id=1, source_target_pairs={{0,1},{1,0},{2,3},{3,2},{4,5},{5,4},{6,7},{7,6},{8,9},{9,8},{10,11... | collective-permute-start | bytes 24584 | tf_op jit(solution)/shard_map/ppermute | solution.py:32
  18.0 0.8 %collective-permute-done.3.other_ref = f32[16,128]{1,0:T(8,128)S(1)} collective-permute-done((f32[16,128]{1,0:T(8,128)S(1)}, f32[16,128]{1,0:T(8,128)S(1)}, u32[]{:S(2)}, u32[]{:S(2)}) %collective-permute-start.3) | collective-permute-done | bytes 8224 | tf_op jit(solution)/shard_map/ppermute | solution.py:32
  18.8 0.3 collective-permute-start.5
  19.2 1.1 %collective-permute-start.4 = (f32[32,128]{1,0:T(8,128)S(1)}, f32[32,128]{1,0:T(8,128)S(1)}, u32[]{:S(2)}, u32[]{:S(2)}) collective-permute-start(f32[32,128]{1,0:T(8,128)S(1)} %constant_dynamic-update-slice_fusion.2), channel_id=1, source_target_pairs={{0,2},{1,3},{2,0},{3,1},{4,6},{5,7},{6,4},{7,5},{8,10},{9,11},{10,... | collective-permute-start | bytes 49160 | tf_op jit(solution)/shard_map/ppermute | solution.py:34
  20.2 2.4 %energy_own.1 = (f32[17,128,128]{2,1,0:T(8,128)S(1)}, f32[17,128,128]{2,1,0:T(8,128)S(1)}, f32[17,128,128]{2,1,0:T(8,128)S(1)}, f32[16,128]{1,0:T(8,128)}) custom-call(s32[1]{0:T(128)} %bitcast.slab_ref, s32[8,128]{1,0:T(8,128)S(1)} %get-tuple-element.28.plan_ref, f32[80,8,128]{2,1,0:T(8,128)S(1)} %get-tuple-element.34.blocks_ref, ...), custom_call_target="tpu_custom_call" | custom-call | flops 134217728 | tf_op jit(solution)/shard_map/energy_own/pallas_call | solution.py:461
  22.7 0.0 collective-permute-done.5.odd_ref
  22.7 0.0 collective-permute-done.4.even_ref
  22.7 2.4 %energy_rest.1 = (f32[16,128]{1,0:T(8,128)S(1)}, f32[256,1,128]{2,1,0:T(1,128)S(1)}, f32[17,128,128]{2,1,0:T(8,128)S(1)}) custom-call(s32[1]{0:T(128)} %bitcast.slab_ref, s32[8,128]{1,0:T(8,128)S(1)} %get-tuple-element.39.plan_ref, f32[80,8,128]{2,1,0:T(8,128)S(1)} %get-tuple-element.34.blocks_ref, ...), custom_call_target="tpu_custom_call", output_to_operand_aliasing={{2}: (9, {})} | custom-call | tf_op jit(solution)/shard_map/energy_rest/pallas_call | solution.py:461
  25.1 29.7 %all_to_all.5.shares_ref = f32[256,1,128]{2,1,0:T(1,128)S(1)} all-to-all(f32[256,1,128]{2,1,0:T(1,128)S(1)} %get-tuple-element.43), channel_id=1, replica_groups=mesh['slab_0'=4,'slab_1'=8,'slab_2'=4,'slab_3'=2] {'slab_0','slab_1','sl..., dimensions={0} | all-to-all | bytes 262144 | tf_op jit(solution)/shard_map/all_to_all | solution.py:527
  54.8 1.1 %total.1 = (f32[1]{0:T(128)}, f32[16,128]{1,0:T(8,128)}) custom-call(f32[256,1,128]{2,1,0:T(1,128)S(1)} %all_to_all.5.shares_ref, f32[16,128]{1,0:T(8,128)S(1)} %get-tuple-element.44.energy_ref), custom_call_target="tpu_custom_call" | custom-call | tf_op jit(solution)/shard_map/total/pallas_call | solution.py:461
  (4 shorter events, 0.0 us)
Async XLA Ops:
  2.2 4.2 %collective-permute-start = (f32[88,128]{1,0:T(8,128)S(1)}, f32[88,128]{1,0:T(8,128)S(1)}, u32[]{:S(2)}, u32[]{:S(2)}) collective-permute-start(f32[88,128]{1,0:T(8,128)S(1)} %get-tuple-element.26.own_ref), channel_id=1, source_target_pairs={{0,1},{1,0},{2,3},{3,2},{4,5},{5,4},{6,7},{7,6},{8,9},{9,8},{10,11... | collective-permute-start | bytes 135176 | tf_op jit(solution)/shard_map/ppermute | solution.py:32
  6.4 5.1 %collective-permute-start.2 = (f32[176,128]{1,0:T(8,128)S(1)}, f32[176,128]{1,0:T(8,128)S(1)}, u32[]{:S(2)}, u32[]{:S(2)}) collective-permute-start(f32[176,128]{1,0:T(8,128)S(1)} %constant_dynamic-update-slice_fusion), channel_id=1, source_target_pairs={{0,1},{1,0},{2,4},{3,5},{4,2},{5,3},{6,8},{7,9},{8,6},{9,7},{10,12... | collective-permute-start | bytes 270344 | tf_op jit(solution)/shard_map/ppermute | solution.py:34
  6.8 4.7 %collective-permute-start.1 = (f32[176,128]{1,0:T(8,128)S(1)}, f32[176,128]{1,0:T(8,128)S(1)}, u32[]{:S(2)}, u32[]{:S(2)}) collective-permute-start(f32[176,128]{1,0:T(8,128)S(1)} %constant_dynamic-update-slice_fusion), channel_id=1, source_target_pairs={{0,2},{1,3},{2,0},{3,1},{4,6},{5,7},{6,4},{7,5},{8,10},{9,11},{10,... | collective-permute-start | bytes 270344 | tf_op jit(solution)/shard_map/ppermute | solution.py:34
  14.4 4.4 %collective-permute-start.3 = (f32[16,128]{1,0:T(8,128)S(1)}, f32[16,128]{1,0:T(8,128)S(1)}, u32[]{:S(2)}, u32[]{:S(2)}) collective-permute-start(f32[16,128]{1,0:T(8,128)S(1)} %get-tuple-element.36.own_ref), channel_id=1, source_target_pairs={{0,1},{1,0},{2,3},{3,2},{4,5},{5,4},{6,7},{7,6},{8,9},{9,8},{10,11... | collective-permute-start | bytes 24584 | tf_op jit(solution)/shard_map/ppermute | solution.py:32
  18.8 3.9 %collective-permute-start.5 = (f32[32,128]{1,0:T(8,128)S(1)}, f32[32,128]{1,0:T(8,128)S(1)}, u32[]{:S(2)}, u32[]{:S(2)}) collective-permute-start(f32[32,128]{1,0:T(8,128)S(1)} %constant_dynamic-update-slice_fusion.2), channel_id=1, source_target_pairs={{0,1},{1,0},{2,4},{3,5},{4,2},{5,3},{6,8},{7,9},{8,6},{9,7},{10,12... | collective-permute-start | bytes 49160 | tf_op jit(solution)/shard_map/ppermute | solution.py:34
  19.2 3.5 %collective-permute-start.4 = (f32[32,128]{1,0:T(8,128)S(1)}, f32[32,128]{1,0:T(8,128)S(1)}, u32[]{:S(2)}, u32[]{:S(2)}) collective-permute-start(f32[32,128]{1,0:T(8,128)S(1)} %constant_dynamic-update-slice_fusion.2), channel_id=1, source_target_pairs={{0,2},{1,3},{2,0},{3,1},{4,6},{5,7},{6,4},{7,5},{8,10},{9,11},{10,... | collective-permute-start | bytes 49160 | tf_op jit(solution)/shard_map/ppermute | solution.py:34
